TPU v7x, 8 devices: a whole 2x2x1 slice. The times are simulated.
8 devices in a mesh: rep: 1 (over z), dp: 8 (over x, y, core).
Axes of the slice: x: 2, y: 2, z: 1, core: 2. Of those that a mesh axis runs over, the one named last changes fastest.
Arguments:
- x: bfloat16 [8, 2048, 896], P(('rep', 'dp'))
- dy: bfloat16 [8, 2048, 896], P(('rep', 'dp'))
- w_gate: bfloat16 [2, 896, 2304], replicated
- w_up: bfloat16 [2, 896, 2304], replicated
- w_down: bfloat16 [2, 2304, 896], replicated
- m_w_gate: float32 [2, 896, 2304], replicated
- m_w_up: float32 [2, 896, 2304], replicated
- m_w_down: float32 [2, 2304, 896], replicated
- v_w_gate: float32 [2, 896, 2304], replicated
- v_w_up: float32 [2, 896, 2304], replicated
- v_w_down: float32 [2, 2304, 896], replicated
Outputs:
- output 1: bfloat16 [2, 896, 2304], P('rep')
- output 2: bfloat16 [2, 896, 2304], P('rep')
- output 3: bfloat16 [2, 2304, 896], P('rep')
- output 4: float32 [2, 896, 2304], P('rep')
- output 5: float32 [2, 896, 2304], P('rep')
- output 6: float32 [2, 2304, 896], P('rep')
- output 7: float32 [2, 896, 2304], P('rep')
- output 8: float32 [2, 896, 2304], P('rep')
- output 9: float32 [2, 2304, 896], P('rep')
All inputs are finite; a program needn't handle non-finite values.
Results may differ from a plain program's by a relative error of at most 0.022.
Values are sent between devices in bfloat16 or wider.
A program may use at most 2.5 GiB of HBM per device.

v0:
```python
import jax
import jax.numpy as jnp
from jax import lax
from jax.sharding import PartitionSpec as P

NAMES = ("w_gate", "w_up", "w_down")


def matmul(a, w):
    return jnp.dot(a, w, preferred_element_type=jnp.float32).astype(jnp.bfloat16)


def normed(h):
    wide = h.astype(jnp.float32)
    scale = lax.rsqrt(jnp.mean(wide**2, -1, keepdims=True) + 1e-6)
    return (wide * scale).astype(jnp.bfloat16)


def layer(h, w):
    a = normed(h)
    gate = jnp.dot(a, w["w_gate"], preferred_element_type=jnp.float32)
    up = jnp.dot(a, w["w_up"], preferred_element_type=jnp.float32)
    return h + matmul((jax.nn.silu(gate) * up).astype(jnp.bfloat16), w["w_down"])


def adamw(w, m, v, g):
    m = 0.9 * m + 0.1 * g
    v = 0.95 * v + 0.05 * g * g
    step = m * lax.rsqrt(v + 1e-8) + 0.1 * w
    return (w - 0.02 * step).astype(jnp.bfloat16), m, v


def clipped(gradients, sum_of_squares, count):
    factor = jnp.minimum(1.0, 0.5 * lax.rsqrt(sum_of_squares / count + 1e-30))
    return [g * factor for g in gradients]


def solution(mesh):
    def step(x, dy, *arrays):
        weights, m, v = (arrays[i : i + 3] for i in (0, 3, 6))
        layers = weights[0].shape[0]
        h, kept = x[0], []
        for number in range(layers):
            kept.append(h)
            h = layer(h, {name: w[number] for name, w in zip(NAMES, weights, strict=True)})
        by_h, summed = dy[0], [None] * layers
        for number in reversed(range(layers)):
            _, back = jax.vjp(lambda w, h: layer(h, w), {name: w[number] for name, w in zip(NAMES, weights, strict=True)}, kept[number])
            by_w, by_h = back(by_h)
            summed[number] = [lax.psum(by_w[name], "dp") for name in NAMES]
        gradients = [jnp.stack([summed[number][i] for number in range(layers)]).astype(jnp.float32) for i in range(3)]
        gradients = clipped(gradients, sum(jnp.sum(g * g) for g in gradients), sum(g.size for g in gradients))
        new = [adamw(w.astype(jnp.float32), m, v, g) for w, m, v, g in zip(weights, m, v, gradients, strict=True)]
        return tuple(one[which] for which in range(3) for one in new)

    return jax.shard_map(
        step,
        mesh=mesh,
        in_specs=(P(("rep", "dp"), None, None),) * 2 + (P(None, None, None),) * 9,
        out_specs=(P("rep", None, None),) * 9,
        check_vma=False,
    )
```

profile of v0, /device:TPU:0, one launch (start us, length us, event | category | flops | bytes accessed | tf_op | source)
XLA Modules:
  0.0 698.6 jit_solution(17856018437985822765)
XLA Ops:
  7.2 6.1 copy.20
  16.1 6.1 copy.21
  22.3 15.2 %convolution_convert_fusion.1 = bf16[2048,2304]{1,0:T(8,128)(2,1)} fusion(bf16[2,2304,896]{2,1,0:T(8,128)(2,1)} %param.15, bf16[1,2048,896]{2,1,0:T(8,128)(2,1)} %param.12), kind=kOutput, calls=%fused_computation.63 | convolution fusion | flops 8460435456 | bytes 17235968 | tf_op jit(solution)/shard_map/transpose(jvp())/dot_general | solution.py:10
  37.5 15.5 %fusion.70 = f32[2048,2304]{1,0:T(8,128)} fusion(bf16[2,896,2304]{2,1,0:T(8,128)(2,1)} %param.13, bf16[1,2048,896]{2,1,0:T(8,128)(2,1)S(1)} %copy-done.4, f32[2048]{0:T(1024)S(1)} %add_rsqrt_fusion), kind=kOutput, calls=%fused_computation.105 | convolution fusion | flops 8461221888 | bytes 26681344 | tf_op jit(solution)/shard_map/dot_general | solution.py:21
  53.0 21.6 %multiply_convert_fusion.1 = (bf16[2048,2304]{1,0:T(8,128)(2,1)}, f32[2048,2304]{1,0:T(8,128)}) fusion(f32[2048,2304]{1,0:T(8,128)} %fusion.70, bf16[2,896,2304]{2,1,0:T(8,128)(2,1)} %param.14, bf16[1,2048,896]{2,1,0:T(8,128)(2,1)} %param.11, f32[2048]{0:T(1024)S(1)} %add_rsqrt_fusion), kind=kOutput, calls=%fused_computation.35 | convolution fusion | flops 8489533440 | bytes 54992896 | tf_op jit(solution)/shard_map/dot_general | solution.py:22
  74.6 14.1 %fusion.40 = (f32[2048]{0:T(1024)S(1)}, bf16[2048,896]{0,1:T(8,128)(2,1)S(1)}) fusion(bf16[2048,2304]{1,0:T(8,128)(2,1)} %get-tuple-element.24, bf16[2,2304,896]{2,1,0:T(8,128)(2,1)} %param.15, bf16[1,2048,896]{1,2,0:T(8,128)(2,1)} %copy.20), kind=kOutput, calls=%fused_computation.76 | convolution fusion | flops 8464889856 | bytes 20914176 | tf_op jit(solution)/shard_map/dot_general | solution.py:10
  88.7 16.3 %fusion.57 = f32[2048,2304]{1,0:T(8,128)} fusion(bf16[2,896,2304]{2,1,0:T(8,128)(2,1)} %param.14, bf16[2048,896]{0,1:T(8,128)(2,1)S(1)} %get-tuple-element.27, f32[2048]{0:T(1024)S(1)} %fusion.98), kind=kOutput, calls=%fused_computation.92 | convolution fusion | flops 8461221888 | bytes 26681344 | tf_op jit(solution)/shard_map/jvp()/dot_general | solution.py:22
  105.1 26.4 %fusion.5 = (bf16[2048,2304]{1,0:T(8,128)(2,1)}, f32[2048,2304]{1,0:T(8,128)}) fusion(f32[2048,2304]{1,0:T(8,128)} %fusion.57, bf16[2048,2304]{1,0:T(8,128)(2,1)} %convolution_convert_fusion.1, bf16[2,896,2304]{2,1,0:T(8,128)(2,1)} %param.13, bf16[2048,896]{0,1:T(8,128)(2,1)S(1)} %get-tuple-element.27, f32[2048]{0:T(1024)S(1)} %fusion.98), kind=kOutput, calls=%fused_computation.26 | convolution fusion | flops 8517844992 | bytes 64430080 | tf_op jit(solution)/shard_map/jvp()/dot_general | solution.py:21
  131.4 16.8 %fusion.33 = bf16[2048,896]{0,1:T(8,128)(2,1)} fusion(bf16[2048,2304]{1,0:T(8,128)(2,1)} %convolution_convert_fusion.1, bf16[2,896,2304]{2,1,0:T(8,128)(2,1)} %param.14, f32[2048,2304]{1,0:T(8,128)} %get-tuple-element.29), kind=kOutput, calls=%fused_computation.57 | convolution fusion | flops 8484028416 | bytes 36110336 | tf_op jit(solution)/shard_map/transpose(jvp())/dot_general | solution.py:22
  148.2 18.0 %fusion.53 = bf16[1,896,2304]{2,1,0:T(8,128)(2,1)} fusion(bf16[2048,2304]{1,0:T(8,128)(2,1)} %convolution_convert_fusion.1, bf16[2048,896]{0,1:T(8,128)(2,1)} %copy-done.5, f32[2048]{0:T(1024)S(1)} %fusion.98, f32[2048,2304]{1,0:T(8,128)} %get-tuple-element.29), kind=kOutput, calls=%fused_computation.88 | convolution fusion | flops 8491597824 | bytes 36118528 | tf_op jit(solution)/shard_map/transpose(jvp())/dot_general | solution.py:22
  166.2 19.7 %fusion.55 = bf16[1,2304,896]{2,1,0:T(8,128)(2,1)} fusion(f32[2048,2304]{1,0:T(8,128)} %fusion.57, bf16[1,2048,896]{2,1,0:T(8,128)(2,1)} %param.12, f32[2048,2304]{1,0:T(8,128)} %get-tuple-element.29), kind=kOutput, calls=%fused_computation.90 | convolution fusion | flops 8486092800 | bytes 45547520 | tf_op jit(solution)/shard_map/transpose(jvp())/dot_general | solution.py:10
  185.9 14.6 %fusion.54 = bf16[1,896,2304]{2,1,0:T(8,128)(2,1)} fusion(bf16[2048,2304]{1,0:T(8,128)(2,1)} %get-tuple-element.28, bf16[2048,896]{0,1:T(8,128)(2,1)} %copy-done.5, f32[2048]{0:T(1024)S(1)} %fusion.98), kind=kOutput, calls=%fused_computation.89 | convolution fusion | flops 8461221888 | bytes 17244160 | tf_op jit(solution)/shard_map/transpose(jvp())/dot_general | solution.py:21
  200.5 14.0 %fusion.42 = (f32[2048]{0:T(1024)S(1)}, bf16[2048,896]{0,1:T(8,128)(2,1)S(1)}) fusion(bf16[2048,896]{0,1:T(8,128)(2,1)S(1)} %copy-done.6, bf16[2048,896]{0,1:T(8,128)(2,1)} %fusion.33, bf16[2048,2304]{1,0:T(8,128)(2,1)} %get-tuple-element.28, bf16[2,896,2304]{2,1,0:T(8,128)(2,1)} %param.13), kind=kOutput, calls=%fused_computation.78 | convolution fusion | flops 8464889856 | bytes 24584192 | tf_op jit(solution)/shard_map/transpose(jvp())/dot_general | solution.py:21
  214.5 4.6 fusion.76
  219.2 14.6 %convolution_convert_fusion = bf16[2048,2304]{1,0:T(8,128)(2,1)} fusion(bf16[2048,896]{0,1:T(8,128)(2,1)} %fusion.76, bf16[2,2304,896]{2,1,0:T(8,128)(2,1)S(1)} %bitcast.75), kind=kOutput, calls=%fused_computation.62 | convolution fusion | flops 8460435456 | bytes 17235968 | tf_op jit(solution)/shard_map/transpose(jvp())/dot_general | solution.py:10
  233.8 14.1 %fusion.56 = bf16[1,2304,896]{2,1,0:T(8,128)(2,1)} fusion(bf16[2048,2304]{1,0:T(8,128)(2,1)} %get-tuple-element.24, bf16[2048,896]{0,1:T(8,128)(2,1)S(1)} %copy-done.7), kind=kOutput, calls=%fused_computation.91 | convolution fusion | flops 8457781248 | bytes 17235968 | tf_op jit(solution)/shard_map/transpose(jvp())/dot_general | solution.py:10
  247.9 17.1 %fusion.49 = bf16[1,896,2304]{2,1,0:T(8,128)(2,1)} fusion(bf16[2048,2304]{1,0:T(8,128)(2,1)} %convolution_convert_fusion, bf16[1,2048,896]{1,2,0:T(8,128)(2,1)S(1)} %copy-done.2, f32[2048]{0:T(1024)S(1)} %copy-done.11, f32[2048,2304]{1,0:T(8,128)} %fusion.70), kind=kOutput, calls=%fused_computation.86 | convolution fusion | flops 8491597824 | bytes 36118528 | tf_op jit(solution)/shard_map/transpose(jvp())/dot_general | solution.py:22
  265.0 21.0 %fusion.50 = bf16[1,896,2304]{2,1,0:T(8,128)(2,1)} fusion(f32[2048,2304]{1,0:T(8,128)} %fusion.70, f32[2048,2304]{1,0:T(8,128)} %get-tuple-element.25, bf16[2048,2304]{1,0:T(8,128)(2,1)} %convolution_convert_fusion, bf16[1,2048,896]{1,2,0:T(8,128)(2,1)S(1)} %copy-done.2, f32[2048]{0:T(1024)S(1)} %copy-done.11), kind=kOutput, calls=%fused_computation.87 | convolution fusion | flops 8515190784 | bytes 54992896 | tf_op jit(solution)/shard_map/transpose(jvp())/dot_general | solution.py:21
  286.0 295.1 %all-reduce.3.cloned.1.call-done = (bf16[1,896,2304]{2,1,0:T(8,128)(2,1)}, bf16[1,896,2304]{2,1,0:T(8,128)(2,1)}, bf16[1,896,2304]{2,1,0:T(8,128)(2,1)}, bf16[1,...) async-done(((bf16[1,896,2304]{2,1,0:T(8,128)(2,1)}, bf16[1,896,2304]{2,1,0:T(8,128)(2,1)}, bf16[1,896,2304]{2,1,0:T(8,128)(2,1)}, ...) | async-done | bytes 24772624 | tf_op jit(solution)/shard_map/psum | solution.py:50
  581.1 8.4 %fusion.20 = f32[]{:T(128)} fusion(bf16[1,896,2304]{2,1,0:T(8,128)(2,1)} %get-tuple-element.9, bf16[1,896,2304]{2,1,0:T(8,128)(2,1)} %get-tuple-element.10), kind=kLoop, calls=%fused_computation.44 | loop fusion | flops 16515071 | bytes 8257540 | tf_op jit(solution)/shard_map/reduce_sum | solution.py:52
  589.6 4.8 fusion.21
  595.7 8.3 %fusion.22 = f32[]{:T(128)} fusion(bf16[1,2304,896]{2,1,0:T(8,128)(2,1)} %get-tuple-element.13, bf16[1,2304,896]{2,1,0:T(8,128)(2,1)} %get-tuple-element.14), kind=kLoop, calls=%fused_computation.46 | loop fusion | flops 16515071 | bytes 8257540 | tf_op jit(solution)/shard_map/reduce_sum | solution.py:52
  604.7 28.9 %fusion.28 = (bf16[2,2304,896]{2,1,0:T(8,128)(2,1)}, f32[2,2304,896]{2,1,0:T(8,128)}, f32[2,2304,896]{2,1,0:T(8,128)}) fusion(bf16[2,2304,896]{2,1,0:T(8,128)(2,1)} %param.15, f32[]{:T(128)S(6)} %min_shard_map.3, bf16[1,2304,896]{2,1,0:T(8,128)(2,1)} %get-tuple-element.13, bf16[1,2304,896]{2,1,0:T(8,128)(2,1)} %get-tuple-element.14, ...), kind=kLoop, calls=%fused_computation.52 | loop fusion | flops 82575360 | bytes 90832896 | tf_op jit(solution)/shard_map/convert_element_type | solution.py:30
  633.5 57.8 %fusion.19 = (bf16[2,896,2304]{2,1,0:T(8,128)(2,1)}, f32[2,896,2304]{2,1,0:T(8,128)}, f32[2,896,2304]{2,1,0:T(8,128)}, bf16[2,896,2304]{2,1,0:T(8,128)(2,1)}, f3...) fusion(bf16[2,896,2304]{2,1,0:T(8,128)(2,1)} %param.13, f32[]{:T(128)S(6)} %min_shard_map.3, ...), kind=kLoop, calls=%fused_computation.43 | loop fusion | flops 165150720 | bytes 181665792 | tf_op jit(solution)/shard_map/convert_element_type | solution.py:30
  (35 shorter events, 3.0 us)
Async XLA Ops:
  7.2 574.0 %all-reduce.3.cloned.1.call-start = ((), (), s32[]{:S(2)}) async-start(), calls=%async_computation | async-start | bytes 49545216 | tf_op jit(solution)/shard_map/psum | solution.py:50
  16.1 36.9 %copy-start.10 = (f32[2048]{0:T(1024)}, f32[2048]{0:T(1024)S(1)}, u32[]{:S(2)}) copy-start(f32[2048]{0:T(1024)S(1)} %add_rsqrt_fusion) | copy-start | bytes 24580
  22.3 15.2 %copy-start.4 = (bf16[1,2048,896]{2,1,0:T(8,128)(2,1)S(1)}, bf16[1,2048,896]{2,1,0:T(8,128)(2,1)}, u32[]{:S(2)}) copy-start(bf16[1,2048,896]{2,1,0:T(8,128)(2,1)} %param.11) | copy-start | bytes 11010052
  88.7 16.4 %copy-start.5 = (bf16[2048,896]{0,1:T(8,128)(2,1)}, bf16[2048,896]{0,1:T(8,128)(2,1)S(1)}, u32[]{:S(2)}) copy-start(bf16[2048,896]{0,1:T(8,128)(2,1)S(1)} %get-tuple-element.27) | copy-start | bytes 11010052
  88.7 16.4 %copy-start.8 = (f32[2048]{0:T(1024)}, f32[2048]{0:T(1024)S(1)}, u32[]{:S(2)}) copy-start(f32[2048]{0:T(1024)S(1)} %get-tuple-element.26) | copy-start | bytes 24580
  185.9 14.6 %copy-start.6 = (bf16[2048,896]{0,1:T(8,128)(2,1)S(1)}, bf16[2048,896]{0,1:T(8,128)(2,1)}, u32[]{:S(2)}) copy-start(bf16[2048,896]{0,1:T(8,128)(2,1)} %copy-done.5) | copy-start | bytes 11010052
  185.9 33.2 %slice-start = ((s8[8257536]{0:T(1024)(128)(4,1)}), s8[4194304]{0:T(1024)(128)(4,1)S(1)}, s32[]{:S(2)}) async-start(s8[8257536]{0:T(1024)(128)(4,1)} %bitcast.74), calls=%async_computation.1 | async-start | bytes 8388608
  200.5 14.0 %copy-start.9 = (f32[2048]{0:T(1024)S(1)}, f32[2048]{0:T(1024)}, u32[]{:S(2)}) copy-start(f32[2048]{0:T(1024)} %copy-done.8) | copy-start | bytes 24580
  200.5 14.0 %copy-start.3 = (bf16[1,2048,896]{1,2,0:T(8,128)(2,1)S(1)}, bf16[1,2048,896]{1,2,0:T(8,128)(2,1)}, u32[]{:S(2)}) copy-start(bf16[1,2048,896]{1,2,0:T(8,128)(2,1)} %copy.21) | copy-start | bytes 11010052
  200.5 18.7 %slice-start.1 = ((s8[8257536]{0:T(1024)(128)(4,1)}), s8[4063232]{0:T(1024)(128)(4,1)S(1)}, s32[]{:S(2)}) async-start(s8[8257536]{0:T(1024)(128)(4,1)} %bitcast.74), calls=%async_computation.2 | async-start | bytes 8126464
  219.2 14.6 %copy-start.7 = (bf16[2048,896]{0,1:T(8,128)(2,1)S(1)}, bf16[2048,896]{0,1:T(8,128)(2,1)}, u32[]{:S(2)}) copy-start(bf16[2048,896]{0,1:T(8,128)(2,1)} %fusion.76) | copy-start | bytes 11010052
  233.8 14.1 %copy-start.2 = (bf16[1,2048,896]{1,2,0:T(8,128)(2,1)S(1)}, bf16[1,2048,896]{1,2,0:T(8,128)(2,1)}, u32[]{:S(2)}) copy-start(bf16[1,2048,896]{1,2,0:T(8,128)(2,1)} %copy.20) | copy-start | bytes 11010052
  233.8 14.1 %copy-start.11 = (f32[2048]{0:T(1024)S(1)}, f32[2048]{0:T(1024)}, u32[]{:S(2)}) copy-start(f32[2048]{0:T(1024)} %copy-done.10) | copy-start | bytes 24580
  581.1 8.4 %copy-start = (bf16[1,896,2304]{2,1,0:T(8,128)(2,1)S(1)}, bf16[1,896,2304]{2,1,0:T(8,128)(2,1)}, u32[]{:S(2)}) copy-start(bf16[1,896,2304]{2,1,0:T(8,128)(2,1)} %get-tuple-element.11) | copy-start | bytes 12386308
  581.1 8.4 %copy-start.1 = (bf16[1,896,2304]{2,1,0:T(8,128)(2,1)S(1)}, bf16[1,896,2304]{2,1,0:T(8,128)(2,1)}, u32[]{:S(2)}) copy-start(bf16[1,896,2304]{2,1,0:T(8,128)(2,1)} %get-tuple-element.12) | copy-start | bytes 12386308
Sparse Core Ops, SparseCore 0:
  286.1 294.9 all-reduce.2
where the time goes:
time: 707 us; the launch traced here: 699 us
  waiting for transfers between devices  295 us (42%)
  matrix products  259 us (37%)
  other arithmetic  116 us (16%)
  between operations  16.6 us (2%)
  local copies, waits for them, and re-layouts  12.3 us (2%)
    psum x1, waiting for transfers between devices, step(): summed[number] = [lax.psum(by_w[name], 'dp') for name in NAMES]  295 us
    dot_general x5, matrix products, layer(): gate = jnp.dot(a, w['w_gate'], preferred_element_type=jnp.float32)  91.4 us
    dot_general x5, matrix products, layer(): up = jnp.dot(a, w['w_up'], preferred_element_type=jnp.float32)  89.8 us
    convert_element_type x2, other arithmetic, adamw(): return ((w - 0.02 * step).astype(jnp.bfloat16), m, v)  86.6 us
    dot_general x5, matrix products, matmul(): jnp.dot(a, w, preferred_element_type=jnp.float32).astype(jnp.bfloat16)  77.7 us
    reduce_sum x3, other arithmetic, step(): jnp.sum(g * g)  21.5 us
  transfers between devices with their start and end apart: 1, of which 1 were waited for; matrix products, arithmetic and copies ran while one was open for 0% of the time, Pallas kernels for 0%

commit v1 on v0

v1 whole, which is shorter than its diff:
```python
import functools

import jax
import jax.numpy as jnp
from jax import lax
from jax.experimental import pallas as pl
from jax.experimental.pallas import tpu as pltpu
from jax.sharding import PartitionSpec as P

BF16, F32 = jnp.bfloat16, jnp.float32
ROWS = 512
CHUNK = 768
VMEM_LIMIT = 62 * 1024 * 1024


def dot(a, b):
    return jnp.dot(a, b, preferred_element_type=F32)


def dot_t(a, b):
    return lax.dot_general(a, b, (((1,), (1,)), ((), ())), preferred_element_type=F32)


def scale_of(h):
    return lax.rsqrt(jnp.mean(h * h, -1, keepdims=True) + 1e-6)


def sigmoid(x):
    return 1.0 / (1.0 + jnp.exp(-x))


def params(n=1):
    return pltpu.CompilerParams(dimension_semantics=("arbitrary",) * n, vmem_limit_bytes=VMEM_LIMIT)


def cost(flops, nbytes):
    return pl.CostEstimate(flops=flops, bytes_accessed=nbytes, transcendentals=0)


def whole(w, layer):
    return pl.BlockSpec((None,) + w.shape[1:], lambda *_: (layer, 0, 0), pipeline_mode=pl.Buffered(1))


def forward_kernel(h_ref, wg_ref, wu_ref, wd_ref, at_ref, gate_ref, up_ref, actt_ref, y_ref):
    h = h_ref[...].astype(F32)
    a = (h * scale_of(h)).astype(BF16)
    at_ref[...] = a.T
    acts = []
    for start in range(0, wg_ref.shape[1], CHUNK):
        cols = pl.ds(start, CHUNK)
        gate, up = dot(a, wg_ref[:, cols]), dot(a, wu_ref[:, cols])
        gate_ref[:, cols] = gate
        up_ref[:, cols] = up
        act = (gate * sigmoid(gate) * up).astype(BF16)
        actt_ref[cols, :] = act.T
        acts.append(act)
    y = dot(jnp.concatenate(acts, 1), wd_ref[...]).astype(BF16)
    y_ref[...] = h_ref[...] + y


def forward(h, wg, wu, wd, layer):
    t, d = h.shape
    ff = wg.shape[2]
    rows = lambda n: pl.BlockSpec((ROWS, n), lambda i: (i, 0))
    cols = lambda n: pl.BlockSpec((n, ROWS), lambda i: (0, i))
    return pl.pallas_call(
        forward_kernel,
        grid=(t // ROWS,),
        in_specs=[rows(d), whole(wg, layer), whole(wu, layer), whole(wd, layer)],
        out_specs=[cols(d), rows(ff), rows(ff), cols(ff), rows(d)],
        out_shape=[
            jax.ShapeDtypeStruct((d, t), BF16),
            jax.ShapeDtypeStruct((t, ff), F32),
            jax.ShapeDtypeStruct((t, ff), F32),
            jax.ShapeDtypeStruct((ff, t), BF16),
            jax.ShapeDtypeStruct((t, d), BF16),
        ],
        compiler_params=params(),
        cost_estimate=cost(6 * t * d * ff, 12 * t * ff),
        name="forward",
    )(h, wg, wu, wd)


def gate_up_back(gate, up, by_act):
    sig = sigmoid(gate)
    silu = gate * sig
    by_gate = by_act * up * (sig + silu * (1.0 - sig))
    return (silu * up).astype(BF16), by_gate.astype(BF16), (by_act * silu).astype(BF16)


def top_kernel(h_ref, dy_ref, wg_ref, wu_ref, wd_ref, at_ref, actt_ref, bg_ref, bu_ref, bh_ref):
    h = h_ref[...].astype(F32)
    scale = scale_of(h)
    a = (h * scale).astype(BF16)
    at_ref[...] = a.T
    for start in range(0, wg_ref.shape[1], CHUNK):
        cols = pl.ds(start, CHUNK)
        by_act = dot_t(dy_ref[...], wd_ref[cols, :]).astype(BF16).astype(F32)
        act, by_gate, by_up = gate_up_back(dot(a, wg_ref[:, cols]), dot(a, wu_ref[:, cols]), by_act)
        actt_ref[cols, :] = act.T
        bg_ref[:, cols] = by_gate
        bu_ref[:, cols] = by_up
    by_a = (dot_t(bg_ref[...], wg_ref[...]) + dot_t(bu_ref[...], wu_ref[...])).astype(BF16).astype(F32)
    h = h_ref[...].astype(F32)
    by_h = scale * (by_a - h * (scale * scale * jnp.mean(by_a * h, -1, keepdims=True)))
    bh_ref[...] = (dy_ref[...].astype(F32) + by_h).astype(BF16)


def top(h, dy, wg, wu, wd, layer):
    t, d = h.shape
    ff = wg.shape[2]
    rows = lambda n: pl.BlockSpec((ROWS, n), lambda i: (i, 0))
    cols = lambda n: pl.BlockSpec((n, ROWS), lambda i: (0, i))
    return pl.pallas_call(
        top_kernel,
        grid=(t // ROWS,),
        in_specs=[rows(d), rows(d), whole(wg, layer), whole(wu, layer), whole(wd, layer)],
        out_specs=[cols(d), cols(ff), rows(ff), rows(ff), rows(d)],
        out_shape=[
            jax.ShapeDtypeStruct((d, t), BF16),
            jax.ShapeDtypeStruct((ff, t), BF16),
            jax.ShapeDtypeStruct((t, ff), BF16),
            jax.ShapeDtypeStruct((t, ff), BF16),
            jax.ShapeDtypeStruct((t, d), BF16),
        ],
        compiler_params=params(),
        cost_estimate=cost(10 * t * d * ff, 8 * t * ff),
        name="top",
    )(h, dy, wg, wu, wd)


def hidden_back_kernel(by_ref, gate_ref, up_ref, wd_ref, bg_ref, bu_ref):
    for start in range(0, gate_ref.shape[1], CHUNK):
        cols = pl.ds(start, CHUNK)
        by_act = dot_t(by_ref[...], wd_ref[cols, :]).astype(BF16).astype(F32)
        _, bg_ref[:, cols], bu_ref[:, cols] = gate_up_back(gate_ref[:, cols], up_ref[:, cols], by_act)


def hidden_back(by, gate, up, wd, layer):
    t, d = by.shape
    ff = gate.shape[1]
    rows = lambda n: pl.BlockSpec((ROWS, n), lambda i: (i, 0))
    return pl.pallas_call(
        hidden_back_kernel,
        grid=(t // ROWS,),
        in_specs=[rows(d), rows(ff), rows(ff), whole(wd, layer)],
        out_specs=[rows(ff), rows(ff)],
        out_shape=[jax.ShapeDtypeStruct((t, ff), BF16)] * 2,
        compiler_params=params(),
        cost_estimate=cost(2 * t * d * ff, 12 * t * ff),
        name="hidden_back",
    )(by, gate, up, wd)


def product_kernel(a_ref, b_ref, c_ref):
    c_ref[...] = dot(a_ref[...], b_ref[...]).astype(BF16)


def product(a, b, name):
    (m, k), n = a.shape, b.shape[1]
    if m > n:
        specs = [pl.BlockSpec((CHUNK, k), lambda i: (i, 0)), pl.BlockSpec((k, n), lambda i: (0, 0), pipeline_mode=pl.Buffered(1))]
        out = pl.BlockSpec((CHUNK, n), lambda i: (i, 0))
    else:
        specs = [pl.BlockSpec((m, k), lambda i: (0, 0), pipeline_mode=pl.Buffered(1)), pl.BlockSpec((k, CHUNK), lambda i: (0, i))]
        out = pl.BlockSpec((m, CHUNK), lambda i: (0, i))
    return pl.pallas_call(
        product_kernel,
        grid=(max(m, n) // CHUNK,),
        in_specs=specs,
        out_specs=out,
        out_shape=jax.ShapeDtypeStruct((m, n), BF16),
        compiler_params=params(),
        cost_estimate=cost(2 * m * n * k, 2 * (m * k + k * n + m * n)),
        name=name,
    )(a, b)


def adamw_kernel(factor_ref, w_ref, m_ref, v_ref, g_ref, *refs):
    new_w_ref, new_m_ref, new_v_ref = refs[-3:]
    g = g_ref[...].astype(F32) * factor_ref[0, 0]
    m = 0.9 * m_ref[...] + 0.1 * g
    v = 0.95 * v_ref[...] + 0.05 * g * g
    w = w_ref[...].astype(F32)
    new_w_ref[...] = (w - 0.02 * (m * lax.rsqrt(v + 1e-8) + 0.1 * w)).astype(BF16)
    new_m_ref[...] = m
    new_v_ref[...] = v


def adamw(factor, w, m, v, g, layer, so_far):
    _, r, c = w.shape
    block = r // 14 if r % 224 == 0 else r // 16
    part = pl.BlockSpec((None, block, c), lambda i: (layer, i, 0))
    return pl.pallas_call(
        adamw_kernel,
        grid=(r // block,),
        in_specs=[pl.BlockSpec(memory_space=pltpu.SMEM), part, part, part, pl.BlockSpec((block, c), lambda i: (i, 0))]
        + [pl.BlockSpec(memory_space=pl.ANY)] * len(so_far),
        out_specs=[part] * 3,
        out_shape=[jax.ShapeDtypeStruct(w.shape, dtype) for dtype in (BF16, F32, F32)],
        input_output_aliases={5 + i: i for i in range(len(so_far))},
        compiler_params=params(),
        cost_estimate=cost(40 * r * c, 22 * r * c),
        name="adamw",
    )(factor, w, m, v, g, *so_far)


def solution(mesh):
    def step(x, dy, *arrays):
        weights, ms, vs = (arrays[i : i + 3] for i in (0, 3, 6))
        x, dy = x[0], dy[0]
        scatter = lambda g: lax.psum_scatter(g, "dp", scatter_dimension=0, tiled=True)
        gather = lambda g: lax.all_gather(g, "dp", axis=0, tiled=True)

        at0, gate0, up0, actt0, h1 = forward(x, *weights, 0)
        at1, actt1, bg1, bu1, bh1 = top(h1, dy, *weights, 1)
        terms1 = [product(at1, bg1, "gate1"), product(at1, bu1, "up1"), product(actt1, dy, "down1")]
        bg0, bu0 = hidden_back(bh1, gate0, up0, weights[2], 0)
        terms0 = [product(at0, bg0, "gate0"), product(at0, bu0, "up0"), product(actt0, bh1, "down0")]
        shards = [[scatter(g) for g in terms] for terms in (terms0, terms1)]
        total = sum(jnp.sum(jnp.square(g.astype(F32))) for part in shards for g in part)
        total = lax.psum(total, "dp")
        count = sum(w.size for w in weights)
        factor = jnp.minimum(1.0, 0.5 * lax.rsqrt(total / count + 1e-30)).reshape(1, 1)

        new = [()] * 3
        for layer in (1, 0):
            for i in range(3):
                new[i] = adamw(factor, weights[i], ms[i], vs[i], gather(shards[layer][i]), layer, new[i])
        return tuple(one[which] for which in range(3) for one in new)

    return jax.shard_map(
        step,
        mesh=mesh,
        in_specs=(P(("rep", "dp"), None, None),) * 2 + (P(None, None, None),) * 9,
        out_specs=(P("rep", None, None),) * 9,
        check_vma=False,
    )
```

time: 707 us -> 629 us (0.89)
  Pallas kernels: 0 us -> 337 us
  matrix products: 259 us -> 0 us
  other arithmetic: 116 us -> 11.5 us
  waiting for transfers between devices: 295 us -> 231 us
  blocking collectives: 0 us -> 22.6 us
  local copies, waits for them, and re-layouts: 12.3 us -> 0 us
    pallas_call x0 -> x15, Pallas kernels: none -> 337 us  [the longest x6 125 us: adamw(): pl.pallas_call(adamw_kernel, grid=(r // block,), in_specs=[pl.BlockSpec(m...]
    psum x1 -> x0, waiting for transfers between devices: 295 us -> none  [step(): summed[number] = [lax.psum(by_w[name], 'dp') for name in NAMES]]
    dot_general x15 -> x0, matrix products: 259 us -> none  [the longest x5 91.4 us: layer(): gate = jnp.dot(a, w['w_gate'], preferred_element_type=jnp.float32)]
    reduce_scatter x0 -> x6, waiting for transfers between devices: none -> 178 us  [step(): lax.psum_scatter(g, 'dp', scatter_dimension=0, tiled=True)]
    convert_element_type x2 -> x0, other arithmetic: 86.6 us -> none  [adamw(): return ((w - 0.02 * step).astype(jnp.bfloat16), m, v)]
    all_gather x0 -> x6, waiting for transfers between devices: none -> 51.5 us  [step(): gather = lambda g: lax.all_gather(g, 'dp', axis=0, tiled=True)]
    psum x0 -> x1, blocking collectives: none -> 22.6 us  [step(): total = lax.psum(total, 'dp')]
    reduce_sum x4 -> x6, other arithmetic: 24.3 us -> 11.5 us  [step(): jnp.sum(jnp.square(g.astype(F32)))]
  transfers between devices with their start and end apart: 1 -> 12, of which waited for: 1 -> 9; matrix products, arithmetic and copies ran while one was open for 0% -> 2% of each run, Pallas kernels for 0% -> 32%
where the time goes in v1:
time: 629 us; the launch traced here: 621 us
  Pallas kernels  337 us (54%)
  waiting for transfers between devices  231 us (37%)
  blocking collectives  22.6 us (4%)
  between operations  19 us (3%)
  other arithmetic  11.5 us (2%)
    reduce_scatter x6, waiting for transfers between devices, step(): lax.psum_scatter(g, 'dp', scatter_dimension=0, tiled=True)  178 us
    pallas_call x6, Pallas kernels, adamw(): pl.pallas_call(adamw_kernel, grid=(r // block,), in_specs=[pl.BlockSpec(m...  125 us
    pallas_call x6, Pallas kernels, product(): pl.pallas_call(product_kernel, grid=(max(m, n) // CHUNK,), in_specs=specs...  82 us
    pallas_call x1, Pallas kernels, top(): pl.pallas_call(top_kernel, grid=(t // ROWS,), in_specs=[rows(d), rows(d),...  62.7 us
    all_gather x6, waiting for transfers between devices, step(): gather = lambda g: lax.all_gather(g, 'dp', axis=0, tiled=True)  51.5 us
    pallas_call x1, Pallas kernels, forward(): pl.pallas_call(forward_kernel, grid=(t // ROWS,), in_specs=[rows(d), whol...  39.8 us
    pallas_call x1, Pallas kernels, hidden_back(): pl.pallas_call(hidden_back_kernel, grid=(t // ROWS,), in_specs=[rows(d),...  27.7 us
    psum x1, blocking collectives, step(): total = lax.psum(total, 'dp')  22.6 us
  transfers between devices with their start and end apart: 12, of which 9 were waited for; matrix products, arithmetic and copies ran while one was open for 2% of the time, Pallas kernels for 32%

profile of v1, /device:TPU:0, one launch (start us, length us, event | category | flops | bytes accessed | tf_op | source)
XLA Modules:
  0.0 621.2 jit_solution(10423202529816311265)
XLA Ops:
  7.2 39.8 %forward.1 = (bf16[896,2048]{1,0:T(8,128)(2,1)}, f32[2048,2304]{1,0:T(8,128)}, f32[2048,2304]{1,0:T(8,128)}, bf16[2304,2048]{1,0:T(8,128)(2,1)}, bf16[2048,896]{1,0:T(8,128)(2,1)}) custom-call(bf16[2048,896]{1,0:T(8,128)(2,1)} %bitcast.3, bf16[2,896,2304]{2,1,0:T(8,128)(2,1)} %w_ref.7, bf16[2,896,2304]{2,1,0:T(8,128)(2,1)} %w_ref.9, bf16[2,2304,896]{2,1,0:T(8,128)(2,1)} %w_ref.11), custom_call_target="tpu_custom_call" | custom-call | flops 25367150592 | bytes 56623104 | tf_op jit(solution)/shard_map/forward/pallas_call | solution.py:66
  47.0 62.7 %top.1 = (bf16[896,2048]{1,0:T(8,128)(2,1)}, bf16[2304,2048]{1,0:T(8,128)(2,1)}, bf16[2048,2304]{1,0:T(8,128)(2,1)}, bf16[2048,2304]{1,0:T(8,128)(2,1)}, bf16[2048,896]{1,0:T(8,128)(2,1)}) custom-call(bf16[2048,896]{1,0:T(8,128)(2,1)} %get-tuple-element.40.h_ref, bf16[2048,896]{1,0:T(8,128)(2,1)} %bitcast.4, bf16[2,896,2304]{2,1,0:T(8,128)(2,1)} %w_ref.7, ...), custom_call_target="tpu_custom_call" | custom-call | flops 42278584320 | bytes 37748736 | tf_op jit(solution)/shard_map/top/pallas_call | solution.py:114
  109.6 14.3 %down1.1 = bf16[2304,896]{1,0:T(8,128)(2,1)} custom-call(bf16[2304,2048]{1,0:T(8,128)(2,1)} %get-tuple-element.50.a_ref, bf16[2048,896]{1,0:T(8,128)(2,1)} %bitcast.5), custom_call_target="tpu_custom_call" | custom-call | flops 8455716864 | bytes 17235968 | tf_op jit(solution)/shard_map/down1/pallas_call | solution.py:167
  124.1 13.6 %up1.1 = bf16[896,2304]{1,0:T(8,128)(2,1)} custom-call(bf16[896,2048]{1,0:T(8,128)(2,1)} %get-tuple-element.47.a_ref, bf16[2048,2304]{1,0:T(8,128)(2,1)} %get-tuple-element.49.b_ref), custom_call_target="tpu_custom_call" | custom-call | flops 8455716864 | bytes 17235968 | tf_op jit(solution)/shard_map/up1/pallas_call | solution.py:167
  137.8 13.2 %gate1.1 = bf16[896,2304]{1,0:T(8,128)(2,1)} custom-call(bf16[896,2048]{1,0:T(8,128)(2,1)} %get-tuple-element.47.a_ref, bf16[2048,2304]{1,0:T(8,128)(2,1)} %get-tuple-element.48.b_ref), custom_call_target="tpu_custom_call" | custom-call | flops 8455716864 | bytes 17235968 | tf_op jit(solution)/shard_map/gate1/pallas_call | solution.py:167
  151.0 14.3 %down0.1 = bf16[2304,896]{1,0:T(8,128)(2,1)} custom-call(bf16[2304,2048]{1,0:T(8,128)(2,1)} %get-tuple-element.46.a_ref, bf16[2048,896]{1,0:T(8,128)(2,1)} %get-tuple-element.41.by_ref.b_ref), custom_call_target="tpu_custom_call" | custom-call | flops 8455716864 | bytes 17235968 | tf_op jit(solution)/shard_map/down0/pallas_call | solution.py:167
  165.4 27.7 %hidden_back.1 = (bf16[2048,2304]{1,0:T(8,128)(2,1)}, bf16[2048,2304]{1,0:T(8,128)(2,1)}) custom-call(bf16[2048,896]{1,0:T(8,128)(2,1)} %get-tuple-element.41.by_ref.b_ref, f32[2048,2304]{1,0:T(8,128)} %get-tuple-element.42.gate_ref, f32[2048,2304]{1,0:T(8,128)} %get-tuple-element.43.up_ref, bf16[2,2304,896]{2,1,0:T(8,128)(2,1)} %w_ref.11), custom_call_target="tpu_custom_call" | custom-call | flops 8455716864 | bytes 56623104 | tf_op jit(solution)/shard_map/hidden_back/pallas_call | solution.py:143
  193.1 13.2 %up0.1 = bf16[896,2304]{1,0:T(8,128)(2,1)} custom-call(bf16[896,2048]{1,0:T(8,128)(2,1)} %get-tuple-element.39.a_ref, bf16[2048,2304]{1,0:T(8,128)(2,1)} %get-tuple-element.45.b_ref), custom_call_target="tpu_custom_call" | custom-call | flops 8455716864 | bytes 17235968 | tf_op jit(solution)/shard_map/up0/pallas_call | solution.py:167
  206.3 13.3 %gate0.1 = bf16[896,2304]{1,0:T(8,128)(2,1)} custom-call(bf16[896,2048]{1,0:T(8,128)(2,1)} %get-tuple-element.39.a_ref, bf16[2048,2304]{1,0:T(8,128)(2,1)} %get-tuple-element.44.b_ref), custom_call_target="tpu_custom_call" | custom-call | flops 8455716864 | bytes 17235968 | tf_op jit(solution)/shard_map/gate0/pallas_call | solution.py:167
  221.2 40.3 %reduce-scatter.13.cloned.1.call-done = bf16[112,2304]{1,0:T(8,128)(2,1)} async-done(((bf16[896,2304]{1,0:T(8,128)(2,1)}), bf16[112,2304]{1,0:T(8,128)(2,1)}) %reduce-scatter.13.cloned.1.call-update) | async-done | bytes 516112 | tf_op jit(solution)/shard_map/reduce_scatter | solution.py:212
  261.5 45.9 %reduce-scatter.11.cloned.1.call-done = bf16[288,896]{1,0:T(8,128)(2,1)} async-done(((bf16[2304,896]{1,0:T(8,128)(2,1)}), bf16[288,896]{1,0:T(8,128)(2,1)}) %reduce-scatter.11.cloned.1.call-update) | async-done | bytes 516112 | tf_op jit(solution)/shard_map/reduce_scatter | solution.py:212
  307.5 45.9 %reduce-scatter.9.cloned.1.call-done = bf16[112,2304]{1,0:T(8,128)(2,1)} async-done(((bf16[896,2304]{1,0:T(8,128)(2,1)}), bf16[112,2304]{1,0:T(8,128)(2,1)}) %reduce-scatter.9.cloned.1.call-update) | async-done | bytes 516112 | tf_op jit(solution)/shard_map/reduce_scatter | solution.py:212
  353.5 45.9 %reduce-scatter.7.cloned.1.call-done = bf16[112,2304]{1,0:T(8,128)(2,1)} async-done(((bf16[896,2304]{1,0:T(8,128)(2,1)}), bf16[112,2304]{1,0:T(8,128)(2,1)}) %reduce-scatter.7.cloned.1.call-update) | async-done | bytes 516112 | tf_op jit(solution)/shard_map/reduce_scatter | solution.py:212
  414.8 22.6 %psum.7 = f32[]{:T(128)} all-reduce(f32[]{:T(128)S(6)} %add.36), channel_id=1, replica_groups=mesh['rep'=1,'dp'=8] {'dp'}, use_global_device_ids=true, to_apply=%region_12.0 | all-reduce | flops 1 | bytes 8 | tf_op jit(solution)/shard_map/psum | solution.py:222
  438.1 21.3 %adamw.10 = (bf16[2,2304,896]{2,1,0:T(8,128)(2,1)}, f32[2,2304,896]{2,1,0:T(8,128)}, f32[2,2304,896]{2,1,0:T(8,128)}) custom-call(f32[1,1]{1,0:T(1,128)} %bitcast.2.factor_ref, bf16[2,2304,896]{2,1,0:T(8,128)(2,1)} %w_ref.11, f32[2,2304,896]{2,1,0:T(8,128)} %m_ref.11, f32[2,2304,896]{2,1,0:T(8,128)} %v_ref.11, ...), custom_call_target="tpu_custom_call" | custom-call | flops 82575360 | bytes 45416448 | tf_op jit(solution)/shard_map/adamw/pallas_call | solution.py:194
  464.7 20.5 %adamw.8 = (bf16[2,896,2304]{2,1,0:T(8,128)(2,1)}, f32[2,896,2304]{2,1,0:T(8,128)}, f32[2,896,2304]{2,1,0:T(8,128)}) custom-call(f32[1,1]{1,0:T(1,128)} %bitcast.2.factor_ref, bf16[2,896,2304]{2,1,0:T(8,128)(2,1)} %w_ref.9, f32[2,896,2304]{2,1,0:T(8,128)} %m_ref.9, f32[2,896,2304]{2,1,0:T(8,128)} %v_ref.9, bf16[896,2304]{1,0:T(8,128)(2,1)} %all-gather.13.cloned.1.call-done.g_ref), custom_call_target="tpu_custom_call" | custom-call | flops 82575360 | bytes 45416448 | tf_op jit(solution)/shard_map/adamw/pallas_call | solution.py:194
  485.2 11.8 %all-gather.9.cloned.1.call-done.g_ref = bf16[896,2304]{1,0:T(8,128)(2,1)} async-done(((bf16[112,2304]{1,0:T(8,128)(2,1)}), bf16[896,2304]{1,0:T(8,128)(2,1)}) %all-gather.9.cloned.1.call-update) | async-done | bytes 4128784 | tf_op jit(solution)/shard_map/all_gather | solution.py:213
  497.0 20.5 %adamw.6 = (bf16[2,896,2304]{2,1,0:T(8,128)(2,1)}, f32[2,896,2304]{2,1,0:T(8,128)}, f32[2,896,2304]{2,1,0:T(8,128)}) custom-call(f32[1,1]{1,0:T(1,128)} %bitcast.2.factor_ref, bf16[2,896,2304]{2,1,0:T(8,128)(2,1)} %w_ref.7, f32[2,896,2304]{2,1,0:T(8,128)} %m_ref.7, f32[2,896,2304]{2,1,0:T(8,128)} %v_ref.7, bf16[896,2304]{1,0:T(8,128)(2,1)} %all-gather.9.cloned.1.call-done.g_ref), custom_call_target="tpu_custom_call" | custom-call | flops 82575360 | bytes 45416448 | tf_op jit(solution)/shard_map/adamw/pallas_call | solution.py:194
  517.5 11.7 %all-gather.15.cloned.1.call-done.g_ref = bf16[2304,896]{1,0:T(8,128)(2,1)} async-done(((bf16[288,896]{1,0:T(8,128)(2,1)}), bf16[2304,896]{1,0:T(8,128)(2,1)}) %all-gather.15.cloned.1.call-update) | async-done | bytes 4128784 | tf_op jit(solution)/shard_map/all_gather | solution.py:213
  529.2 21.3 %adamw.11 = (bf16[2,2304,896]{2,1,0:T(8,128)(2,1)}, f32[2,2304,896]{2,1,0:T(8,128)}, f32[2,2304,896]{2,1,0:T(8,128)}) custom-call(f32[1,1]{1,0:T(1,128)} %bitcast.2.factor_ref, bf16[2,2304,896]{2,1,0:T(8,128)(2,1)} %w_ref.11, f32[2,2304,896]{2,1,0:T(8,128)} %m_ref.11, ...), custom_call_target="tpu_custom_call", output_to_operand_aliasing={{0}: (5, {}), {1}: (6, {}), {2}: (7, {})} | custom-call | flops 82575360 | bytes 45416448 | tf_op jit(solution)/shard_map/adamw/pallas_call | solution.py:194
  550.4 11.1 %all-gather.11.cloned.1.call-done.g_ref = bf16[896,2304]{1,0:T(8,128)(2,1)} async-done(((bf16[112,2304]{1,0:T(8,128)(2,1)}), bf16[896,2304]{1,0:T(8,128)(2,1)}) %all-gather.11.cloned.1.call-update) | async-done | bytes 4128784 | tf_op jit(solution)/shard_map/all_gather | solution.py:213
  561.5 20.5 %adamw.9 = (bf16[2,896,2304]{2,1,0:T(8,128)(2,1)}, f32[2,896,2304]{2,1,0:T(8,128)}, f32[2,896,2304]{2,1,0:T(8,128)}) custom-call(f32[1,1]{1,0:T(1,128)} %bitcast.2.factor_ref, bf16[2,896,2304]{2,1,0:T(8,128)(2,1)} %w_ref.9, f32[2,896,2304]{2,1,0:T(8,128)} %m_ref.9, ...), custom_call_target="tpu_custom_call", output_to_operand_aliasing={{0}: (5, {}), {1}: (6, {}), {2}: (7, {})} | custom-call | flops 82575360 | bytes 45416448 | tf_op jit(solution)/shard_map/adamw/pallas_call | solution.py:194
  582.0 11.7 %all-gather.7.cloned.1.call-done.g_ref = bf16[896,2304]{1,0:T(8,128)(2,1)} async-done(((bf16[112,2304]{1,0:T(8,128)(2,1)}), bf16[896,2304]{1,0:T(8,128)(2,1)}) %all-gather.7.cloned.1.call-update) | async-done | bytes 4128784 | tf_op jit(solution)/shard_map/all_gather | solution.py:213
  593.7 20.5 %adamw.7 = (bf16[2,896,2304]{2,1,0:T(8,128)(2,1)}, f32[2,896,2304]{2,1,0:T(8,128)}, f32[2,896,2304]{2,1,0:T(8,128)}) custom-call(f32[1,1]{1,0:T(1,128)} %bitcast.2.factor_ref, bf16[2,896,2304]{2,1,0:T(8,128)(2,1)} %w_ref.7, f32[2,896,2304]{2,1,0:T(8,128)} %m_ref.7, ...), custom_call_target="tpu_custom_call", output_to_operand_aliasing={{0}: (5, {}), {1}: (6, {}), {2}: (7, {})} | custom-call | flops 82575360 | bytes 45416448 | tf_op jit(solution)/shard_map/adamw/pallas_call | solution.py:194
  (34 shorter events, 18.8 us)
Async XLA Ops:
  7.2 212.5 %reduce-scatter.17.cloned.1.call-start = ((), (), s32[]{:S(2)}) async-start(), calls=%async_computation.11 | async-start | bytes 4644864 | tf_op jit(solution)/shard_map/reduce_scatter | solution.py:212
  124.0 96.5 %reduce-scatter.15.cloned.1.call-start = ((), (), s32[]{:S(2)}) async-start(), calls=%async_computation.10 | async-start | bytes 4644864 | tf_op jit(solution)/shard_map/reduce_scatter | solution.py:212
  137.7 123.8 %reduce-scatter.13.cloned.1.call-start = ((), (), s32[]{:S(2)}) async-start(), calls=%async_computation.9 | async-start | bytes 4644864 | tf_op jit(solution)/shard_map/reduce_scatter | solution.py:212
  150.9 156.5 %reduce-scatter.11.cloned.1.call-start = ((), (), s32[]{:S(2)}) async-start(), calls=%async_computation.8 | async-start | bytes 4644864 | tf_op jit(solution)/shard_map/reduce_scatter | solution.py:212
  165.4 188.1 %reduce-scatter.9.cloned.1.call-start = ((), (), s32[]{:S(2)}) async-start(), calls=%async_computation.7 | async-start | bytes 4644864 | tf_op jit(solution)/shard_map/reduce_scatter | solution.py:212
  206.2 193.2 %reduce-scatter.7.cloned.1.call-start = ((), (), s32[]{:S(2)}) async-start(), calls=%async_computation.6 | async-start | bytes 4644864 | tf_op jit(solution)/shard_map/reduce_scatter | solution.py:212
  219.7 218.5 %all-gather.17.cloned.1.call-start = ((), (), s32[]{:S(2)}) async-start(), calls=%async_computation.17 | async-start | bytes 4644864 | tf_op jit(solution)/shard_map/all_gather | solution.py:213
  220.4 244.3 %all-gather.13.cloned.1.call-start = ((), (), s32[]{:S(2)}) async-start(), calls=%async_computation.15 | async-start | bytes 4644864 | tf_op jit(solution)/shard_map/all_gather | solution.py:213
  221.2 275.9 %all-gather.9.cloned.1.call-start = ((), (), s32[]{:S(2)}) async-start(), calls=%async_computation.13 | async-start | bytes 4644864 | tf_op jit(solution)/shard_map/all_gather | solution.py:213
  261.5 267.7 %all-gather.15.cloned.1.call-start = ((), (), s32[]{:S(2)}) async-start(), calls=%async_computation.16 | async-start | bytes 4644864 | tf_op jit(solution)/shard_map/all_gather | solution.py:213
  307.5 254.0 %all-gather.11.cloned.1.call-start = ((), (), s32[]{:S(2)}) async-start(), calls=%async_computation.14 | async-start | bytes 4644864 | tf_op jit(solution)/shard_map/all_gather | solution.py:213
  353.5 240.2 %all-gather.7.cloned.1.call-start = ((), (), s32[]{:S(2)}) async-start(), calls=%async_computation.12 | async-start | bytes 4644864 | tf_op jit(solution)/shard_map/all_gather | solution.py:213
Sparse Core Ops, SparseCore 0:
  124.1 45.0 reduce-scatter.16
  173.1 42.1 reduce-scatter.14
  219.3 42.1 reduce-scatter.12
  265.2 42.1 reduce-scatter.10
  311.2 42.1 reduce-scatter.8
  357.2 42.1 reduce-scatter.6
  401.2 31.0 all-gather.16
  434.2 30.4 all-gather.12
  466.5 30.4 all-gather.8
  498.7 30.4 all-gather.14
  531.0 30.4 all-gather.10
  563.2 30.4 all-gather.6

commit v2 on v1

--- a/solution.py
+++ b/solution.py
@@ -1,5 +1,3 @@
-import functools
-
 import jax
 import jax.numpy as jnp
 from jax import lax
@@ -88,22 +86,15 @@
     return (silu * up).astype(BF16), by_gate.astype(BF16), (by_act * silu).astype(BF16)
 
 
-def top_kernel(h_ref, dy_ref, wg_ref, wu_ref, wd_ref, at_ref, actt_ref, bg_ref, bu_ref, bh_ref):
+def top_kernel(h_ref, dy_ref, wg_ref, wu_ref, wd_ref, at_ref, actt_ref, by_ref):
     h = h_ref[...].astype(F32)
-    scale = scale_of(h)
-    a = (h * scale).astype(BF16)
+    a = (h * scale_of(h)).astype(BF16)
     at_ref[...] = a.T
     for start in range(0, wg_ref.shape[1], CHUNK):
         cols = pl.ds(start, CHUNK)
         by_act = dot_t(dy_ref[...], wd_ref[cols, :]).astype(BF16).astype(F32)
-        act, by_gate, by_up = gate_up_back(dot(a, wg_ref[:, cols]), dot(a, wu_ref[:, cols]), by_act)
+        act, by_ref[0, :, cols], by_ref[1, :, cols] = gate_up_back(dot(a, wg_ref[:, cols]), dot(a, wu_ref[:, cols]), by_act)
         actt_ref[cols, :] = act.T
-        bg_ref[:, cols] = by_gate
-        bu_ref[:, cols] = by_up
-    by_a = (dot_t(bg_ref[...], wg_ref[...]) + dot_t(bu_ref[...], wu_ref[...])).astype(BF16).astype(F32)
-    h = h_ref[...].astype(F32)
-    by_h = scale * (by_a - h * (scale * scale * jnp.mean(by_a * h, -1, keepdims=True)))
-    bh_ref[...] = (dy_ref[...].astype(F32) + by_h).astype(BF16)
 
 
 def top(h, dy, wg, wu, wd, layer):
@@ -115,41 +106,195 @@
         top_kernel,
         grid=(t // ROWS,),
         in_specs=[rows(d), rows(d), whole(wg, layer), whole(wu, layer), whole(wd, layer)],
-        out_specs=[cols(d), cols(ff), rows(ff), rows(ff), rows(d)],
+        out_specs=[cols(d), cols(ff), pl.BlockSpec((2, ROWS, ff), lambda i: (0, i, 0))],
         out_shape=[
             jax.ShapeDtypeStruct((d, t), BF16),
             jax.ShapeDtypeStruct((ff, t), BF16),
-            jax.ShapeDtypeStruct((t, ff), BF16),
-            jax.ShapeDtypeStruct((t, ff), BF16),
-            jax.ShapeDtypeStruct((t, d), BF16),
+            jax.ShapeDtypeStruct((2, t, ff), BF16),
         ],
         compiler_params=params(),
-        cost_estimate=cost(10 * t * d * ff, 8 * t * ff),
+        cost_estimate=cost(6 * t * d * ff, 8 * t * ff),
         name="top",
     )(h, dy, wg, wu, wd)
 
 
-def hidden_back_kernel(by_ref, gate_ref, up_ref, wd_ref, bg_ref, bu_ref):
+class Scatter:
+    def __init__(self, g, out, squares, mine, got1, send2, got2, send3, got3, local, sent, received):
+        self.g, self.out, self.squares = g, out, squares
+        self.mine, self.got1, self.send2, self.got2, self.send3, self.got3 = mine, got1, send2, got2, send3, got3
+        self.local, self.sent, self.received = local, sent, received
+        me = lax.axis_index("dp")
+        self.x, self.y, self.core = me // 4, lax.rem(me // 2, 2), lax.rem(me, 2)
+        self.over_core, self.over_x, self.over_y = (self.device(*flip) for flip in ((0, 0, 1), (1, 0, 0), (0, 1, 0)))
+
+    def device(self, x, y, core):
+        flip = lambda at, by: 1 - at if by else at
+        return {"dp": flip(self.x, x) * 4 + flip(self.y, y) * 2 + flip(self.core, core)}
+
+    def part(self, ref, at, half):
+        r, c = half_shape(*ref.shape[1:])
+        if r == ref.shape[1]:
+            return ref[at, :, half * c : (half + 1) * c]
+        return ref[at, half * r : (half + 1) * r, :]
+
+    def own(self, at, half):
+        return self.part(self.mine, at, half).astype(F32) + self.part(self.got1, at, half).astype(F32)
+
+    def send(self, src, dst, number, device):
+        return pltpu.make_async_remote_copy(
+            src_ref=src, dst_ref=dst, send_sem=self.sent.at[number], recv_sem=self.received.at[number],
+            device_id=device, device_id_type=pl.DeviceIdType.MESH,
+        )
+
+    def fetch(self):
+        return pltpu.make_async_copy(self.g.at[:, self.core], self.mine, self.local)
+
+    def first(self):
+        return self.send(self.g.at[:, 1 - self.core], self.got1, 0, self.over_core)
+
+    def pair(self, src, dst, number, devices):
+        return [self.send(src.at[half], dst.at[half], number + half, devices[half]) for half in range(2)]
+
+    def second(self):
+        return self.pair(self.send2, self.got2, 1, (self.over_x, self.over_y))
+
+    def third(self):
+        return self.pair(self.send3, self.got3, 3, (self.over_y, self.over_x))
+
+    def begin(self):
+        barrier = pltpu.get_barrier_semaphore()
+        for device in (self.over_core, self.over_x, self.over_y):
+            pl.semaphore_signal(barrier, inc=1, device_id=device, device_id_type=pl.DeviceIdType.MESH)
+        pl.semaphore_wait(barrier, 3)
+        self.first().start()
+        self.fetch().start()
+
+    def go_second(self):
+        self.fetch().wait()
+        self.first().wait()
+        for j in range(2):
+            self.send2[0, j] = self.own(2 * (1 - self.x) + j, 0).astype(BF16)
+            self.send2[1, j] = self.own(2 * j + (1 - self.y), 1).astype(BF16)
+        for copy in self.second():
+            copy.start()
+
+    def go_third(self):
+        for copy in self.second():
+            copy.wait()
+        x, y = self.x, self.y
+        self.send3[0] = (self.own(2 * x + (1 - y), 0) + self.got2[0, 1 - y].astype(F32)).astype(BF16)
+        self.send3[1] = (self.own(2 * (1 - x) + y, 1) + self.got2[1, 1 - x].astype(F32)).astype(BF16)
+        for copy in self.third():
+            copy.start()
+
+    def end(self):
+        for copy in self.third():
+            copy.wait()
+        x, y = self.x, self.y
+        r, c = self.out.shape
+        hr, hc = half_shape(r, c)
+        for half, kept in ((0, self.got2[0, y]), (1, self.got2[1, x])):
+            total = (self.own(2 * x + y, half) + kept.astype(F32) + self.got3[half].astype(F32)).astype(BF16)
+            square = jnp.square(total.astype(F32))
+            if hr == r:
+                self.out[:, half * hc : (half + 1) * hc] = total
+                self.squares[:, half * hc : (half + 1) * hc] = jnp.sum(square, 0, keepdims=True)
+            else:
+                self.out[half * hr : (half + 1) * hr, :] = total
+                square = jnp.sum(square, 0, keepdims=True)
+                self.squares[...] = square if half == 0 else self.squares[...] + square
+
+
+def half_shape(r, c):
+    return (r, c // 2) if c % 256 == 0 else (r // 2, c)
+
+
+def by_device(term):
+    r, c = term.shape[-2:]
+    return term.reshape(term.shape[:-2] + (4, 2, r // 8, c))
+
+
+def scattering(compute, grid, steps, in_specs, args, out_specs, out_shape, term, which, collective_id, name, cost_estimate):
+    term = by_device(term)
+    r, c = term.shape[-2:]
+    hr, hc = half_shape(r, c)
+    n_in, n_out = len(args), len(out_shape)
+
+    def kernel(*refs):
+        ins, g, outs, (out, squares), scratch = refs[:n_in], refs[n_in], refs[n_in + 1 :][:n_out], refs[n_in + 1 + n_out :][:2], refs[n_in + 3 + n_out :]
+        scatter = Scatter(g if which is None else g.at[which], out, squares, *scratch)
+        step = pl.program_id(0)
+        pl.when(step == 0)(scatter.begin)
+        if compute is not None:
+            compute(*ins, *outs)
+        pl.when(step == steps[0])(scatter.go_second)
+        pl.when(step == steps[1])(scatter.go_third)
+        pl.when(step == grid - 1)(scatter.end)
+
+    fixed = lambda *shape: pl.BlockSpec(shape, lambda i: (0,) * len(shape))
+    return pl.pallas_call(
+        kernel,
+        grid=(grid,),
+        in_specs=list(in_specs) + [pl.BlockSpec(memory_space=pl.ANY)],
+        out_specs=list(out_specs) + [fixed(r, c), fixed(1, c)],
+        out_shape=list(out_shape) + [jax.ShapeDtypeStruct((r, c), BF16), jax.ShapeDtypeStruct((1, c), F32)],
+        scratch_shapes=[
+            pltpu.VMEM((4, r, c), BF16),
+            pltpu.VMEM((4, r, c), BF16),
+            pltpu.VMEM((2, 2, hr, hc), BF16),
+            pltpu.VMEM((2, 2, hr, hc), BF16),
+            pltpu.VMEM((2, hr, hc), BF16),
+            pltpu.VMEM((2, hr, hc), BF16),
+            pltpu.SemaphoreType.DMA,
+            pltpu.SemaphoreType.DMA((5,)),
+            pltpu.SemaphoreType.DMA((5,)),
+        ],
+        compiler_params=pltpu.CompilerParams(
+            dimension_semantics=("arbitrary",), vmem_limit_bytes=VMEM_LIMIT, collective_id=collective_id, has_side_effects=True
+        ),
+        cost_estimate=cost_estimate,
+        name=name,
+    )(*args, term)
+
+
+def input_back_kernel(h_ref, dy_ref, by_ref, wg_ref, wu_ref, bh_ref):
+    by_a = (dot_t(by_ref[0], wg_ref[...]) + dot_t(by_ref[1], wu_ref[...])).astype(BF16).astype(F32)
+    h = h_ref[...].astype(F32)
+    scale = scale_of(h)
+    by_h = scale * (by_a - h * (scale * scale * jnp.mean(by_a * h, -1, keepdims=True)))
+    bh_ref[...] = (dy_ref[...].astype(F32) + by_h).astype(BF16)
+
+
+def input_back(h, dy, by, wg, wu, layer, term, which, collective_id):
+    t, d = h.shape
+    ff = wg.shape[2]
+    rows = lambda n: pl.BlockSpec((ROWS, n), lambda i: (i, 0))
+    return scattering(
+        input_back_kernel, t // ROWS, (0, 2),
+        [rows(d), rows(d), pl.BlockSpec((2, ROWS, ff), lambda i: (0, i, 0)), whole(wg, layer), whole(wu, layer)],
+        (h, dy, by, wg, wu),
+        [rows(d)], [jax.ShapeDtypeStruct((t, d), BF16)],
+        term, which, collective_id, "input_back", cost(4 * t * d * ff, 6 * t * ff),
+    )
+
+
+def hidden_back_kernel(by_ref, gate_ref, up_ref, wd_ref, out_ref):
     for start in range(0, gate_ref.shape[1], CHUNK):
         cols = pl.ds(start, CHUNK)
         by_act = dot_t(by_ref[...], wd_ref[cols, :]).astype(BF16).astype(F32)
-        _, bg_ref[:, cols], bu_ref[:, cols] = gate_up_back(gate_ref[:, cols], up_ref[:, cols], by_act)
-
-
-def hidden_back(by, gate, up, wd, layer):
+        _, out_ref[0, :, cols], out_ref[1, :, cols] = gate_up_back(gate_ref[:, cols], up_ref[:, cols], by_act)
+
+
+def hidden_back(by, gate, up, wd, layer, term, which, collective_id):
     t, d = by.shape
     ff = gate.shape[1]
     rows = lambda n: pl.BlockSpec((ROWS, n), lambda i: (i, 0))
-    return pl.pallas_call(
-        hidden_back_kernel,
-        grid=(t // ROWS,),
-        in_specs=[rows(d), rows(ff), rows(ff), whole(wd, layer)],
-        out_specs=[rows(ff), rows(ff)],
-        out_shape=[jax.ShapeDtypeStruct((t, ff), BF16)] * 2,
-        compiler_params=params(),
-        cost_estimate=cost(2 * t * d * ff, 12 * t * ff),
-        name="hidden_back",
-    )(by, gate, up, wd)
+    return scattering(
+        hidden_back_kernel, t // ROWS, (0, 2),
+        [rows(d), rows(ff), rows(ff), whole(wd, layer)], (by, gate, up, wd),
+        [pl.BlockSpec((2, ROWS, ff), lambda i: (0, i, 0))], [jax.ShapeDtypeStruct((2, t, ff), BF16)],
+        term, which, collective_id, "hidden_back", cost(2 * t * d * ff, 12 * t * ff),
+    )
 
 
 def product_kernel(a_ref, b_ref, c_ref):
@@ -158,22 +303,30 @@
 
 def product(a, b, name):
     (m, k), n = a.shape, b.shape[1]
-    if m > n:
-        specs = [pl.BlockSpec((CHUNK, k), lambda i: (i, 0)), pl.BlockSpec((k, n), lambda i: (0, 0), pipeline_mode=pl.Buffered(1))]
-        out = pl.BlockSpec((CHUNK, n), lambda i: (i, 0))
-    else:
-        specs = [pl.BlockSpec((m, k), lambda i: (0, 0), pipeline_mode=pl.Buffered(1)), pl.BlockSpec((k, CHUNK), lambda i: (0, i))]
-        out = pl.BlockSpec((m, CHUNK), lambda i: (0, i))
     return pl.pallas_call(
         product_kernel,
-        grid=(max(m, n) // CHUNK,),
-        in_specs=specs,
-        out_specs=out,
+        grid=(m // CHUNK,),
+        in_specs=[pl.BlockSpec((CHUNK, k), lambda i: (i, 0)), pl.BlockSpec((k, n), lambda i: (0, 0), pipeline_mode=pl.Buffered(1))],
+        out_specs=pl.BlockSpec((CHUNK, n), lambda i: (i, 0)),
         out_shape=jax.ShapeDtypeStruct((m, n), BF16),
         compiler_params=params(),
         cost_estimate=cost(2 * m * n * k, 2 * (m * k + k * n + m * n)),
         name=name,
     )(a, b)
+
+
+def products(a, b, those, steps, term, which, collective_id):
+    (m, k), n = a.shape, b.shape[2]
+    chunks = n // CHUNK
+    grid = len(those) * chunks
+    first = those[0]
+    return scattering(
+        product_kernel, grid, steps,
+        [pl.BlockSpec((m, k), lambda i: (0, 0), pipeline_mode=pl.Buffered(1)), pl.BlockSpec((None, k, CHUNK), lambda i: (first + i // chunks, 0, lax.rem(i, chunks)))],
+        (a, b),
+        [pl.BlockSpec((None, m, CHUNK), lambda i: (i // chunks, 0, lax.rem(i, chunks)))], [jax.ShapeDtypeStruct((len(those), m, n), BF16)],
+        term, which, collective_id, "products", cost(2 * m * n * k * len(those), 2 * (m * k + k * n + m * n) * len(those)),
+    )
 
 
 def adamw_kernel(factor_ref, w_ref, m_ref, v_ref, g_ref, *refs):
@@ -189,7 +342,7 @@
 
 def adamw(factor, w, m, v, g, layer, so_far):
     _, r, c = w.shape
-    block = r // 14 if r % 224 == 0 else r // 16
+    block = r // 7 if r % 112 == 0 else r // 8
     part = pl.BlockSpec((None, block, c), lambda i: (layer, i, 0))
     return pl.pallas_call(
         adamw_kernel,
@@ -209,23 +362,36 @@
     def step(x, dy, *arrays):
         weights, ms, vs = (arrays[i : i + 3] for i in (0, 3, 6))
         x, dy = x[0], dy[0]
-        scatter = lambda g: lax.psum_scatter(g, "dp", scatter_dimension=0, tiled=True)
         gather = lambda g: lax.all_gather(g, "dp", axis=0, tiled=True)
 
         at0, gate0, up0, actt0, h1 = forward(x, *weights, 0)
-        at1, actt1, bg1, bu1, bh1 = top(h1, dy, *weights, 1)
-        terms1 = [product(at1, bg1, "gate1"), product(at1, bu1, "up1"), product(actt1, dy, "down1")]
-        bg0, bu0 = hidden_back(bh1, gate0, up0, weights[2], 0)
-        terms0 = [product(at0, bg0, "gate0"), product(at0, bu0, "up0"), product(actt0, bh1, "down0")]
-        shards = [[scatter(g) for g in terms] for terms in (terms0, terms1)]
-        total = sum(jnp.sum(jnp.square(g.astype(F32))) for part in shards for g in part)
-        total = lax.psum(total, "dp")
+        at1, actt1, by1 = top(h1, dy, *weights, 1)
+        shards, squares = [[None] * 3, [None] * 3], []
+
+        def keep(layer, i, shard, square):
+            shards[layer][i] = shard
+            squares.append(square)
+
+        down1 = product(actt1, dy, "down1")
+        pair1, *rest = products(at1, by1, (0, 1), (0, 3), down1, None, 1)
+        keep(1, 2, *rest)
+        bh1, *rest = input_back(h1, dy, by1, *weights[:2], 1, pair1, 0, 2)
+        keep(1, 0, *rest)
+        down0 = product(actt0, bh1, "down0")
+        by0, *rest = hidden_back(bh1, gate0, up0, weights[2], 0, pair1, 1, 3)
+        keep(1, 1, *rest)
+        gate_term, *rest = products(at0, by0, (0,), (0, 2), down0, None, 4)
+        keep(0, 2, *rest)
+        up_term, *rest = products(at0, by0, (1,), (0, 2), gate_term, 0, 5)
+        keep(0, 0, *rest)
+        keep(0, 1, *scattering(None, 1, (0, 0), [], (), [], [], up_term, 0, 6, "scatter", cost(2**30, 2**20)))
+        total = lax.psum(sum(jnp.sum(square) for square in squares), "dp")
         count = sum(w.size for w in weights)
         factor = jnp.minimum(1.0, 0.5 * lax.rsqrt(total / count + 1e-30)).reshape(1, 1)
 
         new = [()] * 3
         for layer in (1, 0):
-            for i in range(3):
+            for i in (2, 0, 1):
                 new[i] = adamw(factor, weights[i], ms[i], vs[i], gather(shards[layer][i]), layer, new[i])
         return tuple(one[which] for which in range(3) for one in new)
 

time: 629 us -> 498 us (0.79)
  waiting for transfers between devices: 231 us -> 0.95 us
  Pallas kernels: 337 us -> 444 us
  other arithmetic: 11.5 us -> 5.1 us
    reduce_scatter x6 -> x0, waiting for transfers between devices: 178 us -> none  [step(): lax.psum_scatter(g, 'dp', scatter_dimension=0, tiled=True)]
    pallas_call x7 -> x8, Pallas kernels: 110 us -> 255 us  [the longest x6 226 us: scattering(): pl.pallas_call(kernel, grid=(grid,), in_specs=list(in_specs) + [pl.BlockS...]
    all_gather x6, waiting for transfers between devices: 51.5 us -> 0.09 us  [step(): gather = lambda g: lax.all_gather(g, 'dp', axis=0, tiled=True)]
    pallas_call x1, Pallas kernels: 62.7 us -> 41.4 us  [top(): pl.pallas_call(top_kernel, grid=(t // ROWS,), in_specs=[rows(d), rows(d),...]
    pallas_call x6, Pallas kernels: 125 us -> 108 us  [adamw(): pl.pallas_call(adamw_kernel, grid=(r // block,), in_specs=[pl.BlockSpec(m...]
    reduce_sum x6, other arithmetic: 11.5 us -> 5.1 us  [step(): total = lax.psum(sum((jnp.sum(square) for square in squares)), 'dp')]
  transfers between devices with their start and end apart: 12 -> 6, of which waited for: 9 -> 0; matrix products, arithmetic and copies ran while one was open for 2% -> 1% of each run, Pallas kernels for 32% -> 60%
where the time goes in v2:
time: 498 us; the launch traced here: 493 us
  Pallas kernels  444 us (89%)
  blocking collectives  22.8 us (5%)
  between operations  19 us (4%)
  other arithmetic  5.1 us (1%)
    pallas_call x6, Pallas kernels, scattering(): pl.pallas_call(kernel, grid=(grid,), in_specs=list(in_specs) + [pl.BlockS...  226 us
    pallas_call x6, Pallas kernels, adamw(): pl.pallas_call(adamw_kernel, grid=(r // block,), in_specs=[pl.BlockSpec(m...  108 us
    pallas_call x1, Pallas kernels, top(): pl.pallas_call(top_kernel, grid=(t // ROWS,), in_specs=[rows(d), rows(d),...  41.4 us
    pallas_call x1, Pallas kernels, forward(): pl.pallas_call(forward_kernel, grid=(t // ROWS,), in_specs=[rows(d), whol...  39.7 us
    pallas_call x2, Pallas kernels, product(): pl.pallas_call(product_kernel, grid=(m // CHUNK,), in_specs=[pl.BlockSpec...  28.7 us
    psum x1, blocking collectives, step(): total = lax.psum(sum((jnp.sum(square) for square in squares)), 'dp')  22.8 us
  transfers between devices with their start and end apart: 6, of which 0 were waited for; matrix products, arithmetic and copies ran while one was open for 1% of the time, Pallas kernels for 60%

profile of v2, /device:TPU:0, one launch (start us, length us, event | category | flops | bytes accessed | tf_op | source)
XLA Modules:
  0.0 492.6 jit_solution(7016518286225830623)
XLA Ops:
  7.2 39.7 %forward.1 = (bf16[896,2048]{1,0:T(8,128)(2,1)}, f32[2048,2304]{1,0:T(8,128)}, f32[2048,2304]{1,0:T(8,128)}, bf16[2304,2048]{1,0:T(8,128)(2,1)}, bf16[2048,896]{1,0:T(8,128)(2,1)}) custom-call(bf16[2048,896]{1,0:T(8,128)(2,1)} %bitcast.11, bf16[2,896,2304]{2,1,0:T(8,128)(2,1)} %w_ref.7, bf16[2,896,2304]{2,1,0:T(8,128)(2,1)} %w_ref.9, ...), custom_call_target="tpu_custom_call" | custom-call | flops 25367150592 | bytes 56623104 | tf_op jit(solution)/shard_map/forward/pallas_call | solution.py:64
  46.9 41.4 %top.1 = (bf16[896,2048]{1,0:T(8,128)(2,1)}, bf16[2304,2048]{1,0:T(8,128)(2,1)}, bf16[2,2048,2304]{2,1,0:T(8,128)(2,1)}) custom-call(bf16[2048,896]{1,0:T(8,128)(2,1)} %get-tuple-element.52.h_ref.refs_0_, bf16[2048,896]{1,0:T(8,128)(2,1)} %bitcast.12, bf16[2,896,2304]{2,1,0:T(8,128)(2,1)} %w_ref.7, bf16[2,896,2304]{2,1,0:T(8,128)(2,1)} %w_ref.9, ...), custom_call_target="tpu_custom_call" | custom-call | flops 25367150592 | bytes 37748736 | tf_op jit(solution)/shard_map/top/pallas_call | solution.py:105
  88.3 14.3 %down1.1 = bf16[2304,896]{1,0:T(8,128)(2,1)} custom-call(bf16[2304,2048]{1,0:T(8,128)(2,1)} %get-tuple-element.55.a_ref, bf16[2048,896]{1,0:T(8,128)(2,1)} %bitcast.13), custom_call_target="tpu_custom_call" | custom-call | flops 8455716864 | bytes 17235968 | tf_op jit(solution)/shard_map/down1/pallas_call | solution.py:306
  102.6 33.4 %products.3 = (bf16[2,896,2304]{2,1,0:T(8,128)(2,1)}, bf16[288,896]{1,0:T(8,128)(2,1)}, f32[1,896]{1,0:T(1,128)}) custom-call(bf16[896,2048]{1,0:T(8,128)(2,1)} %get-tuple-element.53.refs_0_, bf16[2,2048,2304]{2,1,0:T(8,128)(2,1)} %get-tuple-element.54.refs_1_.refs_2_, bf16[4,2,288,896]{3,2,1,0:T(8,128)(2,1)} %bitcast.16), custom_call_target="tpu_custom_call" | custom-call | flops 16911433728 | bytes 34471936 | tf_op jit(solution)/shard_map/products/pallas_call | solution.py:235
  136.1 43.1 %input_back.1 = (bf16[2048,896]{1,0:T(8,128)(2,1)}, bf16[112,2304]{1,0:T(8,128)(2,1)}, f32[1,2304]{1,0:T(1,128)}) custom-call(bf16[2048,896]{1,0:T(8,128)(2,1)} %get-tuple-element.52.h_ref.refs_0_, bf16[2048,896]{1,0:T(8,128)(2,1)} %bitcast.14, bf16[2,2048,2304]{2,1,0:T(8,128)(2,1)} %get-tuple-element.54.refs_1_.refs_2_, bf16[2,896,2304]{2,1,0:T(8,128)(2,1)} %w_ref.7, ...), custom_call_target="tpu_custom_call" | custom-call | flops 16911433728 | bytes 28311552 | tf_op jit(solution)/shard_map/input_back/pallas_call | solution.py:235
  179.3 34.8 %hidden_back.1 = (bf16[2,2048,2304]{2,1,0:T(8,128)(2,1)}, bf16[112,2304]{1,0:T(8,128)(2,1)}, f32[1,2304]{1,0:T(1,128)}) custom-call(bf16[2048,896]{1,0:T(8,128)(2,1)} %get-tuple-element.59.refs_0_.b_ref, f32[2048,2304]{1,0:T(8,128)} %get-tuple-element.60.refs_1_, f32[2048,2304]{1,0:T(8,128)} %get-tuple-element.61.refs_2_, bf16[2,2304,896]{2,1,0:T(8,128)(2,1)} %w_ref.11, ...), custom_call_target="tpu_custom_call" | custom-call | flops 8455716864 | bytes 56623104 | tf_op jit(solution)/shard_map/hidden_back/pallas_call | solution.py:235
  214.9 14.3 %down0.1 = bf16[2304,896]{1,0:T(8,128)(2,1)} custom-call(bf16[2304,2048]{1,0:T(8,128)(2,1)} %get-tuple-element.65.a_ref, bf16[2048,896]{1,0:T(8,128)(2,1)} %get-tuple-element.59.refs_0_.b_ref), custom_call_target="tpu_custom_call" | custom-call | flops 8455716864 | bytes 17235968 | tf_op jit(solution)/shard_map/down0/pallas_call | solution.py:306
  229.3 40.0 %products.4 = (bf16[1,896,2304]{2,1,0:T(8,128)(2,1)}, bf16[288,896]{1,0:T(8,128)(2,1)}, f32[1,896]{1,0:T(1,128)}) custom-call(bf16[896,2048]{1,0:T(8,128)(2,1)} %get-tuple-element.63.refs_0_, bf16[2,2048,2304]{2,1,0:T(8,128)(2,1)} %get-tuple-element.64.refs_1_, bf16[4,2,288,896]{3,2,1,0:T(8,128)(2,1)} %bitcast.17), custom_call_target="tpu_custom_call" | custom-call | flops 8455716864 | bytes 17235968 | tf_op jit(solution)/shard_map/products/pallas_call | solution.py:235
  269.4 39.6 %products.5 = (bf16[1,896,2304]{2,1,0:T(8,128)(2,1)}, bf16[112,2304]{1,0:T(8,128)(2,1)}, f32[1,2304]{1,0:T(1,128)}) custom-call(bf16[896,2048]{1,0:T(8,128)(2,1)} %get-tuple-element.63.refs_0_, bf16[2,2048,2304]{2,1,0:T(8,128)(2,1)} %get-tuple-element.64.refs_1_, bf16[1,4,2,112,2304]{4,3,2,1,0:T(8,128)(2,1)} %bitcast.15), custom_call_target="tpu_custom_call" | custom-call | flops 8455716864 | bytes 17235968 | tf_op jit(solution)/shard_map/products/pallas_call | solution.py:235
  309.0 35.5 %scatter.1 = (bf16[112,2304]{1,0:T(8,128)(2,1)}, f32[1,2304]{1,0:T(1,128)}) custom-call(bf16[1,4,2,112,2304]{4,3,2,1,0:T(8,128)(2,1)} %bitcast.10), custom_call_target="tpu_custom_call" | custom-call | flops 1073741824 | bytes 1048576 | tf_op jit(solution)/shard_map/scatter/pallas_call | solution.py:235
  344.5 0.5 all-gather.7.cloned.1.call-update
  345.1 0.6 reduce_sum.54
  345.7 0.6 reduce_sum.56
  346.3 0.6 reduce_sum.55
  346.9 0.6 reduce_sum.57
  347.5 1.3 reduce_sum.58
  348.9 1.3 reduce_sum.59
  354.1 22.8 %psum.7 = f32[]{:T(128)} all-reduce(f32[]{:T(128)S(6)} %add.24), channel_id=1, replica_groups=mesh['rep'=1,'dp'=8] {'dp'}, use_global_device_ids=true, to_apply=%region_6.0 | all-reduce | flops 1 | bytes 8 | tf_op jit(solution)/shard_map/psum | solution.py:388
  377.6 17.4 %adamw.10 = (bf16[2,2304,896]{2,1,0:T(8,128)(2,1)}, f32[2,2304,896]{2,1,0:T(8,128)}, f32[2,2304,896]{2,1,0:T(8,128)}) custom-call(f32[1,1]{1,0:T(1,128)} %bitcast.7.factor_ref, bf16[2,2304,896]{2,1,0:T(8,128)(2,1)} %w_ref.11, f32[2,2304,896]{2,1,0:T(8,128)} %m_ref.11, f32[2,2304,896]{2,1,0:T(8,128)} %v_ref.11, ...), custom_call_target="tpu_custom_call" | custom-call | flops 82575360 | bytes 45416448 | tf_op jit(solution)/shard_map/adamw/pallas_call | solution.py:347
  395.0 18.3 %adamw.8 = (bf16[2,896,2304]{2,1,0:T(8,128)(2,1)}, f32[2,896,2304]{2,1,0:T(8,128)}, f32[2,896,2304]{2,1,0:T(8,128)}) custom-call(f32[1,1]{1,0:T(1,128)} %bitcast.7.factor_ref, bf16[2,896,2304]{2,1,0:T(8,128)(2,1)} %w_ref.9, f32[2,896,2304]{2,1,0:T(8,128)} %m_ref.9, f32[2,896,2304]{2,1,0:T(8,128)} %v_ref.9, bf16[896,2304]{1,0:T(8,128)(2,1)} %all-gather.13.cloned.1.call-done.g_ref), custom_call_target="tpu_custom_call" | custom-call | flops 82575360 | bytes 45416448 | tf_op jit(solution)/shard_map/adamw/pallas_call | solution.py:347
  413.3 18.3 %adamw.6 = (bf16[2,896,2304]{2,1,0:T(8,128)(2,1)}, f32[2,896,2304]{2,1,0:T(8,128)}, f32[2,896,2304]{2,1,0:T(8,128)}) custom-call(f32[1,1]{1,0:T(1,128)} %bitcast.7.factor_ref, bf16[2,896,2304]{2,1,0:T(8,128)(2,1)} %w_ref.7, f32[2,896,2304]{2,1,0:T(8,128)} %m_ref.7, f32[2,896,2304]{2,1,0:T(8,128)} %v_ref.7, bf16[896,2304]{1,0:T(8,128)(2,1)} %all-gather.9.cloned.1.call-done.g_ref), custom_call_target="tpu_custom_call" | custom-call | flops 82575360 | bytes 45416448 | tf_op jit(solution)/shard_map/adamw/pallas_call | solution.py:347
  431.6 17.4 %adamw.11 = (bf16[2,2304,896]{2,1,0:T(8,128)(2,1)}, f32[2,2304,896]{2,1,0:T(8,128)}, f32[2,2304,896]{2,1,0:T(8,128)}) custom-call(f32[1,1]{1,0:T(1,128)} %bitcast.7.factor_ref, bf16[2,2304,896]{2,1,0:T(8,128)(2,1)} %w_ref.11, f32[2,2304,896]{2,1,0:T(8,128)} %m_ref.11, ...), custom_call_target="tpu_custom_call", output_to_operand_aliasing={{0}: (5, {}), {1}: (6, {}), {2}: (7, {})} | custom-call | flops 82575360 | bytes 45416448 | tf_op jit(solution)/shard_map/adamw/pallas_call | solution.py:347
  449.0 18.3 %adamw.9 = (bf16[2,896,2304]{2,1,0:T(8,128)(2,1)}, f32[2,896,2304]{2,1,0:T(8,128)}, f32[2,896,2304]{2,1,0:T(8,128)}) custom-call(f32[1,1]{1,0:T(1,128)} %bitcast.7.factor_ref, bf16[2,896,2304]{2,1,0:T(8,128)(2,1)} %w_ref.9, f32[2,896,2304]{2,1,0:T(8,128)} %m_ref.9, ...), custom_call_target="tpu_custom_call", output_to_operand_aliasing={{0}: (5, {}), {1}: (6, {}), {2}: (7, {})} | custom-call | flops 82575360 | bytes 45416448 | tf_op jit(solution)/shard_map/adamw/pallas_call | solution.py:347
  467.3 18.3 %adamw.7 = (bf16[2,896,2304]{2,1,0:T(8,128)(2,1)}, f32[2,896,2304]{2,1,0:T(8,128)}, f32[2,896,2304]{2,1,0:T(8,128)}) custom-call(f32[1,1]{1,0:T(1,128)} %bitcast.7.factor_ref, bf16[2,896,2304]{2,1,0:T(8,128)(2,1)} %w_ref.7, f32[2,896,2304]{2,1,0:T(8,128)} %m_ref.7, ...), custom_call_target="tpu_custom_call", output_to_operand_aliasing={{0}: (5, {}), {1}: (6, {}), {2}: (7, {})} | custom-call | flops 82575360 | bytes 45416448 | tf_op jit(solution)/shard_map/adamw/pallas_call | solution.py:347
  (25 shorter events, 1.1 us)
Async XLA Ops:
  7.2 370.4 %all-gather.17.cloned.1.call-start = ((), (), s32[]{:S(2)}) async-start(), calls=%async_computation.5 | async-start | bytes 4644864 | tf_op jit(solution)/shard_map/all_gather | solution.py:365
  136.1 258.9 %all-gather.13.cloned.1.call-start = ((), (), s32[]{:S(2)}) async-start(), calls=%async_computation.3 | async-start | bytes 4644864 | tf_op jit(solution)/shard_map/all_gather | solution.py:365
  214.1 199.2 %all-gather.9.cloned.1.call-start = ((), (), s32[]{:S(2)}) async-start(), calls=%async_computation.1 | async-start | bytes 4644864 | tf_op jit(solution)/shard_map/all_gather | solution.py:365
  214.9 216.7 %all-gather.15.cloned.1.call-start = ((), (), s32[]{:S(2)}) async-start(), calls=%async_computation.4 | async-start | bytes 4644864 | tf_op jit(solution)/shard_map/all_gather | solution.py:365
  269.3 179.7 %all-gather.11.cloned.1.call-start = ((), (), s32[]{:S(2)}) async-start(), calls=%async_computation.2 | async-start | bytes 4644864 | tf_op jit(solution)/shard_map/all_gather | solution.py:365
  269.3 75.7 %copy-start.2 = (f32[1,896]{1,0:T(1,128)S(1)}, f32[1,896]{1,0:T(1,128)}, u32[]{:S(2)}) copy-start(f32[1,896]{1,0:T(1,128)} %get-tuple-element.56) | copy-start | bytes 10756
  269.4 76.3 %copy-start.1 = (f32[1,2304]{1,0:T(1,128)S(1)}, f32[1,2304]{1,0:T(1,128)}, u32[]{:S(2)}) copy-start(f32[1,2304]{1,0:T(1,128)} %get-tuple-element.62) | copy-start | bytes 27652
  269.4 76.9 %copy-start = (f32[1,2304]{1,0:T(1,128)S(1)}, f32[1,2304]{1,0:T(1,128)}, u32[]{:S(2)}) copy-start(f32[1,2304]{1,0:T(1,128)} %get-tuple-element.58) | copy-start | bytes 27652
  269.4 77.6 %copy-start.3 = (f32[1,896]{1,0:T(1,128)S(1)}, f32[1,896]{1,0:T(1,128)}, u32[]{:S(2)}) copy-start(f32[1,896]{1,0:T(1,128)} %get-tuple-element.66) | copy-start | bytes 10756
  344.5 122.8 %all-gather.7.cloned.1.call-start = ((), (), s32[]{:S(2)}) async-start(), calls=%async_computation | async-start | bytes 4644864 | tf_op jit(solution)/shard_map/all_gather | solution.py:365
Sparse Core Ops, SparseCore 0:
  136.2 40.8 all-gather.16
  214.2 34.1 all-gather.12
  250.2 39.0 all-gather.8
  291.0 41.2 all-gather.14
  344.6 31.1 all-gather.10
  377.5 30.4 all-gather.6

commit v3 on v2

--- a/solution.py
+++ b/solution.py
@@ -209,6 +209,12 @@
     return (r, c // 2) if c % 256 == 0 else (r // 2, c)
 
 
+def scatter_scratch(r, c):
+    hr, hc = half_shape(r, c)
+    blocks = ((4, r, c), (4, r, c), (2, 2, hr, hc), (2, 2, hr, hc), (2, hr, hc), (2, hr, hc))
+    return [pltpu.VMEM(block, BF16) for block in blocks] + [pltpu.SemaphoreType.DMA, pltpu.SemaphoreType.DMA((5,)), pltpu.SemaphoreType.DMA((5,))]
+
+
 def by_device(term):
     r, c = term.shape[-2:]
     return term.reshape(term.shape[:-2] + (4, 2, r // 8, c))
@@ -217,7 +223,6 @@
 def scattering(compute, grid, steps, in_specs, args, out_specs, out_shape, term, which, collective_id, name, cost_estimate):
     term = by_device(term)
     r, c = term.shape[-2:]
-    hr, hc = half_shape(r, c)
     n_in, n_out = len(args), len(out_shape)
 
     def kernel(*refs):
@@ -225,8 +230,7 @@
         scatter = Scatter(g if which is None else g.at[which], out, squares, *scratch)
         step = pl.program_id(0)
         pl.when(step == 0)(scatter.begin)
-        if compute is not None:
-            compute(*ins, *outs)
+        compute(*ins, *outs)
         pl.when(step == steps[0])(scatter.go_second)
         pl.when(step == steps[1])(scatter.go_third)
         pl.when(step == grid - 1)(scatter.end)
@@ -238,23 +242,53 @@
         in_specs=list(in_specs) + [pl.BlockSpec(memory_space=pl.ANY)],
         out_specs=list(out_specs) + [fixed(r, c), fixed(1, c)],
         out_shape=list(out_shape) + [jax.ShapeDtypeStruct((r, c), BF16), jax.ShapeDtypeStruct((1, c), F32)],
-        scratch_shapes=[
-            pltpu.VMEM((4, r, c), BF16),
-            pltpu.VMEM((4, r, c), BF16),
-            pltpu.VMEM((2, 2, hr, hc), BF16),
-            pltpu.VMEM((2, 2, hr, hc), BF16),
-            pltpu.VMEM((2, hr, hc), BF16),
-            pltpu.VMEM((2, hr, hc), BF16),
-            pltpu.SemaphoreType.DMA,
-            pltpu.SemaphoreType.DMA((5,)),
-            pltpu.SemaphoreType.DMA((5,)),
-        ],
+        scratch_shapes=scatter_scratch(r, c),
         compiler_params=pltpu.CompilerParams(
             dimension_semantics=("arbitrary",), vmem_limit_bytes=VMEM_LIMIT, collective_id=collective_id, has_side_effects=True
         ),
         cost_estimate=cost_estimate,
         name=name,
     )(*args, term)
+
+
+def last_scatter(term, which, squares, collective_id):
+    term = by_device(term)
+    r, c = term.shape[-2:]
+
+    def kernel(*refs):
+        g, others, (out, total_ref), (own, mine, theirs, *scratch) = refs[0], refs[1 : 1 + len(squares)], refs[1 + len(squares) :][:2], refs[3 + len(squares) :]
+        *scratch, sent, received = scratch
+        scatter = Scatter(g.at[which], out, own, *scratch)
+        scatter.begin()
+        rest = sum(jnp.sum(other[...], keepdims=True) for other in others)
+        scatter.go_second()
+        scatter.go_third()
+        scatter.end()
+        total = jnp.broadcast_to(rest + jnp.sum(own[...], keepdims=True), (8, 128))
+        for i, device in enumerate((scatter.over_core, scatter.over_x, scatter.over_y)):
+            mine[i] = total
+            copy = pltpu.make_async_remote_copy(
+                src_ref=mine.at[i], dst_ref=theirs.at[i], send_sem=sent.at[i], recv_sem=received.at[i],
+                device_id=device, device_id_type=pl.DeviceIdType.MESH,
+            )
+            copy.start()
+            copy.wait()
+            total = total + theirs[i]
+        total_ref[...] = total
+
+    vmem = pl.BlockSpec(memory_space=pltpu.VMEM)
+    return pl.pallas_call(
+        kernel,
+        in_specs=[pl.BlockSpec(memory_space=pl.ANY)] + [vmem] * len(squares),
+        out_specs=[vmem, vmem],
+        out_shape=[jax.ShapeDtypeStruct((r, c), BF16), jax.ShapeDtypeStruct((8, 128), F32)],
+        scratch_shapes=[pltpu.VMEM((1, c), F32), pltpu.VMEM((3, 8, 128), F32), pltpu.VMEM((3, 8, 128), F32)]
+        + scatter_scratch(r, c)
+        + [pltpu.SemaphoreType.DMA((3,)), pltpu.SemaphoreType.DMA((3,))],
+        compiler_params=pltpu.CompilerParams(vmem_limit_bytes=VMEM_LIMIT, collective_id=collective_id, has_side_effects=True),
+        cost_estimate=cost(2**34, 2**20),
+        name="last_scatter",
+    )(term, *squares)
 
 
 def input_back_kernel(h_ref, dy_ref, by_ref, wg_ref, wu_ref, bh_ref):
@@ -329,33 +363,56 @@
     )
 
 
-def adamw_kernel(factor_ref, w_ref, m_ref, v_ref, g_ref, *refs):
-    new_w_ref, new_m_ref, new_v_ref = refs[-3:]
-    g = g_ref[...].astype(F32) * factor_ref[0, 0]
-    m = 0.9 * m_ref[...] + 0.1 * g
-    v = 0.95 * v_ref[...] + 0.05 * g * g
-    w = w_ref[...].astype(F32)
-    new_w_ref[...] = (w - 0.02 * (m * lax.rsqrt(v + 1e-8) + 0.1 * w)).astype(BF16)
-    new_m_ref[...] = m
-    new_v_ref[...] = v
-
-
-def adamw(factor, w, m, v, g, layer, so_far):
-    _, r, c = w.shape
-    block = r // 7 if r % 112 == 0 else r // 8
-    part = pl.BlockSpec((None, block, c), lambda i: (layer, i, 0))
-    return pl.pallas_call(
-        adamw_kernel,
-        grid=(r // block,),
-        in_specs=[pl.BlockSpec(memory_space=pltpu.SMEM), part, part, part, pl.BlockSpec((block, c), lambda i: (i, 0))]
-        + [pl.BlockSpec(memory_space=pl.ANY)] * len(so_far),
-        out_specs=[part] * 3,
-        out_shape=[jax.ShapeDtypeStruct(w.shape, dtype) for dtype in (BF16, F32, F32)],
-        input_output_aliases={5 + i: i for i in range(len(so_far))},
+def adamw(total, count, items, layer):
+    blocks = [w.shape[1] // 7 if w.shape[1] % 112 == 0 else w.shape[1] // 8 for w, *_ in items]
+    steps = [w.shape[1] // block for (w, *_), block in zip(items, blocks, strict=True)]
+    starts = [sum(steps[:i]) for i in range(len(items))]
+    n_far = sum(len(so_far) for *_, so_far in items)
+
+    def kernel(total_ref, *refs):
+        factor = jnp.minimum(1.0, 0.5 * lax.rsqrt(total_ref[0:1, 0:1] / count + 1e-30))
+        ins, outs = refs[: 4 * len(items)], refs[4 * len(items) + n_far :]
+        for i in range(len(items)):
+            w_ref, m_ref, v_ref, g_ref = ins[4 * i : 4 * i + 4]
+            new_w_ref, new_m_ref, new_v_ref = outs[3 * i : 3 * i + 3]
+
+            def update(w_ref=w_ref, m_ref=m_ref, v_ref=v_ref, g_ref=g_ref, new_w_ref=new_w_ref, new_m_ref=new_m_ref, new_v_ref=new_v_ref):
+                g = g_ref[...].astype(F32) * factor
+                m = 0.9 * m_ref[...] + 0.1 * g
+                v = 0.95 * v_ref[...] + 0.05 * g * g
+                w = w_ref[...].astype(F32)
+                new_w_ref[...] = (w - 0.02 * (m * lax.rsqrt(v + 1e-8) + 0.1 * w)).astype(BF16)
+                new_m_ref[...] = m
+                new_v_ref[...] = v
+
+            if len(items) == 1:
+                update()
+            else:
+                step = pl.program_id(0)
+                pl.when((step >= starts[i]) & (step < starts[i] + steps[i]))(update)
+
+    in_specs, args, out_specs, out_shape = [pl.BlockSpec((8, 128), lambda i: (0, 0))], [total], [], []
+    for (w, m, v, g, _), block, n, start in zip(items, blocks, steps, starts, strict=True):
+        at = lambda i, n=n, start=start: jnp.clip(i - start, 0, n - 1)
+        part = pl.BlockSpec((None, block, w.shape[2]), lambda i, at=at: (layer, at(i), 0))
+        in_specs += [part, part, part, pl.BlockSpec((block, w.shape[2]), lambda i, at=at: (at(i), 0))]
+        args += [w, m, v, g]
+        out_specs += [part] * 3
+        out_shape += [jax.ShapeDtypeStruct(w.shape, dtype) for dtype in (BF16, F32, F32)]
+    far = [one for *_, so_far in items for one in so_far]
+    size = sum(w.size for w, *_ in items) // 2
+    new = pl.pallas_call(
+        kernel,
+        grid=(sum(steps),),
+        in_specs=in_specs + [pl.BlockSpec(memory_space=pl.ANY)] * n_far,
+        out_specs=out_specs,
+        out_shape=out_shape,
+        input_output_aliases={len(args) + i: i for i in range(n_far)},
         compiler_params=params(),
-        cost_estimate=cost(40 * r * c, 22 * r * c),
+        cost_estimate=cost(40 * size, 22 * size),
         name="adamw",
-    )(factor, w, m, v, g, *so_far)
+    )(*args, *far)
+    return [tuple(new[3 * i : 3 * i + 3]) for i in range(len(items))]
 
 
 def solution(mesh):
@@ -384,15 +441,16 @@
         keep(0, 2, *rest)
         up_term, *rest = products(at0, by0, (1,), (0, 2), gate_term, 0, 5)
         keep(0, 0, *rest)
-        keep(0, 1, *scattering(None, 1, (0, 0), [], (), [], [], up_term, 0, 6, "scatter", cost(2**30, 2**20)))
-        total = lax.psum(sum(jnp.sum(square) for square in squares), "dp")
+        shards[0][1], total = last_scatter(up_term, 0, squares, 6)
+        held, _ = lax.optimization_barrier((shards[0], total))
+
         count = sum(w.size for w in weights)
-        factor = jnp.minimum(1.0, 0.5 * lax.rsqrt(total / count + 1e-30)).reshape(1, 1)
-
-        new = [()] * 3
-        for layer in (1, 0):
-            for i in (2, 0, 1):
-                new[i] = adamw(factor, weights[i], ms[i], vs[i], gather(shards[layer][i]), layer, new[i])
+        order = (2, 0, 1)
+        items = [(weights[i], ms[i], vs[i], gather(shards[1][i]), ()) for i in order]
+        new = dict(zip(order, adamw(total, count, items, 1), strict=True))
+        for i in order:
+            (new[i],) = adamw(total, count, [(weights[i], ms[i], vs[i], gather(held[i]), new[i])], 0)
+        new = [new[i] for i in range(3)]
         return tuple(one[which] for which in range(3) for one in new)
 
     return jax.shard_map(

time: 498 us -> 470 us (0.944)
  blocking collectives: 22.8 us -> 0 us
  other arithmetic: 5.1 us -> 0 us
    pallas_call x6 -> x5, Pallas kernels: 108 us -> 157 us  [the longest x4 115 us: adamw(): pl.pallas_call(kernel, grid=(sum(steps),), in_specs=in_specs + [pl.BlockS...]
    pallas_call x6 -> x5, Pallas kernels: 226 us -> 180 us  [scattering(): pl.pallas_call(kernel, grid=(grid,), in_specs=list(in_specs) + [pl.BlockS...]
    psum x1 -> x0, blocking collectives: 22.8 us -> none  [step(): total = lax.psum(sum((jnp.sum(square) for square in squares)), 'dp')]
    reduce_sum x6 -> x0, other arithmetic: 5.1 us -> none  [step(): total = lax.psum(sum((jnp.sum(square) for square in squares)), 'dp')]
  transfers between devices with their start and end apart: 6 -> 6, of which waited for: 0 -> 0; matrix products, arithmetic and copies ran while one was open for 1% -> 0% of each run, Pallas kernels for 60% -> 50%
where the time goes in v3:
time: 470 us; the launch traced here: 465 us
  Pallas kernels  447 us (95%)
  between operations  14.7 us (3%)
    pallas_call x5, Pallas kernels, scattering(): pl.pallas_call(kernel, grid=(grid,), in_specs=list(in_specs) + [pl.BlockS...  180 us
    pallas_call x4, Pallas kernels, adamw(): pl.pallas_call(kernel, grid=(sum(steps),), in_specs=in_specs + [pl.BlockS...  115 us
    pallas_call x1, Pallas kernels, last_scatter(): pl.pallas_call(kernel, in_specs=[pl.BlockSpec(memory_space=pl.ANY)] + [vm...  42.7 us
    pallas_call x1, Pallas kernels, top(): pl.pallas_call(top_kernel, grid=(t // ROWS,), in_specs=[rows(d), rows(d),...  41.7 us
    pallas_call x1, Pallas kernels, forward(): pl.pallas_call(forward_kernel, grid=(t // ROWS,), in_specs=[rows(d), whol...  39.7 us
    pallas_call x2, Pallas kernels, product(): pl.pallas_call(product_kernel, grid=(m // CHUNK,), in_specs=[pl.BlockSpec...  28.7 us
  transfers between devices with their start and end apart: 6, of which 0 were waited for; matrix products, arithmetic and copies ran while one was open for 0% of the time, Pallas kernels for 50%

profile of v3, /device:TPU:0, one launch (start us, length us, event | category | flops | bytes accessed | tf_op | source)
XLA Modules:
  0.0 464.8 jit_solution(12477207764606656201)
XLA Ops:
  7.2 0.0 all-gather.13.cloned.1.call-start
  7.2 39.7 %forward.1 = (bf16[896,2048]{1,0:T(8,128)(2,1)}, f32[2048,2304]{1,0:T(8,128)}, f32[2048,2304]{1,0:T(8,128)}, bf16[2304,2048]{1,0:T(8,128)(2,1)}, bf16[2048,896]{1,0:T(8,128)(2,1)}) custom-call(bf16[2048,896]{1,0:T(8,128)(2,1)} %bitcast.9, bf16[2,896,2304]{2,1,0:T(8,128)(2,1)} %refs_0_.5, bf16[2,896,2304]{2,1,0:T(8,128)(2,1)} %refs_0_.6, ...), custom_call_target="tpu_custom_call" | custom-call | flops 25367150592 | bytes 56623104 | tf_op jit(solution)/shard_map/forward/pallas_call | solution.py:64
  46.9 41.7 %top.1 = (bf16[896,2048]{1,0:T(8,128)(2,1)}, bf16[2304,2048]{1,0:T(8,128)(2,1)}, bf16[2,2048,2304]{2,1,0:T(8,128)(2,1)}) custom-call(bf16[2048,896]{1,0:T(8,128)(2,1)} %get-tuple-element.56.h_ref.refs_0_, bf16[2048,896]{1,0:T(8,128)(2,1)} %bitcast.10, bf16[2,896,2304]{2,1,0:T(8,128)(2,1)} %refs_0_.5, bf16[2,896,2304]{2,1,0:T(8,128)(2,1)} %refs_0_.6, ...), custom_call_target="tpu_custom_call" | custom-call | flops 25367150592 | bytes 37748736 | tf_op jit(solution)/shard_map/top/pallas_call | solution.py:105
  88.6 14.3 %down1.1 = bf16[2304,896]{1,0:T(8,128)(2,1)} custom-call(bf16[2304,2048]{1,0:T(8,128)(2,1)} %get-tuple-element.59.a_ref, bf16[2048,896]{1,0:T(8,128)(2,1)} %bitcast.11), custom_call_target="tpu_custom_call" | custom-call | flops 8455716864 | bytes 17235968 | tf_op jit(solution)/shard_map/down1/pallas_call | solution.py:340
  102.9 33.3 %products.3 = (bf16[2,896,2304]{2,1,0:T(8,128)(2,1)}, bf16[288,896]{1,0:T(8,128)(2,1)}, f32[1,896]{1,0:T(1,128)}) custom-call(bf16[896,2048]{1,0:T(8,128)(2,1)} %get-tuple-element.58.refs_0_, bf16[2,2048,2304]{2,1,0:T(8,128)(2,1)} %get-tuple-element.57.refs_1_.refs_2_, bf16[4,2,288,896]{3,2,1,0:T(8,128)(2,1)} %bitcast.15), custom_call_target="tpu_custom_call" | custom-call | flops 16911433728 | bytes 34471936 | tf_op jit(solution)/shard_map/products/pallas_call | solution.py:239
  136.3 32.4 %input_back.1 = (bf16[2048,896]{1,0:T(8,128)(2,1)}, bf16[112,2304]{1,0:T(8,128)(2,1)}, f32[1,2304]{1,0:T(1,128)}) custom-call(bf16[2048,896]{1,0:T(8,128)(2,1)} %get-tuple-element.56.h_ref.refs_0_, bf16[2048,896]{1,0:T(8,128)(2,1)} %bitcast.12, bf16[2,2048,2304]{2,1,0:T(8,128)(2,1)} %get-tuple-element.57.refs_1_.refs_2_, bf16[2,896,2304]{2,1,0:T(8,128)(2,1)} %refs_0_.5, ...), custom_call_target="tpu_custom_call" | custom-call | flops 16911433728 | bytes 28311552 | tf_op jit(solution)/shard_map/input_back/pallas_call | solution.py:239
  168.7 36.2 %hidden_back.1 = (bf16[2,2048,2304]{2,1,0:T(8,128)(2,1)}, bf16[112,2304]{1,0:T(8,128)(2,1)}, f32[1,2304]{1,0:T(1,128)}) custom-call(bf16[2048,896]{1,0:T(8,128)(2,1)} %get-tuple-element.61.refs_0_.b_ref, f32[2048,2304]{1,0:T(8,128)} %get-tuple-element.62.refs_1_, f32[2048,2304]{1,0:T(8,128)} %get-tuple-element.63.refs_2_, bf16[2,2304,896]{2,1,0:T(8,128)(2,1)} %refs_0_.7, ...), custom_call_target="tpu_custom_call" | custom-call | flops 8455716864 | bytes 56623104 | tf_op jit(solution)/shard_map/hidden_back/pallas_call | solution.py:239
  204.8 0.0 all-gather.11.cloned.1.call-start
  204.9 0.7 all-gather.11.cloned.1.call-update
  205.6 0.2 all-gather.9.cloned.1.call-start
  205.9 0.5 all-gather.9.cloned.1.call-update
  206.3 0.0 all-gather.17.cloned.1.call-start
  206.4 14.3 %down0.1 = bf16[2304,896]{1,0:T(8,128)(2,1)} custom-call(bf16[2304,2048]{1,0:T(8,128)(2,1)} %get-tuple-element.65.a_ref, bf16[2048,896]{1,0:T(8,128)(2,1)} %get-tuple-element.61.refs_0_.b_ref), custom_call_target="tpu_custom_call" | custom-call | flops 8455716864 | bytes 17235968 | tf_op jit(solution)/shard_map/down0/pallas_call | solution.py:340
  220.7 39.0 %products.4 = (bf16[1,896,2304]{2,1,0:T(8,128)(2,1)}, bf16[288,896]{1,0:T(8,128)(2,1)}, f32[1,896]{1,0:T(1,128)}) custom-call(bf16[896,2048]{1,0:T(8,128)(2,1)} %get-tuple-element.55.refs_0_, bf16[2,2048,2304]{2,1,0:T(8,128)(2,1)} %get-tuple-element.64.refs_1_, bf16[4,2,288,896]{3,2,1,0:T(8,128)(2,1)} %bitcast.16), custom_call_target="tpu_custom_call" | custom-call | flops 8455716864 | bytes 17235968 | tf_op jit(solution)/shard_map/products/pallas_call | solution.py:239
  259.7 39.2 %products.5 = (bf16[1,896,2304]{2,1,0:T(8,128)(2,1)}, bf16[112,2304]{1,0:T(8,128)(2,1)}, f32[1,2304]{1,0:T(1,128)}) custom-call(bf16[896,2048]{1,0:T(8,128)(2,1)} %get-tuple-element.55.refs_0_, bf16[2,2048,2304]{2,1,0:T(8,128)(2,1)} %get-tuple-element.64.refs_1_, bf16[1,4,2,112,2304]{4,3,2,1,0:T(8,128)(2,1)} %bitcast.14), custom_call_target="tpu_custom_call" | custom-call | flops 8455716864 | bytes 17235968 | tf_op jit(solution)/shard_map/products/pallas_call | solution.py:239
  298.9 42.7 %last_scatter.1 = (bf16[112,2304]{1,0:T(8,128)(2,1)}, f32[8,128]{1,0:T(8,128)}) custom-call(bf16[1,4,2,112,2304]{4,3,2,1,0:T(8,128)(2,1)} %bitcast.13, f32[1,896]{1,0:T(1,128)} %get-tuple-element.68.refs_1_, f32[1,2304]{1,0:T(1,128)} %get-tuple-element.69.refs_2_, f32[1,2304]{1,0:T(1,128)} %get-tuple-element.70.refs_3_, f32[1,896]{1,0:T(1,128)} %get-tuple-element.71.refs_4_, ...), custom_call_target="tpu_custom_call" | custom-call | flops 17179869184 | bytes 1048576 | tf_op jit(solution)/shard_map/last_scatter/pallas_call | solution.py:280
  341.7 0.0 all-gather.15.cloned.1.call-start
  341.7 0.5 all-gather.15.cloned.1.call-update
  342.3 0.3 all-gather.7.cloned.1.call-start
  342.6 0.3 all-gather.7.cloned.1.call-update
  342.9 59.9 %adamw.4 = (bf16[2,2304,896]{2,1,0:T(8,128)(2,1)}, f32[2,2304,896]{2,1,0:T(8,128)}, f32[2,2304,896]{2,1,0:T(8,128)}, bf16[2,896,2304]{2,1,0:T(8,128)(2,1)}, f32[...) custom-call(f32[8,128]{1,0:T(8,128)} %get-tuple-element.73.total_ref, ...), custom_call_target="tpu_custom_call" | custom-call | flops 247726080 | bytes 136249344 | tf_op jit(solution)/shard_map/adamw/pallas_call | solution.py:404
  402.9 17.8 %adamw.7 = (bf16[2,2304,896]{2,1,0:T(8,128)(2,1)}, f32[2,2304,896]{2,1,0:T(8,128)}, f32[2,2304,896]{2,1,0:T(8,128)}) custom-call(f32[8,128]{1,0:T(8,128)} %get-tuple-element.73.total_ref, bf16[2,2304,896]{2,1,0:T(8,128)(2,1)} %refs_0_.7, f32[2,2304,896]{2,1,0:T(8,128)} %refs_1_.7, ...), custom_call_target="tpu_custom_call", output_to_operand_aliasing={{0}: (5, {}), {1}: (6, {}), {2}: (7, {})} | custom-call | flops 82575360 | bytes 45416448 | tf_op jit(solution)/shard_map/adamw/pallas_call | solution.py:404
  420.7 18.4 %adamw.6 = (bf16[2,896,2304]{2,1,0:T(8,128)(2,1)}, f32[2,896,2304]{2,1,0:T(8,128)}, f32[2,896,2304]{2,1,0:T(8,128)}) custom-call(f32[8,128]{1,0:T(8,128)} %get-tuple-element.73.total_ref, bf16[2,896,2304]{2,1,0:T(8,128)(2,1)} %refs_0_.6, f32[2,896,2304]{2,1,0:T(8,128)} %refs_1_.6, ...), custom_call_target="tpu_custom_call", output_to_operand_aliasing={{0}: (5, {}), {1}: (6, {}), {2}: (7, {})} | custom-call | flops 82575360 | bytes 45416448 | tf_op jit(solution)/shard_map/adamw/pallas_call | solution.py:404
  439.1 18.4 %adamw.5 = (bf16[2,896,2304]{2,1,0:T(8,128)(2,1)}, f32[2,896,2304]{2,1,0:T(8,128)}, f32[2,896,2304]{2,1,0:T(8,128)}) custom-call(f32[8,128]{1,0:T(8,128)} %get-tuple-element.73.total_ref, bf16[2,896,2304]{2,1,0:T(8,128)(2,1)} %refs_0_.5, f32[2,896,2304]{2,1,0:T(8,128)} %refs_1_.5, ...), custom_call_target="tpu_custom_call", output_to_operand_aliasing={{0}: (5, {}), {1}: (6, {}), {2}: (7, {})} | custom-call | flops 82575360 | bytes 45416448 | tf_op jit(solution)/shard_map/adamw/pallas_call | solution.py:404
  (8 shorter events, 0.1 us)
Async XLA Ops:
  7.2 335.7 %all-gather.13.cloned.1.call-start = ((), (), s32[]{:S(2)}) async-start(), calls=%async_computation.3 | async-start | bytes 4644864 | tf_op jit(solution)/shard_map/all_gather | solution.py:422
  204.8 138.1 %all-gather.11.cloned.1.call-start = ((), (), s32[]{:S(2)}) async-start(), calls=%async_computation.2 | async-start | bytes 4644864 | tf_op jit(solution)/shard_map/all_gather | solution.py:422
  205.6 137.3 %all-gather.9.cloned.1.call-start = ((), (), s32[]{:S(2)}) async-start(), calls=%async_computation.1 | async-start | bytes 4644864 | tf_op jit(solution)/shard_map/all_gather | solution.py:422
  206.3 196.5 %all-gather.17.cloned.1.call-start = ((), (), s32[]{:S(2)}) async-start(), calls=%async_computation.5 | async-start | bytes 4644864 | tf_op jit(solution)/shard_map/all_gather | solution.py:422
  341.7 79.0 %all-gather.15.cloned.1.call-start = ((), (), s32[]{:S(2)}) async-start(), calls=%async_computation.4 | async-start | bytes 4644864 | tf_op jit(solution)/shard_map/all_gather | solution.py:422
  342.3 96.8 %all-gather.7.cloned.1.call-start = ((), (), s32[]{:S(2)}) async-start(), calls=%async_computation | async-start | bytes 4644864 | tf_op jit(solution)/shard_map/all_gather | solution.py:422
Sparse Core Ops, SparseCore 0:
  205.0 33.4 all-gather.12
  240.3 39.9 all-gather.10
  282.1 40.7 all-gather.8
  341.8 30.4 all-gather.16
  374.0 30.4 all-gather.14
  406.2 30.4 all-gather.6

commit v4 on v3

--- a/solution.py
+++ b/solution.py
@@ -150,28 +150,37 @@
         return pltpu.make_async_copy(self.g.at[:, self.core], self.mine, self.local)
 
     def first(self):
-        return self.send(self.g.at[:, 1 - self.core], self.got1, 0, self.over_core)
+        r, c = half_shape(*self.got1.shape[1:])
+        whole_rows = r == self.got1.shape[1]
+        copies = []
+        for at in range(4):
+            for half in range(2):
+                rows, cols = (pl.ds(0, r), pl.ds(half * c, c)) if whole_rows else (pl.ds(half * r, r), pl.ds(0, c))
+                copies.append(self.send(self.g.at[at, 1 - self.core, rows, cols], self.got1.at[at, rows, cols], 4 + len(copies), self.over_core))
+        return copies
 
     def pair(self, src, dst, number, devices):
         return [self.send(src.at[half], dst.at[half], number + half, devices[half]) for half in range(2)]
 
     def second(self):
-        return self.pair(self.send2, self.got2, 1, (self.over_x, self.over_y))
+        return self.pair(self.send2, self.got2, 0, (self.over_x, self.over_y))
 
     def third(self):
-        return self.pair(self.send3, self.got3, 3, (self.over_y, self.over_x))
+        return self.pair(self.send3, self.got3, 2, (self.over_y, self.over_x))
 
     def begin(self):
         barrier = pltpu.get_barrier_semaphore()
         for device in (self.over_core, self.over_x, self.over_y):
             pl.semaphore_signal(barrier, inc=1, device_id=device, device_id_type=pl.DeviceIdType.MESH)
         pl.semaphore_wait(barrier, 3)
-        self.first().start()
+        for copy in self.first():
+            copy.start()
         self.fetch().start()
 
     def go_second(self):
         self.fetch().wait()
-        self.first().wait()
+        for copy in self.first():
+            copy.wait()
         for j in range(2):
             self.send2[0, j] = self.own(2 * (1 - self.x) + j, 0).astype(BF16)
             self.send2[1, j] = self.own(2 * j + (1 - self.y), 1).astype(BF16)
@@ -212,7 +221,7 @@
 def scatter_scratch(r, c):
     hr, hc = half_shape(r, c)
     blocks = ((4, r, c), (4, r, c), (2, 2, hr, hc), (2, 2, hr, hc), (2, hr, hc), (2, hr, hc))
-    return [pltpu.VMEM(block, BF16) for block in blocks] + [pltpu.SemaphoreType.DMA, pltpu.SemaphoreType.DMA((5,)), pltpu.SemaphoreType.DMA((5,))]
+    return [pltpu.VMEM(block, BF16) for block in blocks] + [pltpu.SemaphoreType.DMA, pltpu.SemaphoreType.DMA((12,)), pltpu.SemaphoreType.DMA((12,))]
 
 
 def by_device(term):
@@ -432,13 +441,20 @@
         down1 = product(actt1, dy, "down1")
         pair1, *rest = products(at1, by1, (0, 1), (0, 3), down1, None, 1)
         keep(1, 2, *rest)
+        gathered = [None] * 3
+        gathered[2] = gather(shards[1][2])
         bh1, *rest = input_back(h1, dy, by1, *weights[:2], 1, pair1, 0, 2)
         keep(1, 0, *rest)
-        down0 = product(actt0, bh1, "down0")
+        bh1, gathered[2] = lax.optimization_barrier((bh1, gathered[2]))
+        gathered[0] = gather(shards[1][0])
         by0, *rest = hidden_back(bh1, gate0, up0, weights[2], 0, pair1, 1, 3)
         keep(1, 1, *rest)
+        by0, gathered[0] = lax.optimization_barrier((by0, gathered[0]))
+        gathered[1] = gather(shards[1][1])
+        down0 = product(actt0, bh1, "down0")
         gate_term, *rest = products(at0, by0, (0,), (0, 2), down0, None, 4)
         keep(0, 2, *rest)
+        gate_term, gathered[1] = lax.optimization_barrier((gate_term, gathered[1]))
         up_term, *rest = products(at0, by0, (1,), (0, 2), gate_term, 0, 5)
         keep(0, 0, *rest)
         shards[0][1], total = last_scatter(up_term, 0, squares, 6)
@@ -446,7 +462,7 @@
 
         count = sum(w.size for w in weights)
         order = (2, 0, 1)
-        items = [(weights[i], ms[i], vs[i], gather(shards[1][i]), ()) for i in order]
+        items = [(weights[i], ms[i], vs[i], gathered[i], ()) for i in order]
         new = dict(zip(order, adamw(total, count, items, 1), strict=True))
         for i in order:
             (new[i],) = adamw(total, count, [(weights[i], ms[i], vs[i], gather(held[i]), new[i])], 0)

time: 470 us -> 468 us (level)
    pallas_call x1, Pallas kernels: 42.7 us -> 34.8 us  [last_scatter(): pl.pallas_call(kernel, in_specs=[pl.BlockSpec(memory_space=pl.ANY)] + [vm...]
    pallas_call x5, Pallas kernels: 180 us -> 187 us  [scattering(): pl.pallas_call(kernel, grid=(grid,), in_specs=list(in_specs) + [pl.BlockS...]
  transfers between devices with their start and end apart: 6 -> 6, of which waited for: 0 -> 0; matrix products, arithmetic and copies ran while one was open for 0% -> 0% of each run, Pallas kernels for 50% -> 51%
where the time goes in v4:
time: 468 us; the launch traced here: 463 us
  Pallas kernels  447 us (96%)
  between operations  14.7 us (3%)
    pallas_call x5, Pallas kernels, scattering(): pl.pallas_call(kernel, grid=(grid,), in_specs=list(in_specs) + [pl.BlockS...  187 us
    pallas_call x4, Pallas kernels, adamw(): pl.pallas_call(kernel, grid=(sum(steps),), in_specs=in_specs + [pl.BlockS...  115 us
    pallas_call x1, Pallas kernels, top(): pl.pallas_call(top_kernel, grid=(t // ROWS,), in_specs=[rows(d), rows(d),...  41.7 us
    pallas_call x1, Pallas kernels, forward(): pl.pallas_call(forward_kernel, grid=(t // ROWS,), in_specs=[rows(d), whol...  39.7 us
    pallas_call x1, Pallas kernels, last_scatter(): pl.pallas_call(kernel, in_specs=[pl.BlockSpec(memory_space=pl.ANY)] + [vm...  34.8 us
    pallas_call x2, Pallas kernels, product(): pl.pallas_call(product_kernel, grid=(m // CHUNK,), in_specs=[pl.BlockSpec...  28.9 us
  transfers between devices with their start and end apart: 6, of which 0 were waited for; matrix products, arithmetic and copies ran while one was open for 0% of the time, Pallas kernels for 51%

profile of v4, /device:TPU:0, one launch (start us, length us, event | category | flops | bytes accessed | tf_op | source)
XLA Modules:
  0.0 463.1 jit_solution(14659239280889733666)
XLA Ops:
  7.2 0.0 all-gather.7.cloned.1.call-start
  7.2 39.7 %forward.1 = (bf16[896,2048]{1,0:T(8,128)(2,1)}, f32[2048,2304]{1,0:T(8,128)}, f32[2048,2304]{1,0:T(8,128)}, bf16[2304,2048]{1,0:T(8,128)(2,1)}, bf16[2048,896]{1,0:T(8,128)(2,1)}) custom-call(bf16[2048,896]{1,0:T(8,128)(2,1)} %bitcast.9, bf16[2,896,2304]{2,1,0:T(8,128)(2,1)} %refs_0_.5, bf16[2,896,2304]{2,1,0:T(8,128)(2,1)} %refs_0_.6, ...), custom_call_target="tpu_custom_call" | custom-call | flops 25367150592 | bytes 56623104 | tf_op jit(solution)/shard_map/forward/pallas_call | solution.py:64
  46.9 41.7 %top.1 = (bf16[896,2048]{1,0:T(8,128)(2,1)}, bf16[2304,2048]{1,0:T(8,128)(2,1)}, bf16[2,2048,2304]{2,1,0:T(8,128)(2,1)}) custom-call(bf16[2048,896]{1,0:T(8,128)(2,1)} %get-tuple-element.62.h_ref.refs_0_, bf16[2048,896]{1,0:T(8,128)(2,1)} %bitcast.10, bf16[2,896,2304]{2,1,0:T(8,128)(2,1)} %refs_0_.5, bf16[2,896,2304]{2,1,0:T(8,128)(2,1)} %refs_0_.6, ...), custom_call_target="tpu_custom_call" | custom-call | flops 25367150592 | bytes 37748736 | tf_op jit(solution)/shard_map/top/pallas_call | solution.py:105
  88.6 14.3 %down1.1 = bf16[2304,896]{1,0:T(8,128)(2,1)} custom-call(bf16[2304,2048]{1,0:T(8,128)(2,1)} %get-tuple-element.65.a_ref, bf16[2048,896]{1,0:T(8,128)(2,1)} %bitcast.11), custom_call_target="tpu_custom_call" | custom-call | flops 8455716864 | bytes 17235968 | tf_op jit(solution)/shard_map/down1/pallas_call | solution.py:349
  102.9 33.5 %products.3 = (bf16[2,896,2304]{2,1,0:T(8,128)(2,1)}, bf16[288,896]{1,0:T(8,128)(2,1)}, f32[1,896]{1,0:T(1,128)}) custom-call(bf16[896,2048]{1,0:T(8,128)(2,1)} %get-tuple-element.64.refs_0_, bf16[2,2048,2304]{2,1,0:T(8,128)(2,1)} %get-tuple-element.63.refs_1_.refs_2_, bf16[4,2,288,896]{3,2,1,0:T(8,128)(2,1)} %bitcast.15), custom_call_target="tpu_custom_call" | custom-call | flops 16911433728 | bytes 34471936 | tf_op jit(solution)/shard_map/products/pallas_call | solution.py:248
  136.4 0.0 all-gather.9.cloned.1.call-start
  136.5 43.3 %input_back.1 = (bf16[2048,896]{1,0:T(8,128)(2,1)}, bf16[112,2304]{1,0:T(8,128)(2,1)}, f32[1,2304]{1,0:T(1,128)}) custom-call(bf16[2048,896]{1,0:T(8,128)(2,1)} %get-tuple-element.62.h_ref.refs_0_, bf16[2048,896]{1,0:T(8,128)(2,1)} %bitcast.12, bf16[2,2048,2304]{2,1,0:T(8,128)(2,1)} %get-tuple-element.63.refs_1_.refs_2_, bf16[2,896,2304]{2,1,0:T(8,128)(2,1)} %refs_0_.5, ...), custom_call_target="tpu_custom_call" | custom-call | flops 16911433728 | bytes 28311552 | tf_op jit(solution)/shard_map/input_back/pallas_call | solution.py:248
  179.8 0.0 all-gather.11.cloned.1.call-start
  179.8 44.4 %hidden_back.1 = (bf16[2,2048,2304]{2,1,0:T(8,128)(2,1)}, bf16[112,2304]{1,0:T(8,128)(2,1)}, f32[1,2304]{1,0:T(1,128)}) custom-call(bf16[2048,896]{1,0:T(8,128)(2,1)} %get-tuple-element.69.refs_0_.b_ref, f32[2048,2304]{1,0:T(8,128)} %get-tuple-element.70.refs_1_, f32[2048,2304]{1,0:T(8,128)} %get-tuple-element.71.refs_2_, bf16[2,2304,896]{2,1,0:T(8,128)(2,1)} %refs_0_.7, ...), custom_call_target="tpu_custom_call" | custom-call | flops 8455716864 | bytes 56623104 | tf_op jit(solution)/shard_map/hidden_back/pallas_call | solution.py:248
  224.3 0.0 all-gather.17.cloned.1.call-start
  224.4 14.6 %down0.1 = bf16[2304,896]{1,0:T(8,128)(2,1)} custom-call(bf16[2304,2048]{1,0:T(8,128)(2,1)} %get-tuple-element.75.a_ref, bf16[2048,896]{1,0:T(8,128)(2,1)} %get-tuple-element.69.refs_0_.b_ref), custom_call_target="tpu_custom_call" | custom-call | flops 8455716864 | bytes 17235968 | tf_op jit(solution)/shard_map/down0/pallas_call | solution.py:349
  238.9 35.7 %products.4 = (bf16[1,896,2304]{2,1,0:T(8,128)(2,1)}, bf16[288,896]{1,0:T(8,128)(2,1)}, f32[1,896]{1,0:T(1,128)}) custom-call(bf16[896,2048]{1,0:T(8,128)(2,1)} %get-tuple-element.61.refs_0_, bf16[2,2048,2304]{2,1,0:T(8,128)(2,1)} %get-tuple-element.74.refs_1_, bf16[4,2,288,896]{3,2,1,0:T(8,128)(2,1)} %bitcast.16), custom_call_target="tpu_custom_call" | custom-call | flops 8455716864 | bytes 17235968 | tf_op jit(solution)/shard_map/products/pallas_call | solution.py:248
  274.7 0.0 all-gather.11.cloned.1.call-done.refs_11_
  274.7 30.2 %products.5 = (bf16[1,896,2304]{2,1,0:T(8,128)(2,1)}, bf16[112,2304]{1,0:T(8,128)(2,1)}, f32[1,2304]{1,0:T(1,128)}) custom-call(bf16[896,2048]{1,0:T(8,128)(2,1)} %get-tuple-element.61.refs_0_, bf16[2,2048,2304]{2,1,0:T(8,128)(2,1)} %get-tuple-element.74.refs_1_, bf16[1,4,2,112,2304]{4,3,2,1,0:T(8,128)(2,1)} %bitcast.14), custom_call_target="tpu_custom_call" | custom-call | flops 8455716864 | bytes 17235968 | tf_op jit(solution)/shard_map/products/pallas_call | solution.py:248
  304.9 34.8 %last_scatter.1 = (bf16[112,2304]{1,0:T(8,128)(2,1)}, f32[8,128]{1,0:T(8,128)}) custom-call(bf16[1,4,2,112,2304]{4,3,2,1,0:T(8,128)(2,1)} %bitcast.13, f32[1,896]{1,0:T(1,128)} %get-tuple-element.80.refs_1_, f32[1,2304]{1,0:T(1,128)} %get-tuple-element.81.refs_2_, f32[1,2304]{1,0:T(1,128)} %get-tuple-element.82.refs_3_, f32[1,896]{1,0:T(1,128)} %get-tuple-element.83.refs_4_, ...), custom_call_target="tpu_custom_call" | custom-call | flops 17179869184 | bytes 1048576 | tf_op jit(solution)/shard_map/last_scatter/pallas_call | solution.py:289
  339.8 0.0 all-gather.15.cloned.1.call-start
  339.8 0.5 all-gather.15.cloned.1.call-update
  340.4 0.0 all-gather.13.cloned.1.call-start
  340.4 0.5 all-gather.13.cloned.1.call-update
  340.9 60.2 %adamw.4 = (bf16[2,2304,896]{2,1,0:T(8,128)(2,1)}, f32[2,2304,896]{2,1,0:T(8,128)}, f32[2,2304,896]{2,1,0:T(8,128)}, bf16[2,896,2304]{2,1,0:T(8,128)(2,1)}, f32[...) custom-call(f32[8,128]{1,0:T(8,128)} %get-tuple-element.85.total_ref, ...), custom_call_target="tpu_custom_call" | custom-call | flops 247726080 | bytes 136249344 | tf_op jit(solution)/shard_map/adamw/pallas_call | solution.py:413
  401.1 0.0 all-gather.17.cloned.1.call-done.refs_3_
  401.1 17.8 %adamw.7 = (bf16[2,2304,896]{2,1,0:T(8,128)(2,1)}, f32[2,2304,896]{2,1,0:T(8,128)}, f32[2,2304,896]{2,1,0:T(8,128)}) custom-call(f32[8,128]{1,0:T(8,128)} %get-tuple-element.85.total_ref, bf16[2,2304,896]{2,1,0:T(8,128)(2,1)} %refs_0_.7, f32[2,2304,896]{2,1,0:T(8,128)} %refs_1_.7, ...), custom_call_target="tpu_custom_call", output_to_operand_aliasing={{0}: (5, {}), {1}: (6, {}), {2}: (7, {})} | custom-call | flops 82575360 | bytes 45416448 | tf_op jit(solution)/shard_map/adamw/pallas_call | solution.py:413
  419.0 18.4 %adamw.6 = (bf16[2,896,2304]{2,1,0:T(8,128)(2,1)}, f32[2,896,2304]{2,1,0:T(8,128)}, f32[2,896,2304]{2,1,0:T(8,128)}) custom-call(f32[8,128]{1,0:T(8,128)} %get-tuple-element.85.total_ref, bf16[2,896,2304]{2,1,0:T(8,128)(2,1)} %refs_0_.6, f32[2,896,2304]{2,1,0:T(8,128)} %refs_1_.6, ...), custom_call_target="tpu_custom_call", output_to_operand_aliasing={{0}: (5, {}), {1}: (6, {}), {2}: (7, {})} | custom-call | flops 82575360 | bytes 45416448 | tf_op jit(solution)/shard_map/adamw/pallas_call | solution.py:413
  437.4 18.4 %adamw.5 = (bf16[2,896,2304]{2,1,0:T(8,128)(2,1)}, f32[2,896,2304]{2,1,0:T(8,128)}, f32[2,896,2304]{2,1,0:T(8,128)}) custom-call(f32[8,128]{1,0:T(8,128)} %get-tuple-element.85.total_ref, bf16[2,896,2304]{2,1,0:T(8,128)(2,1)} %refs_0_.5, f32[2,896,2304]{2,1,0:T(8,128)} %refs_1_.5, ...), custom_call_target="tpu_custom_call", output_to_operand_aliasing={{0}: (5, {}), {1}: (6, {}), {2}: (7, {})} | custom-call | flops 82575360 | bytes 45416448 | tf_op jit(solution)/shard_map/adamw/pallas_call | solution.py:413
  (8 shorter events, 0.1 us)
Async XLA Ops:
  7.2 172.7 %all-gather.7.cloned.1.call-start = ((), (), s32[]{:S(2)}) async-start(), calls=%async_computation | async-start | bytes 4644864 | tf_op jit(solution)/shard_map/all_gather | solution.py:431
  136.4 87.9 %all-gather.9.cloned.1.call-start = ((), (), s32[]{:S(2)}) async-start(), calls=%async_computation.1 | async-start | bytes 4644864 | tf_op jit(solution)/shard_map/all_gather | solution.py:431
  179.8 94.9 %all-gather.11.cloned.1.call-start = ((), (), s32[]{:S(2)}) async-start(), calls=%async_computation.2 | async-start | bytes 4644864 | tf_op jit(solution)/shard_map/all_gather | solution.py:431
  224.3 176.9 %all-gather.17.cloned.1.call-start = ((), (), s32[]{:S(2)}) async-start(), calls=%async_computation.5 | async-start | bytes 4644864 | tf_op jit(solution)/shard_map/all_gather | solution.py:431
  339.8 79.2 %all-gather.15.cloned.1.call-start = ((), (), s32[]{:S(2)}) async-start(), calls=%async_computation.4 | async-start | bytes 4644864 | tf_op jit(solution)/shard_map/all_gather | solution.py:431
  340.4 97.0 %all-gather.13.cloned.1.call-start = ((), (), s32[]{:S(2)}) async-start(), calls=%async_computation.3 | async-start | bytes 4644864 | tf_op jit(solution)/shard_map/all_gather | solution.py:431
Sparse Core Ops, SparseCore 0:
  136.5 40.8 all-gather.6
  179.9 39.6 all-gather.8
  224.4 34.8 all-gather.10
  339.9 30.4 all-gather.16
  372.1 30.4 all-gather.14
  404.3 30.4 all-gather.12

commit v5 on v4

--- a/solution.py
+++ b/solution.py
@@ -119,9 +119,9 @@
 
 
 class Scatter:
-    def __init__(self, g, out, squares, mine, got1, send2, got2, send3, got3, local, sent, received):
-        self.g, self.out, self.squares = g, out, squares
-        self.mine, self.got1, self.send2, self.got2, self.send3, self.got3 = mine, got1, send2, got2, send3, got3
+    def __init__(self, g, send3, kept, mine, got1, send2, got2, local, sent, received):
+        self.g, self.send3, self.kept = g, send3, kept
+        self.mine, self.got1, self.send2, self.got2 = mine, got1, send2, got2
         self.local, self.sent, self.received = local, sent, received
         me = lax.axis_index("dp")
         self.x, self.y, self.core = me // 4, lax.rem(me // 2, 2), lax.rem(me, 2)
@@ -165,14 +165,13 @@
     def second(self):
         return self.pair(self.send2, self.got2, 0, (self.over_x, self.over_y))
 
-    def third(self):
-        return self.pair(self.send3, self.got3, 2, (self.over_y, self.over_x))
-
-    def begin(self):
+    def begin(self, before=None):
         barrier = pltpu.get_barrier_semaphore()
         for device in (self.over_core, self.over_x, self.over_y):
             pl.semaphore_signal(barrier, inc=1, device_id=device, device_id_type=pl.DeviceIdType.MESH)
         pl.semaphore_wait(barrier, 3)
+        if before is not None:
+            before.start()
         for copy in self.first():
             copy.start()
         self.fetch().start()
@@ -187,30 +186,44 @@
         for copy in self.second():
             copy.start()
 
-    def go_third(self):
+    def end_second(self):
         for copy in self.second():
             copy.wait()
         x, y = self.x, self.y
         self.send3[0] = (self.own(2 * x + (1 - y), 0) + self.got2[0, 1 - y].astype(F32)).astype(BF16)
         self.send3[1] = (self.own(2 * (1 - x) + y, 1) + self.got2[1, 1 - x].astype(F32)).astype(BF16)
-        for copy in self.third():
+        self.kept[0] = self.own(2 * x + y, 0) + self.got2[0, y].astype(F32)
+        self.kept[1] = self.own(2 * x + y, 1) + self.got2[1, x].astype(F32)
+
+
+class Finish:
+    def __init__(self, scatter, send3, kept, out, squares, got3, sent, received):
+        self.copies = [
+            pltpu.make_async_remote_copy(
+                src_ref=send3.at[half], dst_ref=got3.at[half], send_sem=sent.at[half], recv_sem=received.at[half],
+                device_id=device, device_id_type=pl.DeviceIdType.MESH,
+            )
+            for half, device in ((0, scatter.over_y), (1, scatter.over_x))
+        ]
+        self.kept, self.out, self.squares, self.got3 = kept, out, squares, got3
+
+    def start(self):
+        for copy in self.copies:
             copy.start()
 
     def end(self):
-        for copy in self.third():
+        for copy in self.copies:
             copy.wait()
-        x, y = self.x, self.y
         r, c = self.out.shape
         hr, hc = half_shape(r, c)
-        for half, kept in ((0, self.got2[0, y]), (1, self.got2[1, x])):
-            total = (self.own(2 * x + y, half) + kept.astype(F32) + self.got3[half].astype(F32)).astype(BF16)
-            square = jnp.square(total.astype(F32))
+        for half in range(2):
+            total = (self.kept[half] + self.got3[half].astype(F32)).astype(BF16)
+            square = jnp.sum(jnp.square(total.astype(F32)), 0, keepdims=True)
             if hr == r:
                 self.out[:, half * hc : (half + 1) * hc] = total
-                self.squares[:, half * hc : (half + 1) * hc] = jnp.sum(square, 0, keepdims=True)
+                self.squares[:, half * hc : (half + 1) * hc] = square
             else:
                 self.out[half * hr : (half + 1) * hr, :] = total
-                square = jnp.sum(square, 0, keepdims=True)
                 self.squares[...] = square if half == 0 else self.squares[...] + square
 
 
@@ -220,8 +233,12 @@
 
 def scatter_scratch(r, c):
     hr, hc = half_shape(r, c)
-    blocks = ((4, r, c), (4, r, c), (2, 2, hr, hc), (2, 2, hr, hc), (2, hr, hc), (2, hr, hc))
+    blocks = ((4, r, c), (4, r, c), (2, 2, hr, hc), (2, 2, hr, hc))
     return [pltpu.VMEM(block, BF16) for block in blocks] + [pltpu.SemaphoreType.DMA, pltpu.SemaphoreType.DMA((12,)), pltpu.SemaphoreType.DMA((12,))]
+
+
+def finish_scratch(r, c):
+    return [pltpu.VMEM((2,) + half_shape(r, c), BF16), pltpu.SemaphoreType.DMA((2,)), pltpu.SemaphoreType.DMA((2,))]
 
 
 def by_device(term):
@@ -229,50 +246,83 @@
     return term.reshape(term.shape[:-2] + (4, 2, r // 8, c))
 
 
-def scattering(compute, grid, steps, in_specs, args, out_specs, out_shape, term, which, collective_id, name, cost_estimate):
+def left_of(r, c):
+    return [jax.ShapeDtypeStruct((2,) + half_shape(r, c), dtype) for dtype in (BF16, F32)]
+
+
+def shard_of(left):
+    _, hr, hc = left[0].shape
+    return (hr, 2 * hc) if hc % 128 == 0 and hc * 2 % 256 == 0 and hr == 112 else (2 * hr, hc)
+
+
+def scattering(compute, grid, in_specs, args, out_specs, out_shape, term, which, left, collective_id, name, cost_estimate):
     term = by_device(term)
     r, c = term.shape[-2:]
     n_in, n_out = len(args), len(out_shape)
+    fixed = lambda shape: pl.BlockSpec(shape, lambda i: (0,) * len(shape))
+    leaves = left_of(r, c)
+    in_specs, out_specs, out_shape = list(in_specs), list(out_specs), list(out_shape)
+    in_specs += [pl.BlockSpec(memory_space=pl.ANY)]
+    out_specs += [fixed(one.shape) for one in leaves]
+    out_shape += leaves
+    scratch_shapes = scatter_scratch(r, c)
+    if left:
+        before = shard_of(left)
+        in_specs += [pl.BlockSpec(memory_space=pl.ANY), fixed(left[1].shape)]
+        out_specs += [fixed(before), fixed((1, before[1]))]
+        out_shape += [jax.ShapeDtypeStruct(before, BF16), jax.ShapeDtypeStruct((1, before[1]), F32)]
+        scratch_shapes = scratch_shapes + finish_scratch(*before)
 
     def kernel(*refs):
-        ins, g, outs, (out, squares), scratch = refs[:n_in], refs[n_in], refs[n_in + 1 :][:n_out], refs[n_in + 1 + n_out :][:2], refs[n_in + 3 + n_out :]
-        scatter = Scatter(g if which is None else g.at[which], out, squares, *scratch)
+        refs = list(refs)
+        take = lambda n: [refs.pop(0) for _ in range(n)]
+        ins, (g,), previous, outs, leaves, done, scratch = (take(n) for n in (n_in, 1, 2 * bool(left), n_out, 2, 2 * bool(left), 7))
+        scatter = Scatter(g if which is None else g.at[which], *leaves, *scratch)
+        before = Finish(scatter, *previous, *done, *refs) if left else None
         step = pl.program_id(0)
-        pl.when(step == 0)(scatter.begin)
+        pl.when(step == 0)(lambda: scatter.begin(before))
         compute(*ins, *outs)
-        pl.when(step == steps[0])(scatter.go_second)
-        pl.when(step == steps[1])(scatter.go_third)
-        pl.when(step == grid - 1)(scatter.end)
-
-    fixed = lambda *shape: pl.BlockSpec(shape, lambda i: (0,) * len(shape))
-    return pl.pallas_call(
+        pl.when(step == 0)(scatter.go_second)
+        if left:
+            pl.when(step == 1)(before.end)
+        pl.when(step == grid - 1)(scatter.end_second)
+
+    results = pl.pallas_call(
         kernel,
         grid=(grid,),
-        in_specs=list(in_specs) + [pl.BlockSpec(memory_space=pl.ANY)],
-        out_specs=list(out_specs) + [fixed(r, c), fixed(1, c)],
-        out_shape=list(out_shape) + [jax.ShapeDtypeStruct((r, c), BF16), jax.ShapeDtypeStruct((1, c), F32)],
-        scratch_shapes=scatter_scratch(r, c),
+        in_specs=in_specs,
+        out_specs=out_specs,
+        out_shape=out_shape,
+        scratch_shapes=scratch_shapes,
         compiler_params=pltpu.CompilerParams(
             dimension_semantics=("arbitrary",), vmem_limit_bytes=VMEM_LIMIT, collective_id=collective_id, has_side_effects=True
         ),
         cost_estimate=cost_estimate,
         name=name,
-    )(*args, term)
-
-
-def last_scatter(term, which, squares, collective_id):
+    )(*args, term, *left)
+    return *results[:n_out], results[n_out : n_out + 2], *results[n_out + 2 :]
+
+
+def last_scatter(term, which, left, squares, collective_id):
     term = by_device(term)
     r, c = term.shape[-2:]
+    before_shape = shard_of(left)
 
     def kernel(*refs):
-        g, others, (out, total_ref), (own, mine, theirs, *scratch) = refs[0], refs[1 : 1 + len(squares)], refs[1 + len(squares) :][:2], refs[3 + len(squares) :]
-        *scratch, sent, received = scratch
-        scatter = Scatter(g.at[which], out, own, *scratch)
-        scatter.begin()
-        rest = sum(jnp.sum(other[...], keepdims=True) for other in others)
+        refs = list(refs)
+        take = lambda n: [refs.pop(0) for _ in range(n)]
+        (g,), previous, others, (out, old, total_ref), scratch, finish1, finish2 = (take(n) for n in (1, 2, len(squares), 3, 7, 3, 3))
+        send3, kept, own, own_before, mine, theirs, sent, received = refs
+        scatter = Scatter(g.at[which], send3, kept, *scratch)
+        before = Finish(scatter, *previous, old, own_before, *finish1)
+        last = Finish(scatter, send3, kept, out, own, *finish2)
+        scatter.begin(before)
         scatter.go_second()
-        scatter.go_third()
-        scatter.end()
+        before.end()
+        rest = sum(jnp.sum(other[...], keepdims=True) for other in (*others, own_before))
+        scatter.end_second()
+        last.start()
+        last.end()
         total = jnp.broadcast_to(rest + jnp.sum(own[...], keepdims=True), (8, 128))
         for i, device in enumerate((scatter.over_core, scatter.over_x, scatter.over_y)):
             mine[i] = total
@@ -286,18 +336,22 @@
         total_ref[...] = total
 
     vmem = pl.BlockSpec(memory_space=pltpu.VMEM)
+    hbm = pl.BlockSpec(memory_space=pl.ANY)
     return pl.pallas_call(
         kernel,
-        in_specs=[pl.BlockSpec(memory_space=pl.ANY)] + [vmem] * len(squares),
-        out_specs=[vmem, vmem],
-        out_shape=[jax.ShapeDtypeStruct((r, c), BF16), jax.ShapeDtypeStruct((8, 128), F32)],
-        scratch_shapes=[pltpu.VMEM((1, c), F32), pltpu.VMEM((3, 8, 128), F32), pltpu.VMEM((3, 8, 128), F32)]
-        + scatter_scratch(r, c)
+        in_specs=[hbm, hbm, vmem] + [vmem] * len(squares),
+        out_specs=[vmem] * 3,
+        out_shape=[jax.ShapeDtypeStruct((r, c), BF16), jax.ShapeDtypeStruct(before_shape, BF16), jax.ShapeDtypeStruct((8, 128), F32)],
+        scratch_shapes=scatter_scratch(r, c)
+        + finish_scratch(*before_shape)
+        + finish_scratch(r, c)
+        + [pltpu.VMEM(one.shape, one.dtype) for one in left_of(r, c)]
+        + [pltpu.VMEM((1, c), F32), pltpu.VMEM((1, before_shape[1]), F32), pltpu.VMEM((3, 8, 128), F32), pltpu.VMEM((3, 8, 128), F32)]
         + [pltpu.SemaphoreType.DMA((3,)), pltpu.SemaphoreType.DMA((3,))],
         compiler_params=pltpu.CompilerParams(vmem_limit_bytes=VMEM_LIMIT, collective_id=collective_id, has_side_effects=True),
         cost_estimate=cost(2**34, 2**20),
         name="last_scatter",
-    )(term, *squares)
+    )(term, *left, *squares)
 
 
 def input_back_kernel(h_ref, dy_ref, by_ref, wg_ref, wu_ref, bh_ref):
@@ -308,16 +362,16 @@
     bh_ref[...] = (dy_ref[...].astype(F32) + by_h).astype(BF16)
 
 
-def input_back(h, dy, by, wg, wu, layer, term, which, collective_id):
+def input_back(h, dy, by, wg, wu, layer, term, which, left, collective_id):
     t, d = h.shape
     ff = wg.shape[2]
     rows = lambda n: pl.BlockSpec((ROWS, n), lambda i: (i, 0))
     return scattering(
-        input_back_kernel, t // ROWS, (0, 2),
+        input_back_kernel, t // ROWS,
         [rows(d), rows(d), pl.BlockSpec((2, ROWS, ff), lambda i: (0, i, 0)), whole(wg, layer), whole(wu, layer)],
         (h, dy, by, wg, wu),
         [rows(d)], [jax.ShapeDtypeStruct((t, d), BF16)],
-        term, which, collective_id, "input_back", cost(4 * t * d * ff, 6 * t * ff),
+        term, which, left, collective_id, "input_back", cost(4 * t * d * ff, 6 * t * ff),
     )
 
 
@@ -328,15 +382,15 @@
         _, out_ref[0, :, cols], out_ref[1, :, cols] = gate_up_back(gate_ref[:, cols], up_ref[:, cols], by_act)
 
 
-def hidden_back(by, gate, up, wd, layer, term, which, collective_id):
+def hidden_back(by, gate, up, wd, layer, term, which, left, collective_id):
     t, d = by.shape
     ff = gate.shape[1]
     rows = lambda n: pl.BlockSpec((ROWS, n), lambda i: (i, 0))
     return scattering(
-        hidden_back_kernel, t // ROWS, (0, 2),
+        hidden_back_kernel, t // ROWS,
         [rows(d), rows(ff), rows(ff), whole(wd, layer)], (by, gate, up, wd),
         [pl.BlockSpec((2, ROWS, ff), lambda i: (0, i, 0))], [jax.ShapeDtypeStruct((2, t, ff), BF16)],
-        term, which, collective_id, "hidden_back", cost(2 * t * d * ff, 12 * t * ff),
+        term, which, left, collective_id, "hidden_back", cost(2 * t * d * ff, 12 * t * ff),
     )
 
 
@@ -358,70 +412,94 @@
     )(a, b)
 
 
-def products(a, b, those, steps, term, which, collective_id):
+def products(a, b, those, term, which, left, collective_id):
     (m, k), n = a.shape, b.shape[2]
     chunks = n // CHUNK
     grid = len(those) * chunks
     first = those[0]
     return scattering(
-        product_kernel, grid, steps,
+        product_kernel, grid,
         [pl.BlockSpec((m, k), lambda i: (0, 0), pipeline_mode=pl.Buffered(1)), pl.BlockSpec((None, k, CHUNK), lambda i: (first + i // chunks, 0, lax.rem(i, chunks)))],
         (a, b),
         [pl.BlockSpec((None, m, CHUNK), lambda i: (i // chunks, 0, lax.rem(i, chunks)))], [jax.ShapeDtypeStruct((len(those), m, n), BF16)],
-        term, which, collective_id, "products", cost(2 * m * n * k * len(those), 2 * (m * k + k * n + m * n) * len(those)),
+        term, which, left, collective_id, "products", cost(2 * m * n * k * len(those), 2 * (m * k + k * n + m * n) * len(those)),
     )
 
 
-def adamw(total, count, items, layer):
-    blocks = [w.shape[1] // 7 if w.shape[1] % 112 == 0 else w.shape[1] // 8 for w, *_ in items]
-    steps = [w.shape[1] // block for (w, *_), block in zip(items, blocks, strict=True)]
-    starts = [sum(steps[:i]) for i in range(len(items))]
-    n_far = sum(len(so_far) for *_, so_far in items)
+DEEP = 4
+
+
+def adamw(total, count, w, m, v, g, layer, so_far):
+    _, r, c = w.shape
+    block = r // 14 if r % 224 == 0 else r // 16
+    n = r // block
 
     def kernel(total_ref, *refs):
+        ins, outs = refs[:4], refs[4 + len(so_far) : 7 + len(so_far)]
+        bufs, (arrived, left) = refs[7 + len(so_far) : -2], refs[-2:]
+        rows = lambda i: pl.ds(pl.multiple_of(i * block, block), block)
+
+        def fetch(i, slot):
+            return [
+                pltpu.make_async_copy(ref.at[layer, rows(i)] if k < 3 else ref.at[rows(i)], bufs[k].at[slot], arrived.at[k, slot])
+                for k, ref in enumerate(ins)
+            ]
+
+        def store(i, slot):
+            return [pltpu.make_async_copy(bufs[4 + k].at[slot], ref.at[layer, rows(i)], left.at[k, slot]) for k, ref in enumerate(outs)]
+
+        for i in range(DEEP - 1):
+            for copy in fetch(i, i):
+                copy.start()
         factor = jnp.minimum(1.0, 0.5 * lax.rsqrt(total_ref[0:1, 0:1] / count + 1e-30))
-        ins, outs = refs[: 4 * len(items)], refs[4 * len(items) + n_far :]
-        for i in range(len(items)):
-            w_ref, m_ref, v_ref, g_ref = ins[4 * i : 4 * i + 4]
-            new_w_ref, new_m_ref, new_v_ref = outs[3 * i : 3 * i + 3]
-
-            def update(w_ref=w_ref, m_ref=m_ref, v_ref=v_ref, g_ref=g_ref, new_w_ref=new_w_ref, new_m_ref=new_m_ref, new_v_ref=new_v_ref):
-                g = g_ref[...].astype(F32) * factor
-                m = 0.9 * m_ref[...] + 0.1 * g
-                v = 0.95 * v_ref[...] + 0.05 * g * g
-                w = w_ref[...].astype(F32)
-                new_w_ref[...] = (w - 0.02 * (m * lax.rsqrt(v + 1e-8) + 0.1 * w)).astype(BF16)
-                new_m_ref[...] = m
-                new_v_ref[...] = v
-
-            if len(items) == 1:
-                update()
-            else:
-                step = pl.program_id(0)
-                pl.when((step >= starts[i]) & (step < starts[i] + steps[i]))(update)
-
-    in_specs, args, out_specs, out_shape = [pl.BlockSpec((8, 128), lambda i: (0, 0))], [total], [], []
-    for (w, m, v, g, _), block, n, start in zip(items, blocks, steps, starts, strict=True):
-        at = lambda i, n=n, start=start: jnp.clip(i - start, 0, n - 1)
-        part = pl.BlockSpec((None, block, w.shape[2]), lambda i, at=at: (layer, at(i), 0))
-        in_specs += [part, part, part, pl.BlockSpec((block, w.shape[2]), lambda i, at=at: (at(i), 0))]
-        args += [w, m, v, g]
-        out_specs += [part] * 3
-        out_shape += [jax.ShapeDtypeStruct(w.shape, dtype) for dtype in (BF16, F32, F32)]
-    far = [one for *_, so_far in items for one in so_far]
-    size = sum(w.size for w, *_ in items) // 2
-    new = pl.pallas_call(
+
+        def body(i, carry):
+            slot = lax.rem(i, DEEP)
+
+            @pl.when(i + DEEP - 1 < n)
+            def _():
+                for copy in fetch(i + DEEP - 1, lax.rem(i + DEEP - 1, DEEP)):
+                    copy.start()
+
+            for copy in fetch(i, slot):
+                copy.wait()
+
+            @pl.when(i >= DEEP)
+            def _():
+                for copy in store(i - DEEP, slot):
+                    copy.wait()
+
+            w_ref, m_ref, v_ref, g_ref, new_w_ref, new_m_ref, new_v_ref = (buf.at[slot] for buf in bufs)
+            g = g_ref[...].astype(F32) * factor
+            m = 0.9 * m_ref[...] + 0.1 * g
+            v = 0.95 * v_ref[...] + 0.05 * g * g
+            w = w_ref[...].astype(F32)
+            new_w_ref[...] = (w - 0.02 * (m * lax.rsqrt(v + 1e-8) + 0.1 * w)).astype(BF16)
+            new_m_ref[...] = m
+            new_v_ref[...] = v
+            for copy in store(i, slot):
+                copy.start()
+            return carry
+
+        lax.fori_loop(0, n, body, 0)
+        for i in range(n - DEEP, n):
+            for copy in store(i, i % DEEP):
+                copy.wait()
+
+    hbm = pl.BlockSpec(memory_space=pl.ANY)
+    types = (BF16, F32, F32, BF16, BF16, F32, F32)
+    return pl.pallas_call(
         kernel,
-        grid=(sum(steps),),
-        in_specs=in_specs + [pl.BlockSpec(memory_space=pl.ANY)] * n_far,
-        out_specs=out_specs,
-        out_shape=out_shape,
-        input_output_aliases={len(args) + i: i for i in range(n_far)},
-        compiler_params=params(),
-        cost_estimate=cost(40 * size, 22 * size),
+        in_specs=[pl.BlockSpec(memory_space=pltpu.VMEM)] + [hbm] * (4 + len(so_far)),
+        out_specs=[hbm] * 3,
+        out_shape=[jax.ShapeDtypeStruct(w.shape, dtype) for dtype in (BF16, F32, F32)],
+        input_output_aliases={5 + i: i for i in range(len(so_far))},
+        scratch_shapes=[pltpu.VMEM((DEEP, block, c), dtype) for dtype in types]
+        + [pltpu.SemaphoreType.DMA((4, DEEP)), pltpu.SemaphoreType.DMA((3, DEEP))],
+        compiler_params=pltpu.CompilerParams(vmem_limit_bytes=VMEM_LIMIT),
+        cost_estimate=cost(2**32, 22 * r * c),
         name="adamw",
-    )(*args, *far)
-    return [tuple(new[3 * i : 3 * i + 3]) for i in range(len(items))]
+    )(total, w, m, v, g, *so_far)
 
 
 def solution(mesh):
@@ -432,40 +510,36 @@
 
         at0, gate0, up0, actt0, h1 = forward(x, *weights, 0)
         at1, actt1, by1 = top(h1, dy, *weights, 1)
-        shards, squares = [[None] * 3, [None] * 3], []
+        shards, squares, gathered = [[None] * 3, [None] * 3], [], [None] * 3
 
         def keep(layer, i, shard, square):
             shards[layer][i] = shard
             squares.append(square)
 
         down1 = product(actt1, dy, "down1")
-        pair1, *rest = products(at1, by1, (0, 1), (0, 3), down1, None, 1)
-        keep(1, 2, *rest)
-        gathered = [None] * 3
+        pair1, left = products(at1, by1, (0, 1), down1, None, (), 1)
+        bh1, left, *done = input_back(h1, dy, by1, *weights[:2], 1, pair1, 0, left, 2)
+        keep(1, 2, *done)
         gathered[2] = gather(shards[1][2])
-        bh1, *rest = input_back(h1, dy, by1, *weights[:2], 1, pair1, 0, 2)
-        keep(1, 0, *rest)
-        bh1, gathered[2] = lax.optimization_barrier((bh1, gathered[2]))
+        by0, left, *done = hidden_back(bh1, gate0, up0, weights[2], 0, pair1, 1, left, 3)
+        keep(1, 0, *done)
+        by0, gathered[2] = lax.optimization_barrier((by0, gathered[2]))
         gathered[0] = gather(shards[1][0])
-        by0, *rest = hidden_back(bh1, gate0, up0, weights[2], 0, pair1, 1, 3)
-        keep(1, 1, *rest)
-        by0, gathered[0] = lax.optimization_barrier((by0, gathered[0]))
+        down0 = product(actt0, bh1, "down0")
+        gate_term, left, *done = products(at0, by0, (0,), down0, None, left, 4)
+        keep(1, 1, *done)
+        gate_term, gathered[0] = lax.optimization_barrier((gate_term, gathered[0]))
         gathered[1] = gather(shards[1][1])
-        down0 = product(actt0, bh1, "down0")
-        gate_term, *rest = products(at0, by0, (0,), (0, 2), down0, None, 4)
-        keep(0, 2, *rest)
-        gate_term, gathered[1] = lax.optimization_barrier((gate_term, gathered[1]))
-        up_term, *rest = products(at0, by0, (1,), (0, 2), gate_term, 0, 5)
-        keep(0, 0, *rest)
-        shards[0][1], total = last_scatter(up_term, 0, squares, 6)
+        up_term, left, *done = products(at0, by0, (1,), gate_term, 0, left, 5)
+        keep(0, 2, *done)
+        shards[0][1], shards[0][0], total = last_scatter(up_term, 0, left, squares, 6)
         held, _ = lax.optimization_barrier((shards[0], total))
 
         count = sum(w.size for w in weights)
         order = (2, 0, 1)
-        items = [(weights[i], ms[i], vs[i], gathered[i], ()) for i in order]
-        new = dict(zip(order, adamw(total, count, items, 1), strict=True))
+        new = {i: adamw(total, count, weights[i], ms[i], vs[i], gathered[i], 1, ()) for i in order}
         for i in order:
-            (new[i],) = adamw(total, count, [(weights[i], ms[i], vs[i], gather(held[i]), new[i])], 0)
+            new[i] = adamw(total, count, weights[i], ms[i], vs[i], gather(held[i]), 0, new[i])
         new = [new[i] for i in range(3)]
         return tuple(one[which] for which in range(3) for one in new)
 

time: 468 us -> 450 us (0.962)
  Pallas kernels: 447 us -> 422 us
  waiting for transfers between devices: 1.23 us -> 8.74 us
    pallas_call x10 -> x12, Pallas kernels: 337 us -> 312 us  [the longest x5 172 us: scattering(): pl.pallas_call(kernel, grid=(grid,), in_specs=in_specs, out_specs=out_spe...]
    all_gather x6, waiting for transfers between devices: 0.11 us -> 7.62 us  [step(): gather = lambda g: lax.all_gather(g, 'dp', axis=0, tiled=True)]
  transfers between devices with their start and end apart: 6 -> 6, of which waited for: 0 -> 1; matrix products, arithmetic and copies ran while one was open for 0% -> 0% of each run, Pallas kernels for 51% -> 56%
where the time goes in v5:
time: 450 us; the launch traced here: 445 us
  Pallas kernels  422 us (94%)
  between operations  14.8 us (3%)
  waiting for transfers between devices  8.74 us (2%)
    pallas_call x5, Pallas kernels, scattering(): pl.pallas_call(kernel, grid=(grid,), in_specs=in_specs, out_specs=out_spe...  172 us
    pallas_call x6, Pallas kernels, adamw(): pl.pallas_call(kernel, in_specs=[pl.BlockSpec(memory_space=pltpu.VMEM)] +...  103 us
    pallas_call x1, Pallas kernels, top(): pl.pallas_call(top_kernel, grid=(t // ROWS,), in_specs=[rows(d), rows(d),...  41.4 us
    pallas_call x1, Pallas kernels, forward(): pl.pallas_call(forward_kernel, grid=(t // ROWS,), in_specs=[rows(d), whol...  39.7 us
    pallas_call x1, Pallas kernels, last_scatter(): pl.pallas_call(kernel, in_specs=[hbm, hbm, vmem] + [vmem] * len(squares),...  36 us
    pallas_call x2, Pallas kernels, product(): pl.pallas_call(product_kernel, grid=(m // CHUNK,), in_specs=[pl.BlockSpec...  28.9 us
  transfers between devices with their start and end apart: 6, of which 1 were waited for; matrix products, arithmetic and copies ran while one was open for 0% of the time, Pallas kernels for 56%

profile of v5, /device:TPU:0, one launch (start us, length us, event | category | flops | bytes accessed | tf_op | source)
XLA Modules:
  0.0 445.4 jit_solution(16679207297834464562)
XLA Ops:
  7.2 0.0 all-gather.7.cloned.1.call-start
  7.2 39.7 %forward.1 = (bf16[896,2048]{1,0:T(8,128)(2,1)}, f32[2048,2304]{1,0:T(8,128)}, f32[2048,2304]{1,0:T(8,128)}, bf16[2304,2048]{1,0:T(8,128)(2,1)}, bf16[2048,896]{1,0:T(8,128)(2,1)}) custom-call(bf16[2048,896]{1,0:T(8,128)(2,1)} %bitcast.9, bf16[2,896,2304]{2,1,0:T(8,128)(2,1)} %refs_0_.7, bf16[2,896,2304]{2,1,0:T(8,128)(2,1)} %refs_0_.9, ...), custom_call_target="tpu_custom_call" | custom-call | flops 25367150592 | bytes 56623104 | tf_op jit(solution)/shard_map/forward/pallas_call | solution.py:64
  46.9 41.4 %top.1 = (bf16[896,2048]{1,0:T(8,128)(2,1)}, bf16[2304,2048]{1,0:T(8,128)(2,1)}, bf16[2,2048,2304]{2,1,0:T(8,128)(2,1)}) custom-call(bf16[2048,896]{1,0:T(8,128)(2,1)} %get-tuple-element.69.h_ref.refs_0_, bf16[2048,896]{1,0:T(8,128)(2,1)} %bitcast.10, bf16[2,896,2304]{2,1,0:T(8,128)(2,1)} %refs_0_.7, bf16[2,896,2304]{2,1,0:T(8,128)(2,1)} %refs_0_.9, ...), custom_call_target="tpu_custom_call" | custom-call | flops 25367150592 | bytes 37748736 | tf_op jit(solution)/shard_map/top/pallas_call | solution.py:105
  88.3 14.3 %down1.1 = bf16[2304,896]{1,0:T(8,128)(2,1)} custom-call(bf16[2304,2048]{1,0:T(8,128)(2,1)} %get-tuple-element.72.a_ref, bf16[2048,896]{1,0:T(8,128)(2,1)} %bitcast.11), custom_call_target="tpu_custom_call" | custom-call | flops 8455716864 | bytes 17235968 | tf_op jit(solution)/shard_map/down1/pallas_call | solution.py:403
  102.6 28.0 %products.3 = (bf16[2,896,2304]{2,1,0:T(8,128)(2,1)}, bf16[2,144,896]{2,1,0:T(8,128)(2,1)}, f32[2,144,896]{2,1,0:T(8,128)}) custom-call(bf16[896,2048]{1,0:T(8,128)(2,1)} %get-tuple-element.71.refs_0_, bf16[2,2048,2304]{2,1,0:T(8,128)(2,1)} %get-tuple-element.70.refs_1_.refs_2_, bf16[4,2,288,896]{3,2,1,0:T(8,128)(2,1)} %bitcast.16), custom_call_target="tpu_custom_call" | custom-call | flops 16911433728 | bytes 34471936 | tf_op jit(solution)/shard_map/products/pallas_call | solution.py:290
  130.7 32.5 %input_back.1 = (bf16[2048,896]{1,0:T(8,128)(2,1)}, bf16[2,112,1152]{2,1,0:T(8,128)(2,1)}, f32[2,112,1152]{2,1,0:T(8,128)}, bf16[288,896]{1,0:T(8,128)(2,1)}, f32[1,896]{1,0:T(1,128)}) custom-call(bf16[2048,896]{1,0:T(8,128)(2,1)} %get-tuple-element.69.h_ref.refs_0_, bf16[2048,896]{1,0:T(8,128)(2,1)} %bitcast.12, ...), custom_call_target="tpu_custom_call" | custom-call | flops 16911433728 | bytes 28311552 | tf_op jit(solution)/shard_map/input_back/pallas_call | solution.py:290
  163.2 0.0 all-gather.9.cloned.1.call-start
  163.2 40.5 %hidden_back.1 = (bf16[2,2048,2304]{2,1,0:T(8,128)(2,1)}, bf16[2,112,1152]{2,1,0:T(8,128)(2,1)}, f32[2,112,1152]{2,1,0:T(8,128)}, bf16[112,2304]{1,0:T(8,128)(2,1)}, f32[1,2304]{1,0:T(1,128)}) custom-call(bf16[2048,896]{1,0:T(8,128)(2,1)} %get-tuple-element.76.refs_0_.b_ref, f32[2048,2304]{1,0:T(8,128)} %get-tuple-element.77.refs_1_, ...), custom_call_target="tpu_custom_call" | custom-call | flops 8455716864 | bytes 56623104 | tf_op jit(solution)/shard_map/hidden_back/pallas_call | solution.py:290
  203.8 0.0 all-gather.15.cloned.1.call-start
  203.8 14.6 %down0.1 = bf16[2304,896]{1,0:T(8,128)(2,1)} custom-call(bf16[2304,2048]{1,0:T(8,128)(2,1)} %get-tuple-element.84.a_ref, bf16[2048,896]{1,0:T(8,128)(2,1)} %get-tuple-element.76.refs_0_.b_ref), custom_call_target="tpu_custom_call" | custom-call | flops 8455716864 | bytes 17235968 | tf_op jit(solution)/shard_map/down0/pallas_call | solution.py:403
  218.5 36.2 %products.4 = (bf16[1,896,2304]{2,1,0:T(8,128)(2,1)}, bf16[2,144,896]{2,1,0:T(8,128)(2,1)}, f32[2,144,896]{2,1,0:T(8,128)}, bf16[112,2304]{1,0:T(8,128)(2,1)}, f32[1,2304]{1,0:T(1,128)}) custom-call(bf16[896,2048]{1,0:T(8,128)(2,1)} %get-tuple-element.68.refs_0_, bf16[2,2048,2304]{2,1,0:T(8,128)(2,1)} %get-tuple-element.83.refs_1_, ...), custom_call_target="tpu_custom_call" | custom-call | flops 8455716864 | bytes 17235968 | tf_op jit(solution)/shard_map/products/pallas_call | solution.py:290
  254.7 0.0 all-gather.13.cloned.1.call-start
  254.8 35.0 %products.5 = (bf16[1,896,2304]{2,1,0:T(8,128)(2,1)}, bf16[2,112,1152]{2,1,0:T(8,128)(2,1)}, f32[2,112,1152]{2,1,0:T(8,128)}, bf16[288,896]{1,0:T(8,128)(2,1)}, f32[1,896]{1,0:T(1,128)}) custom-call(bf16[896,2048]{1,0:T(8,128)(2,1)} %get-tuple-element.68.refs_0_, bf16[2,2048,2304]{2,1,0:T(8,128)(2,1)} %get-tuple-element.83.refs_1_, ...), custom_call_target="tpu_custom_call" | custom-call | flops 8455716864 | bytes 17235968 | tf_op jit(solution)/shard_map/products/pallas_call | solution.py:290
  289.7 36.0 %last_scatter.1 = (bf16[112,2304]{1,0:T(8,128)(2,1)}, bf16[112,2304]{1,0:T(8,128)(2,1)}, f32[8,128]{1,0:T(8,128)}) custom-call(bf16[1,4,2,112,2304]{4,3,2,1,0:T(8,128)(2,1)} %bitcast.14, bf16[2,112,1152]{2,1,0:T(8,128)(2,1)} %get-tuple-element.93.refs_1_, f32[2,112,1152]{2,1,0:T(8,128)} %get-tuple-element.94.refs_2_, f32[1,896]{1,0:T(1,128)} %get-tuple-element.95.refs_3_, ...), custom_call_target="tpu_custom_call" | custom-call | flops 17179869184 | bytes 1048576 | tf_op jit(solution)/shard_map/last_scatter/pallas_call | solution.py:340
  325.8 0.0 all-gather.17.cloned.1.call-start
  325.8 0.5 all-gather.17.cloned.1.call-update
  326.4 0.5 all-gather.11.cloned.1.call-update
  327.0 17.1 %adamw.10 = (bf16[2,2304,896]{2,1,0:T(8,128)(2,1)}, f32[2,2304,896]{2,1,0:T(8,128)}, f32[2,2304,896]{2,1,0:T(8,128)}) custom-call(f32[8,128]{1,0:T(8,128)} %get-tuple-element.99.total_ref, bf16[2,2304,896]{2,1,0:T(8,128)(2,1)} %refs_0_.11, f32[2,2304,896]{2,1,0:T(8,128)} %refs_1_.11, f32[2,2304,896]{2,1,0:T(8,128)} %refs_2_.11, ...), custom_call_target="tpu_custom_call" | custom-call | flops 4294967296 | bytes 45416448 | tf_op jit(solution)/shard_map/adamw/pallas_call | solution.py:491
  344.1 17.3 %adamw.6 = (bf16[2,896,2304]{2,1,0:T(8,128)(2,1)}, f32[2,896,2304]{2,1,0:T(8,128)}, f32[2,896,2304]{2,1,0:T(8,128)}) custom-call(f32[8,128]{1,0:T(8,128)} %get-tuple-element.99.total_ref, bf16[2,896,2304]{2,1,0:T(8,128)(2,1)} %refs_0_.7, f32[2,896,2304]{2,1,0:T(8,128)} %refs_1_.7, f32[2,896,2304]{2,1,0:T(8,128)} %refs_2_.7, ...), custom_call_target="tpu_custom_call" | custom-call | flops 4294967296 | bytes 45416448 | tf_op jit(solution)/shard_map/adamw/pallas_call | solution.py:491
  361.4 17.3 %adamw.8 = (bf16[2,896,2304]{2,1,0:T(8,128)(2,1)}, f32[2,896,2304]{2,1,0:T(8,128)}, f32[2,896,2304]{2,1,0:T(8,128)}) custom-call(f32[8,128]{1,0:T(8,128)} %get-tuple-element.99.total_ref, bf16[2,896,2304]{2,1,0:T(8,128)(2,1)} %refs_0_.9, f32[2,896,2304]{2,1,0:T(8,128)} %refs_1_.9, f32[2,896,2304]{2,1,0:T(8,128)} %refs_2_.9, ...), custom_call_target="tpu_custom_call" | custom-call | flops 4294967296 | bytes 45416448 | tf_op jit(solution)/shard_map/adamw/pallas_call | solution.py:491
  378.8 17.3 %adamw.9 = (bf16[2,896,2304]{2,1,0:T(8,128)(2,1)}, f32[2,896,2304]{2,1,0:T(8,128)}, f32[2,896,2304]{2,1,0:T(8,128)}) custom-call(f32[8,128]{1,0:T(8,128)} %get-tuple-element.99.total_ref, bf16[2,896,2304]{2,1,0:T(8,128)(2,1)} %refs_0_.9, f32[2,896,2304]{2,1,0:T(8,128)} %refs_1_.9, ...), custom_call_target="tpu_custom_call", output_to_operand_aliasing={{0}: (5, {}), {1}: (6, {}), {2}: (7, {})} | custom-call | flops 4294967296 | bytes 45416448 | tf_op jit(solution)/shard_map/adamw/pallas_call | solution.py:491
  396.1 17.1 %adamw.11 = (bf16[2,2304,896]{2,1,0:T(8,128)(2,1)}, f32[2,2304,896]{2,1,0:T(8,128)}, f32[2,2304,896]{2,1,0:T(8,128)}) custom-call(f32[8,128]{1,0:T(8,128)} %get-tuple-element.99.total_ref, bf16[2,2304,896]{2,1,0:T(8,128)(2,1)} %refs_0_.11, f32[2,2304,896]{2,1,0:T(8,128)} %refs_1_.11, ...), custom_call_target="tpu_custom_call", output_to_operand_aliasing={{0}: (5, {}), {1}: (6, {}), {2}: (7, {})} | custom-call | flops 4294967296 | bytes 45416448 | tf_op jit(solution)/shard_map/adamw/pallas_call | solution.py:491
  413.2 7.5 %all-gather.11.cloned.1.call-done.refs_3_ = bf16[896,2304]{1,0:T(8,128)(2,1)} async-done(((bf16[112,2304]{1,0:T(8,128)(2,1)}), bf16[896,2304]{1,0:T(8,128)(2,1)}) %all-gather.11.cloned.1.call-update) | async-done | bytes 4128784 | tf_op jit(solution)/shard_map/all_gather | solution.py:509
  420.8 17.3 %adamw.7 = (bf16[2,896,2304]{2,1,0:T(8,128)(2,1)}, f32[2,896,2304]{2,1,0:T(8,128)}, f32[2,896,2304]{2,1,0:T(8,128)}) custom-call(f32[8,128]{1,0:T(8,128)} %get-tuple-element.99.total_ref, bf16[2,896,2304]{2,1,0:T(8,128)(2,1)} %refs_0_.7, f32[2,896,2304]{2,1,0:T(8,128)} %refs_1_.7, ...), custom_call_target="tpu_custom_call", output_to_operand_aliasing={{0}: (5, {}), {1}: (6, {}), {2}: (7, {})} | custom-call | flops 4294967296 | bytes 45416448 | tf_op jit(solution)/shard_map/adamw/pallas_call | solution.py:491
  (10 shorter events, 0.2 us)
Async XLA Ops:
  7.2 211.3 %all-gather.7.cloned.1.call-start = ((), (), s32[]{:S(2)}) async-start(), calls=%async_computation | async-start | bytes 4644864 | tf_op jit(solution)/shard_map/all_gather | solution.py:509
  163.2 91.6 %all-gather.9.cloned.1.call-start = ((), (), s32[]{:S(2)}) async-start(), calls=%async_computation.1 | async-start | bytes 4644864 | tf_op jit(solution)/shard_map/all_gather | solution.py:509
  203.8 157.6 %all-gather.15.cloned.1.call-start = ((), (), s32[]{:S(2)}) async-start(), calls=%async_computation.4 | async-start | bytes 4644864 | tf_op jit(solution)/shard_map/all_gather | solution.py:509
  254.7 124.1 %all-gather.13.cloned.1.call-start = ((), (), s32[]{:S(2)}) async-start(), calls=%async_computation.3 | async-start | bytes 4644864 | tf_op jit(solution)/shard_map/all_gather | solution.py:509
  325.8 70.3 %all-gather.17.cloned.1.call-start = ((), (), s32[]{:S(2)}) async-start(), calls=%async_computation.5 | async-start | bytes 4644864 | tf_op jit(solution)/shard_map/all_gather | solution.py:509
  326.4 94.4 %all-gather.11.cloned.1.call-start = ((), (), s32[]{:S(2)}) async-start(), calls=%async_computation.2 | async-start | bytes 4644864 | tf_op jit(solution)/shard_map/all_gather | solution.py:509
Sparse Core Ops, SparseCore 0:
  163.3 42.3 all-gather.6
  207.5 41.8 all-gather.8
  254.8 40.3 all-gather.14
  325.9 30.4 all-gather.12
  358.1 30.4 all-gather.16
  390.3 30.4 all-gather.10

commit v6 on v5

--- a/solution.py
+++ b/solution.py
@@ -165,11 +165,12 @@
     def second(self):
         return self.pair(self.send2, self.got2, 0, (self.over_x, self.over_y))
 
-    def begin(self, before=None):
+    def begin(self, before=None, devices=None):
         barrier = pltpu.get_barrier_semaphore()
-        for device in (self.over_core, self.over_x, self.over_y):
+        devices = (self.over_core, self.over_x, self.over_y) if devices is None else devices
+        for device in devices:
             pl.semaphore_signal(barrier, inc=1, device_id=device, device_id_type=pl.DeviceIdType.MESH)
-        pl.semaphore_wait(barrier, 3)
+        pl.semaphore_wait(barrier, len(devices))
         if before is not None:
             before.start()
         for copy in self.first():
@@ -316,22 +317,30 @@
         scatter = Scatter(g.at[which], send3, kept, *scratch)
         before = Finish(scatter, *previous, old, own_before, *finish1)
         last = Finish(scatter, send3, kept, out, own, *finish2)
-        scatter.begin(before)
+        me = lax.axis_index("dp")
+        everybody = [{"dp": lax.rem(me + by, 8)} for by in range(1, 8)]
+        scatter.begin(before, everybody)
         scatter.go_second()
         before.end()
         rest = sum(jnp.sum(other[...], keepdims=True) for other in (*others, own_before))
         scatter.end_second()
         last.start()
         last.end()
-        total = jnp.broadcast_to(rest + jnp.sum(own[...], keepdims=True), (8, 128))
-        for i, device in enumerate((scatter.over_core, scatter.over_x, scatter.over_y)):
-            mine[i] = total
-            copy = pltpu.make_async_remote_copy(
-                src_ref=mine.at[i], dst_ref=theirs.at[i], send_sem=sent.at[i], recv_sem=received.at[i],
+        mine[...] = jnp.broadcast_to(rest + jnp.sum(own[...], keepdims=True), (8, 128))
+        copies = [
+            pltpu.make_async_remote_copy(
+                src_ref=mine, dst_ref=theirs.at[me], send_sem=sent.at[i], recv_sem=received.at[i],
                 device_id=device, device_id_type=pl.DeviceIdType.MESH,
             )
+            for i, device in enumerate(everybody)
+        ]
+        for copy in copies:
             copy.start()
+        theirs[me] = mine[...]
+        for copy in copies:
             copy.wait()
+        total = theirs[0]
+        for i in range(1, 8):
             total = total + theirs[i]
         total_ref[...] = total
 
@@ -346,8 +355,8 @@
         + finish_scratch(*before_shape)
         + finish_scratch(r, c)
         + [pltpu.VMEM(one.shape, one.dtype) for one in left_of(r, c)]
-        + [pltpu.VMEM((1, c), F32), pltpu.VMEM((1, before_shape[1]), F32), pltpu.VMEM((3, 8, 128), F32), pltpu.VMEM((3, 8, 128), F32)]
-        + [pltpu.SemaphoreType.DMA((3,)), pltpu.SemaphoreType.DMA((3,))],
+        + [pltpu.VMEM((1, c), F32), pltpu.VMEM((1, before_shape[1]), F32), pltpu.VMEM((8, 128), F32), pltpu.VMEM((8, 8, 128), F32)]
+        + [pltpu.SemaphoreType.DMA((7,)), pltpu.SemaphoreType.DMA((7,))],
         compiler_params=pltpu.CompilerParams(vmem_limit_bytes=VMEM_LIMIT, collective_id=collective_id, has_side_effects=True),
         cost_estimate=cost(2**34, 2**20),
         name="last_scatter",
@@ -429,47 +438,44 @@
 DEEP = 4
 
 
-def adamw(total, count, w, m, v, g, layer, so_far):
-    _, r, c = w.shape
-    block = r // 14 if r % 224 == 0 else r // 16
-    n = r // block
-
-    def kernel(total_ref, *refs):
-        ins, outs = refs[:4], refs[4 + len(so_far) : 7 + len(so_far)]
-        bufs, (arrived, left) = refs[7 + len(so_far) : -2], refs[-2:]
-        rows = lambda i: pl.ds(pl.multiple_of(i * block, block), block)
-
-        def fetch(i, slot):
-            return [
-                pltpu.make_async_copy(ref.at[layer, rows(i)] if k < 3 else ref.at[rows(i)], bufs[k].at[slot], arrived.at[k, slot])
-                for k, ref in enumerate(ins)
-            ]
-
-        def store(i, slot):
-            return [pltpu.make_async_copy(bufs[4 + k].at[slot], ref.at[layer, rows(i)], left.at[k, slot]) for k, ref in enumerate(outs)]
-
+class Stream:
+    def __init__(self, layer, block, ins, outs, bufs, arrived, left):
+        self.layer, self.block, self.ins, self.outs, self.bufs, self.arrived, self.left = layer, block, ins, outs, bufs, arrived, left
+        self.n = ins[3].shape[0] // block
+
+    def rows(self, i):
+        return pl.ds(pl.multiple_of(i * self.block, self.block), self.block)
+
+    def fetch(self, i, slot):
+        refs = [ref.at[self.layer, self.rows(i)] if k < 3 else ref.at[self.rows(i)] for k, ref in enumerate(self.ins)]
+        return [pltpu.make_async_copy(ref, self.bufs[k].at[slot], self.arrived.at[k, slot]) for k, ref in enumerate(refs)]
+
+    def store(self, i, slot):
+        return [pltpu.make_async_copy(self.bufs[4 + k].at[slot], ref.at[self.layer, self.rows(i)], self.left.at[k, slot]) for k, ref in enumerate(self.outs)]
+
+    def begin(self):
         for i in range(DEEP - 1):
-            for copy in fetch(i, i):
+            for copy in self.fetch(i, i):
                 copy.start()
-        factor = jnp.minimum(1.0, 0.5 * lax.rsqrt(total_ref[0:1, 0:1] / count + 1e-30))
-
+
+    def run(self, factor):
         def body(i, carry):
             slot = lax.rem(i, DEEP)
 
-            @pl.when(i + DEEP - 1 < n)
+            @pl.when(i + DEEP - 1 < self.n)
             def _():
-                for copy in fetch(i + DEEP - 1, lax.rem(i + DEEP - 1, DEEP)):
+                for copy in self.fetch(i + DEEP - 1, lax.rem(i + DEEP - 1, DEEP)):
                     copy.start()
 
-            for copy in fetch(i, slot):
+            for copy in self.fetch(i, slot):
                 copy.wait()
 
             @pl.when(i >= DEEP)
             def _():
-                for copy in store(i - DEEP, slot):
+                for copy in self.store(i - DEEP, slot):
                     copy.wait()
 
-            w_ref, m_ref, v_ref, g_ref, new_w_ref, new_m_ref, new_v_ref = (buf.at[slot] for buf in bufs)
+            w_ref, m_ref, v_ref, g_ref, new_w_ref, new_m_ref, new_v_ref = (buf.at[slot] for buf in self.bufs)
             g = g_ref[...].astype(F32) * factor
             m = 0.9 * m_ref[...] + 0.1 * g
             v = 0.95 * v_ref[...] + 0.05 * g * g
@@ -477,29 +483,53 @@
             new_w_ref[...] = (w - 0.02 * (m * lax.rsqrt(v + 1e-8) + 0.1 * w)).astype(BF16)
             new_m_ref[...] = m
             new_v_ref[...] = v
-            for copy in store(i, slot):
+            for copy in self.store(i, slot):
                 copy.start()
             return carry
 
-        lax.fori_loop(0, n, body, 0)
-        for i in range(n - DEEP, n):
-            for copy in store(i, i % DEEP):
+        lax.fori_loop(0, self.n, body, 0)
+
+    def end(self):
+        for i in range(self.n - DEEP, self.n):
+            for copy in self.store(i, i % DEEP):
                 copy.wait()
 
+
+def adamw(total, count, items, layer):
+    far = [one for *_, so_far in items for one in so_far]
+    blocks = [w.shape[1] // 14 if w.shape[1] % 224 == 0 else w.shape[1] // 16 for w, *_ in items]
+
+    def kernel(total_ref, *refs):
+        refs = list(refs)
+        take = lambda n: [refs.pop(0) for _ in range(n)]
+        ins, _, outs = [take(4) for _ in items], take(len(far)), [take(3) for _ in items]
+        streams = [Stream(layer, block, i, o, take(7), *take(2)) for block, i, o in zip(blocks, ins, outs, strict=True)]
+        for stream in streams:
+            stream.begin()
+        factor = jnp.minimum(1.0, 0.5 * lax.rsqrt(total_ref[0:1, 0:1] / count + 1e-30))
+        for stream in streams:
+            stream.run(factor)
+        for stream in streams:
+            stream.end()
+
     hbm = pl.BlockSpec(memory_space=pl.ANY)
-    types = (BF16, F32, F32, BF16, BF16, F32, F32)
-    return pl.pallas_call(
+    scratch_shapes = []
+    for (w, *_), block in zip(items, blocks, strict=True):
+        scratch_shapes += [pltpu.VMEM((DEEP, block, w.shape[2]), dtype) for dtype in (BF16, F32, F32, BF16, BF16, F32, F32)]
+        scratch_shapes += [pltpu.SemaphoreType.DMA((4, DEEP)), pltpu.SemaphoreType.DMA((3, DEEP))]
+    size = sum(w.size for w, *_ in items) // 2
+    new = pl.pallas_call(
         kernel,
-        in_specs=[pl.BlockSpec(memory_space=pltpu.VMEM)] + [hbm] * (4 + len(so_far)),
-        out_specs=[hbm] * 3,
-        out_shape=[jax.ShapeDtypeStruct(w.shape, dtype) for dtype in (BF16, F32, F32)],
-        input_output_aliases={5 + i: i for i in range(len(so_far))},
-        scratch_shapes=[pltpu.VMEM((DEEP, block, c), dtype) for dtype in types]
-        + [pltpu.SemaphoreType.DMA((4, DEEP)), pltpu.SemaphoreType.DMA((3, DEEP))],
+        in_specs=[pl.BlockSpec(memory_space=pltpu.VMEM)] + [hbm] * (4 * len(items) + len(far)),
+        out_specs=[hbm] * (3 * len(items)),
+        out_shape=[jax.ShapeDtypeStruct(w.shape, dtype) for w, *_ in items for dtype in (BF16, F32, F32)],
+        input_output_aliases={1 + 4 * len(items) + i: i for i in range(len(far))},
+        scratch_shapes=scratch_shapes,
         compiler_params=pltpu.CompilerParams(vmem_limit_bytes=VMEM_LIMIT),
-        cost_estimate=cost(2**32, 22 * r * c),
+        cost_estimate=cost(2**32 * len(items), 22 * size),
         name="adamw",
-    )(total, w, m, v, g, *so_far)
+    )(total, *[one for item in items for one in item[:4]], *far)
+    return [tuple(new[3 * i : 3 * i + 3]) for i in range(len(items))]
 
 
 def solution(mesh):
@@ -533,13 +563,15 @@
         up_term, left, *done = products(at0, by0, (1,), gate_term, 0, left, 5)
         keep(0, 2, *done)
         shards[0][1], shards[0][0], total = last_scatter(up_term, 0, left, squares, 6)
-        held, _ = lax.optimization_barrier((shards[0], total))
+        (*held, _) = lax.optimization_barrier((*shards[0][:2], total))
+        held.append(shards[0][2])
 
         count = sum(w.size for w in weights)
         order = (2, 0, 1)
-        new = {i: adamw(total, count, weights[i], ms[i], vs[i], gathered[i], 1, ()) for i in order}
+        items = [(weights[i], ms[i], vs[i], gathered[i], ()) for i in order]
+        new = dict(zip(order, adamw(total, count, items, 1), strict=True))
         for i in order:
-            new[i] = adamw(total, count, weights[i], ms[i], vs[i], gather(held[i]), 0, new[i])
+            (new[i],) = adamw(total, count, [(weights[i], ms[i], vs[i], gather(held[i]), new[i])], 0)
         new = [new[i] for i in range(3)]
         return tuple(one[which] for which in range(3) for one in new)
 

time: 450 us -> 448 us (level)
  waiting for transfers between devices: 8.74 us -> 0.71 us
  Pallas kernels: 422 us -> 428 us
    pallas_call x1, Pallas kernels: 36 us -> 45.3 us  [last_scatter(): pl.pallas_call(kernel, in_specs=[hbm, hbm, vmem] + [vmem] * len(squares),...]
    all_gather x6, waiting for transfers between devices: 7.62 us -> 0.1 us  [step(): gather = lambda g: lax.all_gather(g, 'dp', axis=0, tiled=True)]
    pallas_call x6 -> x4, Pallas kernels: 103 us -> 101 us  [adamw(): pl.pallas_call(kernel, in_specs=[pl.BlockSpec(memory_space=pltpu.VMEM)] +...]
  transfers between devices with their start and end apart: 6 -> 6, of which waited for: 1 -> 0; matrix products, arithmetic and copies ran while one was open for 0% -> 0% of each run, Pallas kernels for 56% -> 57%
where the time goes in v6:
time: 448 us; the launch traced here: 444 us
  Pallas kernels  428 us (96%)
  between operations  14.7 us (3%)
    pallas_call x5, Pallas kernels, scattering(): pl.pallas_call(kernel, grid=(grid,), in_specs=in_specs, out_specs=out_spe...  172 us
    pallas_call x4, Pallas kernels, adamw(): pl.pallas_call(kernel, in_specs=[pl.BlockSpec(memory_space=pltpu.VMEM)] +...  101 us
    pallas_call x1, Pallas kernels, last_scatter(): pl.pallas_call(kernel, in_specs=[hbm, hbm, vmem] + [vmem] * len(squares),...  45.3 us
    pallas_call x1, Pallas kernels, top(): pl.pallas_call(top_kernel, grid=(t // ROWS,), in_specs=[rows(d), rows(d),...  41.3 us
    pallas_call x1, Pallas kernels, forward(): pl.pallas_call(forward_kernel, grid=(t // ROWS,), in_specs=[rows(d), whol...  39.7 us
    pallas_call x2, Pallas kernels, product(): pl.pallas_call(product_kernel, grid=(m // CHUNK,), in_specs=[pl.BlockSpec...  28.9 us
  transfers between devices with their start and end apart: 6, of which 0 were waited for; matrix products, arithmetic and copies ran while one was open for 0% of the time, Pallas kernels for 57%

profile of v6, /device:TPU:0, one launch (start us, length us, event | category | flops | bytes accessed | tf_op | source)
XLA Modules:
  0.0 443.5 jit_solution(12764443397005498863)
XLA Ops:
  7.2 0.0 all-gather.7.cloned.1.call-start
  7.2 39.7 %forward.1 = (bf16[896,2048]{1,0:T(8,128)(2,1)}, f32[2048,2304]{1,0:T(8,128)}, f32[2048,2304]{1,0:T(8,128)}, bf16[2304,2048]{1,0:T(8,128)(2,1)}, bf16[2048,896]{1,0:T(8,128)(2,1)}) custom-call(bf16[2048,896]{1,0:T(8,128)(2,1)} %bitcast.9, bf16[2,896,2304]{2,1,0:T(8,128)(2,1)} %refs_0_.5, bf16[2,896,2304]{2,1,0:T(8,128)(2,1)} %refs_0_.6, ...), custom_call_target="tpu_custom_call" | custom-call | flops 25367150592 | bytes 56623104 | tf_op jit(solution)/shard_map/forward/pallas_call | solution.py:64
  46.9 41.3 %top.1 = (bf16[896,2048]{1,0:T(8,128)(2,1)}, bf16[2304,2048]{1,0:T(8,128)(2,1)}, bf16[2,2048,2304]{2,1,0:T(8,128)(2,1)}) custom-call(bf16[2048,896]{1,0:T(8,128)(2,1)} %get-tuple-element.68.h_ref.refs_0_, bf16[2048,896]{1,0:T(8,128)(2,1)} %bitcast.10, bf16[2,896,2304]{2,1,0:T(8,128)(2,1)} %refs_0_.5, bf16[2,896,2304]{2,1,0:T(8,128)(2,1)} %refs_0_.6, ...), custom_call_target="tpu_custom_call" | custom-call | flops 25367150592 | bytes 37748736 | tf_op jit(solution)/shard_map/top/pallas_call | solution.py:105
  88.2 14.3 %down1.1 = bf16[2304,896]{1,0:T(8,128)(2,1)} custom-call(bf16[2304,2048]{1,0:T(8,128)(2,1)} %get-tuple-element.71.a_ref, bf16[2048,896]{1,0:T(8,128)(2,1)} %bitcast.11), custom_call_target="tpu_custom_call" | custom-call | flops 8455716864 | bytes 17235968 | tf_op jit(solution)/shard_map/down1/pallas_call | solution.py:412
  102.6 28.1 %products.3 = (bf16[2,896,2304]{2,1,0:T(8,128)(2,1)}, bf16[2,144,896]{2,1,0:T(8,128)(2,1)}, f32[2,144,896]{2,1,0:T(8,128)}) custom-call(bf16[896,2048]{1,0:T(8,128)(2,1)} %get-tuple-element.70.refs_0_, bf16[2,2048,2304]{2,1,0:T(8,128)(2,1)} %get-tuple-element.69.refs_1_.refs_2_, bf16[4,2,288,896]{3,2,1,0:T(8,128)(2,1)} %bitcast.16), custom_call_target="tpu_custom_call" | custom-call | flops 16911433728 | bytes 34471936 | tf_op jit(solution)/shard_map/products/pallas_call | solution.py:291
  130.6 32.5 %input_back.1 = (bf16[2048,896]{1,0:T(8,128)(2,1)}, bf16[2,112,1152]{2,1,0:T(8,128)(2,1)}, f32[2,112,1152]{2,1,0:T(8,128)}, bf16[288,896]{1,0:T(8,128)(2,1)}, f32[1,896]{1,0:T(1,128)}) custom-call(bf16[2048,896]{1,0:T(8,128)(2,1)} %get-tuple-element.68.h_ref.refs_0_, bf16[2048,896]{1,0:T(8,128)(2,1)} %bitcast.12, ...), custom_call_target="tpu_custom_call" | custom-call | flops 16911433728 | bytes 28311552 | tf_op jit(solution)/shard_map/input_back/pallas_call | solution.py:291
  163.1 0.0 all-gather.9.cloned.1.call-start
  163.2 40.5 %hidden_back.1 = (bf16[2,2048,2304]{2,1,0:T(8,128)(2,1)}, bf16[2,112,1152]{2,1,0:T(8,128)(2,1)}, f32[2,112,1152]{2,1,0:T(8,128)}, bf16[112,2304]{1,0:T(8,128)(2,1)}, f32[1,2304]{1,0:T(1,128)}) custom-call(bf16[2048,896]{1,0:T(8,128)(2,1)} %get-tuple-element.75.refs_0_.b_ref, f32[2048,2304]{1,0:T(8,128)} %get-tuple-element.76.refs_1_, ...), custom_call_target="tpu_custom_call" | custom-call | flops 8455716864 | bytes 56623104 | tf_op jit(solution)/shard_map/hidden_back/pallas_call | solution.py:291
  203.7 0.0 all-gather.13.cloned.1.call-start
  203.8 14.6 %down0.1 = bf16[2304,896]{1,0:T(8,128)(2,1)} custom-call(bf16[2304,2048]{1,0:T(8,128)(2,1)} %get-tuple-element.83.a_ref, bf16[2048,896]{1,0:T(8,128)(2,1)} %get-tuple-element.75.refs_0_.b_ref), custom_call_target="tpu_custom_call" | custom-call | flops 8455716864 | bytes 17235968 | tf_op jit(solution)/shard_map/down0/pallas_call | solution.py:412
  218.4 36.1 %products.4 = (bf16[1,896,2304]{2,1,0:T(8,128)(2,1)}, bf16[2,144,896]{2,1,0:T(8,128)(2,1)}, f32[2,144,896]{2,1,0:T(8,128)}, bf16[112,2304]{1,0:T(8,128)(2,1)}, f32[1,2304]{1,0:T(1,128)}) custom-call(bf16[896,2048]{1,0:T(8,128)(2,1)} %get-tuple-element.67.refs_0_, bf16[2,2048,2304]{2,1,0:T(8,128)(2,1)} %get-tuple-element.82.refs_1_, ...), custom_call_target="tpu_custom_call" | custom-call | flops 8455716864 | bytes 17235968 | tf_op jit(solution)/shard_map/products/pallas_call | solution.py:291
  254.5 0.0 all-gather.17.cloned.1.call-start
  254.5 34.9 %products.5 = (bf16[1,896,2304]{2,1,0:T(8,128)(2,1)}, bf16[2,112,1152]{2,1,0:T(8,128)(2,1)}, f32[2,112,1152]{2,1,0:T(8,128)}, bf16[288,896]{1,0:T(8,128)(2,1)}, f32[1,896]{1,0:T(1,128)}) custom-call(bf16[896,2048]{1,0:T(8,128)(2,1)} %get-tuple-element.67.refs_0_, bf16[2,2048,2304]{2,1,0:T(8,128)(2,1)} %get-tuple-element.82.refs_1_, ...), custom_call_target="tpu_custom_call" | custom-call | flops 8455716864 | bytes 17235968 | tf_op jit(solution)/shard_map/products/pallas_call | solution.py:291
  289.5 0.0 all-gather.15.cloned.1.call-start
  289.5 45.3 %last_scatter.1 = (bf16[112,2304]{1,0:T(8,128)(2,1)}, bf16[112,2304]{1,0:T(8,128)(2,1)}, f32[8,128]{1,0:T(8,128)}) custom-call(bf16[1,4,2,112,2304]{4,3,2,1,0:T(8,128)(2,1)} %bitcast.14, bf16[2,112,1152]{2,1,0:T(8,128)(2,1)} %get-tuple-element.92.refs_1_, f32[2,112,1152]{2,1,0:T(8,128)} %get-tuple-element.93.refs_2_, f32[1,896]{1,0:T(1,128)} %get-tuple-element.94.refs_3_, ...), custom_call_target="tpu_custom_call" | custom-call | flops 17179869184 | bytes 1048576 | tf_op jit(solution)/shard_map/last_scatter/pallas_call | solution.py:349
  334.9 0.0 all-gather.11.cloned.1.call-start
  334.9 0.5 all-gather.11.cloned.1.call-update
  335.5 48.9 %adamw.4 = (bf16[2,2304,896]{2,1,0:T(8,128)(2,1)}, f32[2,2304,896]{2,1,0:T(8,128)}, f32[2,2304,896]{2,1,0:T(8,128)}, bf16[2,896,2304]{2,1,0:T(8,128)(2,1)}, f32[...) custom-call(f32[8,128]{1,0:T(8,128)} %get-tuple-element.98.total_ref, ...), custom_call_target="tpu_custom_call" | custom-call | flops 12884901888 | bytes 136249344 | tf_op jit(solution)/shard_map/adamw/pallas_call | solution.py:521
  384.4 0.0 all-gather.17.cloned.1.call-done.refs_3_
  384.4 17.1 %adamw.7 = (bf16[2,2304,896]{2,1,0:T(8,128)(2,1)}, f32[2,2304,896]{2,1,0:T(8,128)}, f32[2,2304,896]{2,1,0:T(8,128)}) custom-call(f32[8,128]{1,0:T(8,128)} %get-tuple-element.98.total_ref, bf16[2,2304,896]{2,1,0:T(8,128)(2,1)} %refs_0_.7, f32[2,2304,896]{2,1,0:T(8,128)} %refs_1_.7, ...), custom_call_target="tpu_custom_call", output_to_operand_aliasing={{0}: (5, {}), {1}: (6, {}), {2}: (7, {})} | custom-call | flops 4294967296 | bytes 45416448 | tf_op jit(solution)/shard_map/adamw/pallas_call | solution.py:521
  401.5 0.0 all-gather.15.cloned.1.call-done.refs_3_
  401.5 17.3 %adamw.6 = (bf16[2,896,2304]{2,1,0:T(8,128)(2,1)}, f32[2,896,2304]{2,1,0:T(8,128)}, f32[2,896,2304]{2,1,0:T(8,128)}) custom-call(f32[8,128]{1,0:T(8,128)} %get-tuple-element.98.total_ref, bf16[2,896,2304]{2,1,0:T(8,128)(2,1)} %refs_0_.6, f32[2,896,2304]{2,1,0:T(8,128)} %refs_1_.6, ...), custom_call_target="tpu_custom_call", output_to_operand_aliasing={{0}: (5, {}), {1}: (6, {}), {2}: (7, {})} | custom-call | flops 4294967296 | bytes 45416448 | tf_op jit(solution)/shard_map/adamw/pallas_call | solution.py:521
  418.8 0.0 all-gather.11.cloned.1.call-done.refs_3_
  418.9 17.3 %adamw.5 = (bf16[2,896,2304]{2,1,0:T(8,128)(2,1)}, f32[2,896,2304]{2,1,0:T(8,128)}, f32[2,896,2304]{2,1,0:T(8,128)}) custom-call(f32[8,128]{1,0:T(8,128)} %get-tuple-element.98.total_ref, bf16[2,896,2304]{2,1,0:T(8,128)(2,1)} %refs_0_.5, f32[2,896,2304]{2,1,0:T(8,128)} %refs_1_.5, ...), custom_call_target="tpu_custom_call", output_to_operand_aliasing={{0}: (5, {}), {1}: (6, {}), {2}: (7, {})} | custom-call | flops 4294967296 | bytes 45416448 | tf_op jit(solution)/shard_map/adamw/pallas_call | solution.py:521
  (8 shorter events, 0.1 us)
Async XLA Ops:
  7.2 211.2 %all-gather.7.cloned.1.call-start = ((), (), s32[]{:S(2)}) async-start(), calls=%async_computation | async-start | bytes 4644864 | tf_op jit(solution)/shard_map/all_gather | solution.py:539
  163.1 91.4 %all-gather.9.cloned.1.call-start = ((), (), s32[]{:S(2)}) async-start(), calls=%async_computation.1 | async-start | bytes 4644864 | tf_op jit(solution)/shard_map/all_gather | solution.py:539
  203.7 131.8 %all-gather.13.cloned.1.call-start = ((), (), s32[]{:S(2)}) async-start(), calls=%async_computation.3 | async-start | bytes 4644864 | tf_op jit(solution)/shard_map/all_gather | solution.py:539
  254.5 129.9 %all-gather.17.cloned.1.call-start = ((), (), s32[]{:S(2)}) async-start(), calls=%async_computation.5 | async-start | bytes 4644864 | tf_op jit(solution)/shard_map/all_gather | solution.py:539
  289.5 112.0 %all-gather.15.cloned.1.call-start = ((), (), s32[]{:S(2)}) async-start(), calls=%async_computation.4 | async-start | bytes 4644864 | tf_op jit(solution)/shard_map/all_gather | solution.py:539
  334.9 84.0 %all-gather.11.cloned.1.call-start = ((), (), s32[]{:S(2)}) async-start(), calls=%async_computation.2 | async-start | bytes 4644864 | tf_op jit(solution)/shard_map/all_gather | solution.py:539
Sparse Core Ops, SparseCore 0:
  163.3 42.3 all-gather.6
  207.5 41.8 all-gather.8
  254.6 40.3 all-gather.12
  296.7 40.2 all-gather.16
  338.7 30.5 all-gather.14
  370.9 30.4 all-gather.10
